TPU v7x, 32 devices: a whole 2x2x4 slice. The times are simulated.
32 devices in a mesh: coil: 4 (over x, core), slab: 8 (over z, y).
Axes of the slice: x: 2, y: 2, z: 4, core: 2. Of those that a mesh axis runs over, the one named last changes fastest.
Arguments:
- kspace_data: bfloat16 [32, 2, 128, 128, 128], P('coil', None, None, 'slab'), may hold values from -4 to 4
- coil_maps: bfloat16 [32, 2, 128, 128, 128], P('coil', None, 'slab'), may hold values from -1.796875 to 1.796875
- sample_mask: int32 [32, 128, 128], P('coil', None, 'slab'), may hold values 0 or 1
- initial_image: float32 [2, 128, 128, 128], P(None, 'slab', 'coil'), may hold values from -6 to 6
Outputs:
- image: float32 [2, 128, 128, 128], P(None, 'slab', 'coil')
All inputs are finite; a program needn't handle non-finite values. No bound on the sum of `sample_mask` on one device may be relied on, other than what follows from the above.
Results may differ from a plain program's by a relative error of at most 0.0045.
Values may be sent and summed in bfloat16 or wider, within the bound.
A program may use at most 128 MiB of HBM per device.

v0:
```python
import functools
import math

import jax
import jax.numpy as jnp
import ml_dtypes
import numpy as np
from jax import lax
from jax.experimental import pallas as pl
from jax.experimental.pallas import tpu as pltpu
from jax.sharding import PartitionSpec as P

ITERS = 2

dual_step = 0.25
primal_step = 0.25
tv_weight = 0.5
f32 = jnp.float32
bf16 = jnp.bfloat16


def from_behind(block, axis, distance):
    devices = range(lax.axis_size(axis))
    route = [(i - distance, i) for i in devices if i - distance in devices]
    return lax.ppermute(block, axis, route)


def dft_table(length, inverse):
    counter = np.arange(length)
    phase = 2.0 * math.pi / length * (np.outer(counter, counter) % length)
    real_part = np.cos(phase) / math.sqrt(length)
    imag_part = np.sin(phase) / math.sqrt(length)
    if not inverse:
        imag_part = -imag_part
    table = np.stack([np.stack([real_part, imag_part]), np.stack([-imag_part, real_part])])
    return table.astype(ml_dtypes.bfloat16)


def on_right(table):
    n = table.shape[2]
    return jnp.asarray(table.transpose(0, 2, 1, 3).reshape(2 * n, 2 * n))


def on_left(table):
    n = table.shape[2]
    return jnp.asarray(table.transpose(1, 3, 0, 2).reshape(2 * n, 2 * n))


def plane(ref, coil, part):
    block = ref[:, coil, 0, part]
    return block.reshape(block.shape[0] * block.shape[1], block.shape[2])


def dot(a, b, dims=((1,), (0,))):
    return lax.dot_general(a, b, (dims, ((), ())), preferred_element_type=f32)


def combine(out_ref, maps_ref, images, group):
    nz, ny = out_ref.shape[2:]
    real_sum = imag_sum = None
    for coil in range(group):
        real = images[coil * nz : (coil + 1) * nz, :ny]
        imag = images[coil * nz : (coil + 1) * nz, ny:]
        maps_real = plane(maps_ref, coil, 0).astype(f32)
        maps_imag = plane(maps_ref, coil, 1).astype(f32)
        real_term = maps_real * real + maps_imag * imag
        imag_term = maps_real * imag - maps_imag * real
        real_sum = real_term if coil == 0 else real_sum + real_term
        imag_sum = imag_term if coil == 0 else imag_sum + imag_term

    @pl.when(pl.program_id(1) == 0)
    def _():
        out_ref[0, 0] = real_sum
        out_ref[0, 1] = imag_sum

    @pl.when(pl.program_id(1) > 0)
    def _():
        out_ref[0, 0] += real_sum
        out_ref[0, 1] += imag_sum


def normal_kernel(group, guess_ref, maps_ref, mask_ref, fy_ref, fz_ref, gz_ref, gy_ref, out_ref):
    nz, ny = out_ref.shape[2:]
    guess_real = guess_ref[0, 0]
    guess_imag = guess_ref[0, 1]
    rows = []
    for coil in range(group):
        maps_real = plane(maps_ref, coil, 0).astype(f32)
        maps_imag = plane(maps_ref, coil, 1).astype(f32)
        real = maps_real * guess_real - maps_imag * guess_imag
        imag = maps_real * guess_imag + maps_imag * guess_real
        rows.append(jnp.concatenate([real.astype(bf16), imag.astype(bf16)], 1))
    pieces = dot(jnp.concatenate(rows, 0), fy_ref[...]).astype(bf16)
    pieces = jnp.concatenate(
        [
            jnp.concatenate(
                [pieces[c * nz : (c + 1) * nz, j * ny : (j + 1) * ny] for c in range(group)], 1
            )
            for j in range(2)
        ],
        0,
    )
    spectrum = dot(fz_ref[...], pieces).astype(bf16)
    mask = jnp.concatenate([mask_ref[c] for c in range(group)], 1)
    spectrum = spectrum * jnp.concatenate([mask, mask], 0)
    pieces = dot(gz_ref[...], spectrum).astype(bf16)
    pieces = jnp.concatenate(
        [
            jnp.concatenate(
                [pieces[j * nz : (j + 1) * nz, c * ny : (c + 1) * ny] for j in range(2)], 1
            )
            for c in range(group)
        ],
        0,
    )
    combine(out_ref, maps_ref, dot(pieces, gy_ref[...]), group)


def data_kernel(group, data_ref, maps_ref, gy_ref, out_ref):
    columns = jnp.concatenate(
        [
            jnp.concatenate([plane(data_ref, c, 0), plane(data_ref, c, 1)], 0)
            for c in range(group)
        ],
        1,
    )
    combine(out_ref, maps_ref, dot(columns, gy_ref[...], ((0,), (0,))), group)


def whole(shape):
    return pl.BlockSpec(shape, lambda x, c: (0,) * len(shape))


def coil_blocks(array, group):
    src, _, _, parts, planes, cols = array.shape
    return pl.BlockSpec((src, group, 1, parts, planes, cols), lambda x, c: (0, c, x, 0, 0, 0))


def call(kernel, group, operands, specs, shape, coils, flops, nbytes):
    return pl.pallas_call(
        functools.partial(kernel, group),
        out_shape=jax.ShapeDtypeStruct(shape, f32),
        grid=(shape[0], coils // group),
        in_specs=specs,
        out_specs=pl.BlockSpec((1,) + shape[1:], lambda x, c: (x, 0, 0, 0)),
        compiler_params=pltpu.CompilerParams(
            dimension_semantics=("arbitrary", "arbitrary"), vmem_limit_bytes=48 * 2**20
        ),
        cost_estimate=pl.CostEstimate(flops=flops, bytes_accessed=nbytes, transcendentals=0),
    )(*operands)


def coil_group(coils):
    return max(g for g in (1, 2, 4) if coils % g == 0)


def apply_normal(guess, maps, mask, tables):
    coils = maps.shape[1]
    group = coil_group(coils)
    shape = guess.shape
    specs = [
        pl.BlockSpec((1,) + shape[1:], lambda x, c: (x, 0, 0, 0)),
        coil_blocks(maps, group),
        pl.BlockSpec((group,) + mask.shape[1:], lambda x, c: (c, 0, 0)),
    ] + [whole(t.shape) for t in tables]
    cells = coils * shape[0] * shape[2] * shape[3]
    return call(
        normal_kernel, group, (guess, maps, mask) + tables, specs, shape, coils, cells * 4096, cells * 4
    )


def apply_data(data, maps, table, shape):
    coils = maps.shape[1]
    group = coil_group(coils)
    specs = [coil_blocks(data, group), coil_blocks(maps, group), whole(table.shape)]
    cells = coils * shape[0] * shape[2] * shape[3]
    return call(data_kernel, group, (data, maps, table), specs, shape, coils, cells * 1024, cells * 8)


def exchange(blocks):
    got = lax.all_to_all(blocks, "slab", split_axis=0, concat_axis=0, tiled=True)
    if got.shape[4] % 16:
        src, coils, width, parts, share, cols = got.shape
        got = got.transpose(1, 2, 3, 0, 4, 5).reshape(1, coils, width, parts, src * share, cols)
    return got


def tv_update(guess, duals):
    width = guess.shape[0]
    size = lax.axis_size("slab") * width
    pos = lax.axis_index("slab") * width + lax.broadcasted_iota(jnp.int32, (width, 1, 1, 1), 0)
    ahead_x = jnp.concatenate([guess[1:], from_behind(guess[:1], "slab", -1)], 0)
    grad_x = jnp.where(pos < size - 1, ahead_x - guess, 0.0)
    grad_z = jnp.concatenate(
        [guess[:, :, 1:] - guess[:, :, :-1], jnp.zeros_like(guess[:, :, :1])], 2
    )
    grad_y = jnp.concatenate([guess[..., 1:] - guess[..., :-1], jnp.zeros_like(guess[..., :1])], 3)
    moved = [dual_step * grad for grad in (grad_z, grad_y, grad_x)]
    if duals is not None:
        moved = [dual + step for dual, step in zip(duals, moved)]
    magnitude = jnp.sqrt(sum(jnp.sum(w * w, 1, keepdims=True) for w in moved))
    factor = 1.0 / jnp.maximum(1.0, magnitude / tv_weight)
    dual_z, dual_y, dual_x = [w * factor for w in moved]
    prior = from_behind(dual_x[-1:], "slab", 1)
    spread_x = jnp.concatenate([prior, dual_x[:-1]], 0) - dual_x
    spread_z = jnp.concatenate([jnp.zeros_like(dual_z[:, :, :1]), dual_z[:, :, :-1]], 2) - dual_z
    spread_y = jnp.concatenate([jnp.zeros_like(dual_y[..., :1]), dual_y[..., :-1]], 3) - dual_y
    return (dual_z, dual_y, dual_x), spread_z + spread_y + spread_x


def on_device(kspace_data, coil_maps, sample_mask, initial_image):
    slabs = lax.axis_size("slab")
    groups = lax.axis_size("coil")
    coils, _, planes, ny, nx = coil_maps.shape
    nz = kspace_data.shape[2]
    shares = kspace_data.shape[3]
    rows = initial_image.shape[2]
    width = nx // slabs
    forward_y, inverse_y = dft_table(ny, False), dft_table(ny, True)
    forward_z, inverse_z = dft_table(nz, False), dft_table(nz, True)
    inverse_x = jnp.asarray(dft_table(nx, True))
    tables = (on_right(forward_y), on_left(forward_z), on_left(inverse_z), on_right(inverse_y))

    image = initial_image.reshape(2, planes, rows, slabs, width).transpose(3, 4, 0, 2, 1)
    image = lax.all_to_all(
        image.reshape(slabs, -1), "slab", split_axis=0, concat_axis=0, tiled=True
    ).reshape(slabs, width, 2, rows, planes)
    image = image.transpose(1, 2, 3, 0, 4).reshape(width, 2, rows, nz)
    image = lax.all_gather(image, "coil", axis=2, tiled=True).swapaxes(2, 3)
    mask = lax.all_gather(sample_mask.astype(bf16), "slab", axis=2, tiled=True)

    maps = coil_maps.reshape(coils, 2, planes, ny, slabs, width).transpose(4, 0, 5, 1, 2, 3)
    maps, image, mask = lax.optimization_barrier((maps, image, mask))
    maps = exchange(maps)

    data = kspace_data * sample_mask[:, None, :, :, None].astype(bf16)
    data = jnp.einsum("ckzyx,kjxw->cjzyw", data, inverse_x, preferred_element_type=f32).astype(bf16)
    data = jnp.einsum(
        "ckzyx,kjzw->cjywx", data, jnp.asarray(inverse_z), preferred_element_type=f32
    ).astype(bf16)
    data = data.reshape(coils, 2, shares, nz, slabs, width).transpose(4, 0, 5, 1, 2, 3)
    data, maps = lax.optimization_barrier((data, maps))
    data = exchange(data)

    normal = apply_normal(image, maps, mask, tables)
    duals, spread = tv_update(image, None)
    data, normal, duals, spread = lax.optimization_barrier((data, normal, duals, spread))
    back_data = apply_data(data, maps, tables[3], image.shape)
    scale = dual_step / (1.0 + dual_step)
    data_grad = lax.psum(scale * (normal - back_data), "coil")
    updated = image - primal_step * (data_grad + spread)
    guess = 2.0 * updated - image
    normal = apply_normal(guess, maps, mask, tables)
    _, spread = tv_update(guess, duals)
    known = updated - primal_step * (data_grad / (1.0 + dual_step) + spread)
    share = known / groups - (primal_step * scale) * (normal - back_data)
    share = lax.psum_scatter(share.swapaxes(2, 3), "coil", scatter_dimension=2, tiled=True)
    share = share.reshape(width, 2, rows, slabs, planes).transpose(3, 1, 4, 2, 0)
    share = lax.all_to_all(
        share.reshape(slabs, -1), "slab", split_axis=0, concat_axis=0, tiled=True
    ).reshape(slabs, 2, planes, rows, width)
    return share.transpose(1, 2, 3, 0, 4).reshape(2, planes, rows, nx)


def solution(mesh):
    placed = (
        P("coil", None, None, "slab", None),
        P("coil", None, "slab", None, None),
        P("coil", None, "slab"),
        P(None, "slab", "coil", None),
    )
    return jax.shard_map(
        on_device,
        mesh=mesh,
        in_specs=placed,
        out_specs=P(None, "slab", "coil", None),
        check_vma=False,
    )
```

profile of v0, /device:TPU:0, one launch (start us, length us, event | category | flops | bytes accessed | tf_op | source)
XLA Modules:
  0.0 741.3 jit_solution(9962698347322002469)
XLA Ops:
  6.5 5.3 copy.69
  11.8 3.7 all_to_all.24
  15.5 21.6 %all_to_all.30 = f32[8,1,16384]{2,1,0:T(1,128)S(1)} all-to-all(f32[8,1,16384]{2,1,0:T(1,128)S(1)} %all_to_all.24), channel_id=1, replica_groups=mesh['coil'=4,'slab'=8] {'slab'}, dimensions={0} | all-to-all | bytes 1048576 | tf_op jit(solution)/shard_map/all_to_all | solution.py:225
  37.1 1.2 reduce
  38.4 3.4 reshape.81
  41.7 2.8 copy.47
  44.6 1.5 copy.48
  46.0 12.0 %copy.42 = bf16[8,2,16,128,128]{3,4,2,1,0:T(8,128)(2,1)} copy(bf16[8,2,16,128,128]{4,3,2,1,0:T(8,128)(2,1)} %param.11) | data formatting | bytes 16777216 | tf_op args[1]
  58.1 16.4 %copy.86 = bf16[8,2,16,128,8,16]{3,2,1,5,0,4:T(8,128)(2,1)} copy(bf16[8,2,16,128,8,16]{3,5,4,2,1,0:T(8,128)(2,1)} %bitcast.68) | data formatting | bytes 16777216 | tf_op jit(solution)/shard_map/reshape | solution.py:232
  74.5 30.9 %all_gather.7 = bf16[8,128,128]{1,0,2:T(8,128)(2,1)S(1)} all-gather(bf16[8,128,16]{1,0,2:T(8,128)(2,1)S(1)} %copy_convert_fusion), channel_id=1, replica_groups=mesh['coil'=4,'slab'=8] {'slab'}, dimensions={2}, use_global_device_ids=true | all-gather | bytes 294912 | tf_op jit(solution)/shard_map/all_gather | solution.py:230
  105.4 2.0 copy.49
  107.4 5.1 all-to-all-start.1
  112.7 7.9 %multiply_bitcast_fusion = bf16[8,2,128,16,128,1]{4,3,2,1,0,5:T(8,128)(2,1)} fusion(bf16[8,2,128,16,128]{4,3,2,1,0:T(8,128)(2,1)} %param.10, bf16[8,128,16]{2,1,0:T(8,128)(2,1)S(1)} %copy.51), kind=kLoop, calls=%fused_computation.6 | loop fusion | flops 4194304 | bytes 16809984 | tf_op jit(solution)/shard_map/mul | solution.py:236
  120.6 9.2 %bitcast_convert_fusion = bf16[8,16,128,2,128]{4,2,3,1,0:T(8,128)(2,1)} fusion(bf16[2,2,128,128,1,1]{3,2,0,1,5,4:T(8,128)(2,1)S(1)} %copy-done.16, bf16[8,2,128,16,128,1]{4,3,2,1,0,5:T(8,128)(2,1)} %multiply_bitcast_fusion), kind=kOutput, calls=%fused_computation | convolution fusion | flops 4303355904 | bytes 16908288 | tf_op jit(solution)/shard_map/ckzyx,kjzw->cjywx/dot_general | solution.py:238
  129.8 16.3 %copy.85 = bf16[8,2,16,128,8,16]{3,2,1,5,0,4:T(8,128)(2,1)} copy(bf16[8,2,16,128,8,16]{3,5,4,1,2,0:T(8,128)(2,1)} %bitcast.77) | data formatting | bytes 16777216 | tf_op jit(solution)/shard_map/reshape | solution.py:241
  146.2 142.6 %all-to-all-done.1.maps_ref = bf16[8,8,16,2,16,128]{5,4,3,2,1,0:T(8,128)(2,1)} async-done(((bf16[8,8,16,2,16,128]{5,4,3,2,1,0:T(8,128)(2,1)}), bf16[8,8,16,2,16,128]{5,4,3,2,1,0:T(8,128)(2,1)}, u32[]{:S(2)}, u32[]{:S(2)}) %all-to-all-start.1) | async-done | bytes 8388640 | tf_op jit(solution)/shard_map/all_to_all | solution.py:181
  288.8 5.0 all-to-all-start.2
  293.9 1.5 collective-permute-start
  295.4 0.6 slice_subtract_fusion.2
  296.0 0.3 slice_subtract_fusion.3
  296.4 0.5 multiply_reduce_fusion.4
  297.0 47.5 %collective-permute-done = f32[1,2,128,128]{3,2,1,0:T(8,128)S(1)} collective-permute-done((f32[1,2,128,128]{3,2,1,0:T(8,128)S(1)}, f32[1,2,128,128]{3,2,1,0:T(8,128)S(1)}, u32[]{:S(2)}, u32[]{:S(2)}) %collective-permute-start) | collective-permute-done | bytes 131104 | tf_op jit(solution)/shard_map/ppermute | solution.py:25
  344.5 0.7 multiply_reduce_fusion.3
  345.1 0.5 divide_multiply_fusion
  345.6 3.2 broadcast_multiply_fusion.3
  348.8 1.3 copy-done.11
  350.1 48.5 %collective-permute-start.1 = (f32[1,2,128,128]{3,2,1,0:T(8,128)S(1)}, f32[1,2,128,128]{3,2,1,0:T(8,128)S(1)}, u32[]{:S(2)}, u32[]{:S(2)}) collective-permute-start(f32[1,2,128,128]{3,2,1,0:T(8,128)S(1)} %slice.82), channel_id=1, source_target_pairs={{0,1},{1,2},{2,3},{3,4},{4,5},{5,6},{6,7},{8,9},{9,10},{10,11},{11... | collective-permute-start | bytes 393224 | tf_op jit(solution)/shard_map/ppermute | solution.py:25
  398.6 0.2 copy.56.mask_ref
  398.9 1.9 slice.83
  400.7 0.4 collective-permute-done.1
  401.1 5.5 fusion.3
  406.6 30.3 %shard_map.100 = f32[16,2,128,128]{3,2,1,0:T(8,128)S(1)} custom-call(f32[16,2,128,128]{3,2,1,0:T(8,128)S(1)} %bitcast.61, bf16[8,8,16,2,16,128]{5,4,3,2,1,0:T(8,128)(2,1)} %all-to-all-done.1.maps_ref, bf16[8,128,128]{2,1,0:T(8,128)(2,1)S(1)} %copy.56.mask_ref, bf16[256,256]{1,0:T(8,128)(2,1)S(1)} %copy-done.7, bf16[256,256]{1,0:T(8,128)(2,1)S(1)} %copy-done.6, ...), custom_call_target="tpu_custom_call" | custom-call | flops 8589934592 | bytes 8388608 | tf_op jit(solution)/shard_map/pallas_call | solution.py:140
  436.9 1.3 copy-done.4
  438.2 38.9 %all-to-all-done.2.data_ref = bf16[8,8,16,2,16,128]{5,4,3,2,1,0:T(8,128)(2,1)} async-done(((bf16[8,8,16,2,16,128]{5,4,3,2,1,0:T(8,128)(2,1)}), bf16[8,8,16,2,16,128]{5,4,3,2,1,0:T(8,128)(2,1)}, u32[]{:S(2)}, u32[]{:S(2)}) %all-to-all-start.2) | async-done | bytes 8388640 | tf_op jit(solution)/shard_map/all_to_all | solution.py:181
  477.1 22.5 %shard_map.101 = f32[16,2,128,128]{3,2,1,0:T(8,128)S(1)} custom-call(bf16[8,8,16,2,16,128]{5,4,3,2,1,0:T(8,128)(2,1)} %all-to-all-done.2.data_ref, bf16[8,8,16,2,16,128]{5,4,3,2,1,0:T(8,128)(2,1)} %all-to-all-done.1.maps_ref, bf16[256,256]{1,0:T(8,128)(2,1)S(1)} %copy-done.6), custom_call_target="tpu_custom_call" | custom-call | flops 2147483648 | bytes 16777216 | tf_op jit(solution)/shard_map/pallas_call | solution.py:140
  499.7 1.3 copy-done.2
  501.0 1.7 subtract_multiply_fusion
  502.8 100.5 %all-reduce.10.cloned.1.call-done = f32[16,2,128,128]{3,2,1,0:T(8,128)} async-done(((f32[16,2,128,128]{3,2,1,0:T(8,128)}), f32[16,2,128,128]{3,2,1,0:T(8,128)}) %all-reduce.10.cloned.1.call-update) | async-done | bytes 2097168 | tf_op jit(solution)/shard_map/psum | solution.py:250
  603.3 2.9 multiply_subtract_fusion.guess_ref
  606.2 0.6 slice_subtract_fusion
  606.8 0.7 copy-done
  607.5 0.3 slice_subtract_fusion.1
  607.9 1.8 collective-permute-start.2
  609.7 0.5 multiply_reduce_fusion.2
  610.2 0.2 copy-done.9
  610.5 0.5 multiply_reduce_fusion.1
  611.0 4.0 collective-permute-done.2
  615.0 2.3 multiply_reduce_fusion
  617.3 1.4 maximum_divide_fusion
  618.7 4.3 broadcast_multiply_fusion.2
  623.0 4.3 collective-permute-start.3
  627.3 30.4 %shard_map.102 = f32[16,2,128,128]{3,2,1,0:T(8,128)S(1)} custom-call(f32[16,2,128,128]{3,2,1,0:T(8,128)S(1)} %copy-done.1, bf16[8,8,16,2,16,128]{5,4,3,2,1,0:T(8,128)(2,1)} %all-to-all-done.1.maps_ref, bf16[8,128,128]{2,1,0:T(8,128)(2,1)S(1)} %copy.56.mask_ref, bf16[256,256]{1,0:T(8,128)(2,1)S(1)} %copy-done.7, bf16[256,256]{1,0:T(8,128)(2,1)S(1)} %copy-done.6, ...), custom_call_target="tpu_custom_call" | custom-call | flops 8589934592 | bytes 8388608 | tf_op jit(solution)/shard_map/pallas_call | solution.py:140
  658.0 1.4 copy-done.3
  659.4 5.2 fusion.13
  664.6 3.1 copy.58
  667.7 29.7 %reduce-scatter.2.cloned.1.call-done = f32[16,2,32,128]{3,0,1,2:T(8,128)} async-done(((f32[16,2,128,128]{3,0,1,2:T(8,128)}), f32[16,2,32,128]{3,0,1,2:T(8,128)}) %reduce-scatter.2.cloned.1.call-update) | async-done | bytes 524304 | tf_op jit(solution)/shard_map/reduce_scatter | solution.py:257
  697.4 1.7 copy.59
  699.0 2.8 copy.60
  701.8 3.7 all_to_all.25
  705.5 20.0 %all_to_all.31 = f32[8,1,16384]{2,1,0:T(1,128)S(1)} all-to-all(f32[8,1,16384]{2,1,0:T(1,128)S(1)} %all_to_all.25), channel_id=1, replica_groups=mesh['coil'=4,'slab'=8] {'slab'}, dimensions={0} | all-to-all | bytes 1048576 | tf_op jit(solution)/shard_map/all_to_all | solution.py:259
  725.5 1.2 reduce.1
  726.7 3.4 reshape.85
  730.1 2.8 copy.62
  732.9 1.4 copy.63
  (47 shorter events, 0.8 us)
Async XLA Ops:
  6.5 98.8 %all-gather.2.cloned.1.call-start = ((), (), s32[]{:S(2)}) async-start(), calls=%async_computation.5 | async-start | bytes 2621440 | tf_op jit(solution)/shard_map/all_gather | solution.py:229
  58.1 16.4 %copy-start.15 = (s32[8,128,16]{1,2,0:T(8,128)S(1)}, s32[8,128,16]{1,2,0:T(8,128)}, u32[]{:S(2)}) copy-start(s32[8,128,16]{1,2,0:T(8,128)} %param.12) | copy-start | bytes 196612
  107.4 181.4 %all-to-all-start.1 = ((bf16[8,8,16,2,16,128]{5,4,3,2,1,0:T(8,128)(2,1)}), bf16[8,8,16,2,16,128]{5,4,3,2,1,0:T(8,128)(2,1)}, u32[]{:S(2)}, u32[]{:S(2)}) async-start(bf16[8,8,16,2,16,128]{5,4,3,2,1,0:T(8,128)(2,1)} %bitcast.67), calls=%async_computation.1 | async-start | bytes 16777216 | tf_op jit(solution)/shard_map/all_to_all | solution.py:181
  112.7 7.9 %copy-start.16 = (bf16[2,2,128,128,1,1]{3,2,0,1,5,4:T(8,128)(2,1)S(1)}, bf16[2,2,128,128,1,1]{3,2,0,1,5,4:T(8,128)(2,1)}, u32[]{:S(2)}) copy-start(bf16[2,2,128,128,1,1]{3,2,0,1,5,4:T(8,128)(2,1)} %constant.55) | copy-start | bytes 393220
  288.8 188.4 %all-to-all-start.2 = ((bf16[8,8,16,2,16,128]{5,4,3,2,1,0:T(8,128)(2,1)}), bf16[8,8,16,2,16,128]{5,4,3,2,1,0:T(8,128)(2,1)}, u32[]{:S(2)}, u32[]{:S(2)}) async-start(bf16[8,8,16,2,16,128]{5,4,3,2,1,0:T(8,128)(2,1)} %bitcast.66), calls=%async_computation.2 | async-start | bytes 16777216 | tf_op jit(solution)/shard_map/all_to_all | solution.py:181
  293.8 309.5 %all-reduce.10.cloned.1.call-start = ((), (), s32[]{:S(2)}) async-start(), calls=%async_computation.6 | async-start | bytes 4194304 | tf_op jit(solution)/shard_map/psum | solution.py:250
  293.9 50.6 %collective-permute-start = (f32[1,2,128,128]{3,2,1,0:T(8,128)S(1)}, f32[1,2,128,128]{3,2,1,0:T(8,128)S(1)}, u32[]{:S(2)}, u32[]{:S(2)}) collective-permute-start(f32[1,2,128,128]{3,2,1,0:T(8,128)S(1)} %slice.65), channel_id=1, source_target_pairs={{1,0},{2,1},{3,2},{4,3},{5,4},{6,5},{7,6},{9,8},{10,9},{11,10},{12... | collective-permute-start | bytes 393224 | tf_op jit(solution)/shard_map/ppermute | solution.py:25
  348.8 1.3 copy-start.11
  350.1 51.0 %collective-permute-start.1 = (f32[1,2,128,128]{3,2,1,0:T(8,128)S(1)}, f32[1,2,128,128]{3,2,1,0:T(8,128)S(1)}, u32[]{:S(2)}, u32[]{:S(2)}) collective-permute-start(f32[1,2,128,128]{3,2,1,0:T(8,128)S(1)} %slice.82), channel_id=1, source_target_pairs={{0,1},{1,2},{2,3},{3,4},{4,5},{5,6},{6,7},{8,9},{9,10},{10,11},{11... | collective-permute-start | bytes 393224 | tf_op jit(solution)/shard_map/ppermute | solution.py:25
  398.8 2.3 copy-start.8
  401.1 5.5 copy-start.6
  401.1 5.5 copy-start.7
  436.8 1.3 copy-start.4
  477.1 23.9 %copy-start.5 = (f32[16,2,128,128]{3,2,1,0:T(8,128)S(1)}, f32[16,2,128,128]{3,2,1,0:T(8,128)}, u32[]{:S(2)}) copy-start(f32[16,2,128,128]{3,2,1,0:T(8,128)} %copy-done.4) | copy-start | bytes 6291460
  499.7 1.4 copy-start.2
  502.8 194.6 %reduce-scatter.2.cloned.1.call-start = ((), (), s32[]{:S(2)}) async-start(), calls=%async_computation.7 | async-start | bytes 2621440 | tf_op jit(solution)/shard_map/reduce_scatter | solution.py:257
  606.2 1.3 copy-start
  607.5 2.2 copy-start.10
  607.8 2.4 copy-start.13
  607.9 2.6 copy-start.9
  607.9 7.2 collective-permute-start.2
  609.7 5.3 copy-start.12
  610.5 4.6 copy-start.1
  610.5 4.6 slice-start
  623.0 34.9 %collective-permute-start.3 = (f32[1,2,128,128]{3,2,1,0:T(8,128)S(1)}, f32[1,2,128,128]{3,2,1,0:T(8,128)S(1)}, u32[]{:S(2)}, u32[]{:S(2)}) collective-permute-start(f32[1,2,128,128]{3,2,1,0:T(8,128)S(1)} %slice.92), channel_id=1, source_target_pairs={{0,1},{1,2},{2,3},{3,4},{4,5},{5,6},{6,7},{8,9},{9,10},{10,11},{11... | collective-permute-start | bytes 393224 | tf_op jit(solution)/shard_map/ppermute | solution.py:25
  627.3 30.7 %copy-start.14 = (f32[16,2,128,128]{3,2,1,0:T(8,128)S(1)}, f32[16,2,128,128]{3,2,1,0:T(8,128)}, u32[]{:S(2)}) copy-start(f32[16,2,128,128]{3,2,1,0:T(8,128)} %fusion.3) | copy-start | bytes 6291460
  657.8 1.6 copy-start.3
Sparse Core Ops, SparseCore 0:
  46.2 21.5 all-gather.1
  502.9 100.3 all-reduce.9
  667.8 29.5 reduce-scatter.1
where the time goes:
time: 749 us; the launch traced here: 741 us
  waiting for transfers between devices  364 us (49%)
  local copies, waits for them, and re-layouts  91 us (12%)
  Pallas kernels  83.2 us (11%)
  blocking collectives  72.5 us (10%)
  starting transfers between devices  66.4 us (9%)
  other arithmetic  41.3 us (6%)
  between operations  14 us (2%)
  matrix products  9.21 us (1%)
    all_to_all x2, waiting for transfers between devices, exchange(): lax.all_to_all(blocks, 'slab', split_axis=0, concat_axis=0, tiled=True)  182 us
    psum x1, waiting for transfers between devices, on_device(): data_grad = lax.psum(scale * (normal - back_data), 'coil')  100 us
    pallas_call x3, Pallas kernels, call(): pl.pallas_call(functools.partial(kernel, group), out_shape=jax.ShapeDtype...  83.2 us
    ppermute x4, starting transfers between devices, from_behind(): return lax.ppermute(block, axis, route)  56.1 us
    ppermute x4, waiting for transfers between devices, from_behind(): return lax.ppermute(block, axis, route)  51.9 us
    all_gather x1, blocking collectives, on_device(): mask = lax.all_gather(sample_mask.astype(bf16), 'slab', axis=2, tiled=True)  30.9 us
    reduce_scatter x1, waiting for transfers between devices, on_device(): lax.psum_scatter(share.swapaxes(2, 3), 'coil', scatter_dimension=2, tiled...  29.7 us
    all_to_all x1, blocking collectives, on_device(): lax.all_to_all(image.reshape(slabs, -1), 'slab', split_axis=0, concat_axi...  21.6 us
  transfers between devices with their start and end apart: 9, of which 7 were waited for; matrix products, arithmetic and copies ran while one was open for 10% of the time, Pallas kernels for 8%

commit v1 on v0

--- a/solution.py
+++ b/solution.py
@@ -7,6 +7,7 @@
 import numpy as np
 from jax import lax
 from jax.experimental import pallas as pl
+from jax.experimental.layout import Layout, with_layout_constraint
 from jax.experimental.pallas import tpu as pltpu
 from jax.sharding import PartitionSpec as P
 
@@ -262,6 +263,266 @@
     return share.transpose(1, 2, 3, 0, 4).reshape(2, planes, rows, nx)
 
 
+def all_planes(ref, coil, part):
+    block = ref[:, coil, 0, 0, part]
+    return block.reshape(block.shape[0] * block.shape[1], block.shape[2])
+
+
+def combine_planes(out_ref, maps, images):
+    nz, ny = out_ref.shape[2:]
+    real_sum = imag_sum = None
+    for coil, (maps_real, maps_imag) in enumerate(maps):
+        real = images[coil * nz : (coil + 1) * nz, :ny]
+        imag = images[coil * nz : (coil + 1) * nz, ny:]
+        real_term = maps_real * real + maps_imag * imag
+        imag_term = maps_real * imag - maps_imag * real
+        real_sum = real_term if coil == 0 else real_sum + real_term
+        imag_sum = imag_term if coil == 0 else imag_sum + imag_term
+
+    @pl.when(pl.program_id(1) == 0)
+    def _():
+        out_ref[0, 0] = real_sum
+        out_ref[0, 1] = imag_sum
+
+    @pl.when(pl.program_id(1) > 0)
+    def _():
+        out_ref[0, 0] += real_sum
+        out_ref[0, 1] += imag_sum
+
+
+def planes_of(maps_ref):
+    return [
+        (all_planes(maps_ref, c, 0).astype(f32), all_planes(maps_ref, c, 1).astype(f32))
+        for c in range(maps_ref.shape[1])
+    ]
+
+
+def normal_planes(guess_ref, maps_ref, mask_ref, fy_ref, fz_ref, gz_ref, gy_ref, out_ref):
+    nz, ny = out_ref.shape[2:]
+    group = maps_ref.shape[1]
+    guess_real = guess_ref[0, 0]
+    guess_imag = guess_ref[0, 1]
+    maps = planes_of(maps_ref)
+    rows = []
+    for maps_real, maps_imag in maps:
+        real = maps_real * guess_real - maps_imag * guess_imag
+        imag = maps_real * guess_imag + maps_imag * guess_real
+        rows.append(jnp.concatenate([real.astype(bf16), imag.astype(bf16)], 1))
+    pieces = dot(jnp.concatenate(rows, 0), fy_ref[...]).astype(bf16)
+    pieces = jnp.concatenate(
+        [
+            jnp.concatenate(
+                [pieces[c * nz : (c + 1) * nz, j * ny : (j + 1) * ny] for c in range(group)], 1
+            )
+            for j in range(2)
+        ],
+        0,
+    )
+    spectrum = dot(fz_ref[...], pieces).astype(bf16)
+    mask = jnp.concatenate([mask_ref[c, 0] for c in range(group)], 1)
+    spectrum = spectrum * jnp.concatenate([mask, mask], 0)
+    pieces = dot(gz_ref[...], spectrum).astype(bf16)
+    pieces = jnp.concatenate(
+        [
+            jnp.concatenate(
+                [pieces[j * nz : (j + 1) * nz, c * ny : (c + 1) * ny] for j in range(2)], 1
+            )
+            for c in range(group)
+        ],
+        0,
+    )
+    combine_planes(out_ref, maps, dot(pieces, gy_ref[...]))
+
+
+def data_planes(data_ref, maps_ref, gy_ref, out_ref):
+    columns = jnp.concatenate(
+        [
+            jnp.concatenate([all_planes(data_ref, c, 0), all_planes(data_ref, c, 1)], 0)
+            for c in range(data_ref.shape[1])
+        ],
+        1,
+    )
+    combine_planes(out_ref, planes_of(maps_ref), dot(columns, gy_ref[...], ((0,), (0,))))
+
+
+def plane_call(kernel, operands, specs, shape, steps, flops, nbytes):
+    return pl.pallas_call(
+        kernel,
+        out_shape=jax.ShapeDtypeStruct(shape, f32),
+        grid=(shape[0], steps),
+        in_specs=specs,
+        out_specs=pl.BlockSpec((1,) + shape[1:], lambda x, c: (x, 0, 0, 0)),
+        compiler_params=pltpu.CompilerParams(
+            dimension_semantics=("arbitrary", "arbitrary"), vmem_limit_bytes=48 * 2**20
+        ),
+        cost_estimate=pl.CostEstimate(flops=flops, bytes_accessed=nbytes, transcendentals=0),
+    )(*operands)
+
+
+def every_source(array, start=0):
+    slabs, groups, _, _, parts, rows, cols = array.shape
+    return pl.BlockSpec(
+        (slabs, groups, 1, 1, parts, rows, cols), lambda x, c: (0, 0, x, start + c, 0, 0, 0)
+    )
+
+
+def normal_of(guess, maps, mask, first, tables):
+    shape = guess.shape
+    coils = maps.shape[3]
+    groups = maps.shape[1]
+    specs = [
+        pl.BlockSpec((1,) + shape[1:], lambda x, c: (x, 0, 0, 0)),
+        every_source(maps),
+        pl.BlockSpec((groups, 1) + mask.shape[2:], lambda x, c: (0, first + c, 0, 0)),
+    ] + [whole(t.shape) for t in tables]
+    cells = groups * coils * shape[0] * shape[2] * shape[3]
+    return plane_call(
+        normal_planes, (guess, maps, mask) + tables, specs, shape, coils, cells * 4096, cells * 4
+    )
+
+
+def back_of(data, maps, table, shape, data_start, maps_start, coils):
+    specs = [every_source(data, data_start), every_source(maps, maps_start), whole(table.shape)]
+    cells = maps.shape[1] * coils * shape[0] * shape[2] * shape[3]
+    return plane_call(data_planes, (data, maps, table), specs, shape, coils, cells * 1024, cells * 8)
+
+
+EVERY = ("slab", "coil")
+
+
+def swap(blocks):
+    return lax.all_to_all(blocks, EVERY, split_axis=0, concat_axis=0, tiled=True)
+
+
+def tv_planes(guess, duals, first, total):
+    here, ahead = guess[:-1], guess[1:]
+    pos = first - 1 + lax.broadcasted_iota(jnp.int32, (here.shape[0], 1, 1, 1), 0)
+    grad_x = jnp.where(pos < total - 1, ahead - here, 0.0)
+    grad_z = jnp.concatenate([here[:, :, 1:] - here[:, :, :-1], jnp.zeros_like(here[:, :, :1])], 2)
+    grad_y = jnp.concatenate([here[..., 1:] - here[..., :-1], jnp.zeros_like(here[..., :1])], 3)
+    moved = [dual_step * grad for grad in (grad_z, grad_y, grad_x)]
+    if duals is not None:
+        moved = [dual + step for dual, step in zip(duals, moved)]
+    magnitude = jnp.sqrt(sum(jnp.sum(w * w, 1, keepdims=True) for w in moved))
+    factor = 1.0 / jnp.maximum(1.0, magnitude / tv_weight)
+    duals = [w * factor for w in moved]
+    dual_z, dual_y = duals[0][1:], duals[1][1:]
+    dual_x = jnp.where(pos < 0, 0.0, duals[2])
+    spread_x = dual_x[:-1] - dual_x[1:]
+    spread_z = jnp.concatenate([jnp.zeros_like(dual_z[:, :, :1]), dual_z[:, :, :-1]], 2) - dual_z
+    spread_y = jnp.concatenate([jnp.zeros_like(dual_y[..., :1]), dual_y[..., :-1]], 3) - dual_y
+    return duals, spread_z + spread_y + spread_x
+
+
+def by_planes(kspace_data, coil_maps, sample_mask, initial_image):
+    slabs = lax.axis_size("slab")
+    groups = lax.axis_size("coil")
+    devices = slabs * groups
+    coils, _, depth, ny, nx = coil_maps.shape
+    nz, shares = kspace_data.shape[2:4]
+    rows = initial_image.shape[2]
+    width = nx // devices
+    me = lax.axis_index(EVERY)
+    forward_y, inverse_y = dft_table(ny, False), dft_table(ny, True)
+    forward_z, inverse_z = dft_table(nz, False), dft_table(nz, True)
+    inverse_x = jnp.asarray(dft_table(nx, True))
+    tables = (on_right(forward_y), on_left(forward_z), on_left(inverse_z), on_right(inverse_y))
+    few = max(1, coils // 8)
+    hold = lax.optimization_barrier
+
+    def packed(array):
+        return array.reshape((devices, width) + array.shape[1:])
+
+    def sent(array):
+        return swap(array).reshape((slabs, groups) + array.shape[1:])
+
+    def in_place(array):
+        order = Layout(major_to_minor=tuple(range(array.ndim)))
+        return with_layout_constraint(array, order)
+
+    first_maps = packed(coil_maps[:few].transpose(4, 0, 1, 2, 3))
+    later_maps = packed(coil_maps[few:].transpose(4, 0, 1, 2, 3))
+    image = initial_image.reshape(-1, nx).astype(bf16).T.reshape(devices, width, -1)
+    edge = jnp.zeros_like(image[:1, :1])
+    image = jnp.concatenate(
+        [
+            jnp.concatenate([edge, image[:-1, -1:]], 0),
+            image,
+            jnp.concatenate([image[1:, :1], edge], 0),
+        ],
+        1,
+    )
+    joined = jnp.concatenate(
+        [first_maps.reshape(devices, -1, ny), image.reshape(devices, -1, ny)], 1
+    )
+    joined = swap(joined)
+    mask = lax.all_gather(sample_mask.astype(bf16), "slab", axis=2, tiled=True)
+    joined, mask, later_maps = hold((joined, mask, later_maps))
+    later_maps = sent(later_maps)
+
+    image = joined[:, -image.shape[1] * image.shape[2] // ny :]
+    first_maps = joined[:, : joined.shape[1] - image.shape[1]]
+    first_maps = first_maps.reshape(slabs, groups, width, few, 2, depth, ny)
+    image = image.reshape(slabs, groups, width + 2, 2, depth, rows)
+    image = image.transpose(2, 3, 0, 4, 1, 5).reshape(width + 2, 2, nz, ny).astype(f32)
+    own = image[1:-1]
+
+    data = kspace_data * sample_mask[:, None, :, :, None].astype(bf16)
+    data = jnp.einsum("ckzyx,kjxw->cjzyw", data, inverse_x, preferred_element_type=f32).astype(bf16)
+    data = jnp.einsum(
+        "ckzyx,kjzw->xcjyw", data, jnp.asarray(inverse_z), preferred_element_type=f32
+    ).astype(bf16)
+    back_edges = sorted({0, coils - few, coils})
+    data = [in_place(packed(data[:, a:b])) for a, b in zip(back_edges[:-1], back_edges[1:])]
+    mask, data = hold((mask, data))
+    masks = []
+    for half in (mask[: coils // 2], mask[coils // 2 :]):
+        if masks:
+            half, _ = hold((half, masks[0]))
+        masks.append(lax.all_gather(half, "coil", axis=0))
+    mask = jnp.concatenate(masks, 1)
+    first_maps, later_maps, mask, data = hold((first_maps, later_maps, mask, data))
+
+    maps = [(first_maps, 0), (later_maps, few)]
+    scale = dual_step / (1.0 + dual_step)
+    normal = sum(normal_of(own, m, mask, a, tables) for m, a in maps)
+    duals, spread = tv_planes(image, None, me * width, nx)
+    back = 0.0
+    ready = None
+    for piece, (a, b) in enumerate(zip(back_edges[:-1], back_edges[1:])):
+        got = sent(data[piece])
+        if ready is not None:
+            back += ready
+        if piece == 0:
+            got, normal, duals, spread, data = hold((got, normal, duals, spread, data))
+        elif piece < len(data) - 1:
+            got, back, data = hold((got, back, data))
+        else:
+            got, back = hold((got, back))
+        ready = None
+        for m, start in maps:
+            low, high = max(a, start), min(b, start + m.shape[3])
+            if low < high:
+                term = back_of(
+                    got, m, tables[3], own.shape, low - a, low - start, high - low
+                )
+                ready = term if ready is None else ready + term
+    back += ready
+    data_grad = scale * (normal - back)
+    change = -primal_step * (data_grad + spread)
+    guess = own + 2.0 * change
+    line = [g * slabs + s for s in range(slabs) for g in range(groups)]
+    before = lax.ppermute(guess[-1:], ("coil", "slab"), list(zip(line[:-1], line[1:])))
+    after = lax.ppermute(guess[:1], ("coil", "slab"), list(zip(line[1:], line[:-1])))
+    normal = sum(normal_of(guess, m, mask, a, tables) for m, a in maps)
+    _, spread = tv_planes(jnp.concatenate([before, guess, after], 0), duals, me * width, nx)
+    data_grad = data_grad / (1.0 + dual_step) + scale * (normal - back)
+    final = (own + change - primal_step * (data_grad + spread)).astype(bf16)
+    final = final.reshape(width, 2, slabs, depth, groups, rows).transpose(2, 4, 0, 1, 3, 5)
+    final = swap(final.reshape(devices, -1)).reshape(nx, -1).T
+    return final.reshape(initial_image.shape).astype(f32)
+
+
 def solution(mesh):
     placed = (
         P("coil", None, None, "slab", None),
@@ -269,8 +530,14 @@
         P("coil", None, "slab"),
         P(None, "slab", "coil", None),
     )
+
+    def on_each(kspace_data, coil_maps, sample_mask, initial_image):
+        whole_planes = coil_maps.shape[4] % mesh.size == 0
+        form = by_planes if whole_planes else on_device
+        return form(kspace_data, coil_maps, sample_mask, initial_image)
+
     return jax.shard_map(
-        on_device,
+        on_each,
         mesh=mesh,
         in_specs=placed,
         out_specs=P(None, "slab", "coil", None),

time: 749 us -> 501 us (0.67)
  waiting for transfers between devices: 364 us -> 204 us
  starting transfers between devices: 66.4 us -> 20.4 us
  local copies, waits for them, and re-layouts: 91 us -> 66.4 us
  other arithmetic: 41.3 us -> 26.8 us
  between operations: 14 us -> 1 us
  blocking collectives: 72.5 us -> 83.2 us
    psum x1 -> x0, waiting for transfers between devices: 100 us -> none  [on_device(): data_grad = lax.psum(scale * (normal - back_data), 'coil')]
    ppermute x4 -> x2, starting transfers between devices: 56.1 us -> 2.72 us  [the longest x1 1.42 us: by_planes(): lax.ppermute(guess[:1], ('coil', 'slab'), list(zip(line[1:], line[:-1])))]
    ppermute x4 -> x2, waiting for transfers between devices: 51.9 us -> 0.01 us  [the longest x1 0.01 us: by_planes(): lax.ppermute(guess[-1:], ('coil', 'slab'), list(zip(line[:-1], line[1:])))]
    reshape x6 -> x4, local copies, waits for them, and re-layouts: 42.3 us -> 1.22 us  [the longest x2 0.65 us: by_planes(): final.reshape(width, 2, slabs, depth, groups, rows)]
    all_gather x1 -> x3, blocking collectives: 30.9 us -> 66 us  [the longest x1 34 us: by_planes(): mask = lax.all_gather(sample_mask.astype(bf16), 'slab', axis=2, tiled=True)]
    reduce_scatter x1 -> x0, waiting for transfers between devices: 29.7 us -> none  [on_device(): lax.psum_scatter(share.swapaxes(2, 3), 'coil', scatter_dimension=2, tiled...]
    slice x9 -> x20, local copies, waits for them, and re-layouts: 2.25 us -> 30.6 us  [the longest x6 12.5 us: by_planes(): data[:, a:b]]
    all_to_all x2 -> x1, blocking collectives: 41.6 us -> 17.2 us  [swap(): lax.all_to_all(blocks, EVERY, split_axis=0, concat_axis=0, tiled=True)]
  transfers between devices with their start and end apart: 9 -> 6, of which waited for: 7 -> 3; matrix products, arithmetic and copies ran while one was open for 10% -> 17% of each run, Pallas kernels for 8% -> 16%
where the time goes in v1:
time: 501 us; the launch traced here: 495 us
  waiting for transfers between devices  204 us (41%)
  Pallas kernels  83.6 us (17%)
  blocking collectives  83.2 us (17%)
  local copies, waits for them, and re-layouts  66.4 us (13%)
  other arithmetic  26.8 us (5%)
  starting transfers between devices  20.4 us (4%)
  matrix products  9.24 us (2%)
    all_to_all x4, waiting for transfers between devices, swap(): lax.all_to_all(blocks, EVERY, split_axis=0, concat_axis=0, tiled=True)  204 us
    pallas_call x7, Pallas kernels, plane_call(): pl.pallas_call(kernel, out_shape=jax.ShapeDtypeStruct(shape, f32), grid=(...  83.6 us
    all_gather x1, blocking collectives, by_planes(): mask = lax.all_gather(sample_mask.astype(bf16), 'slab', axis=2, tiled=True)  34 us
    all_gather x2, blocking collectives, by_planes(): masks.append(lax.all_gather(half, 'coil', axis=0))  32 us
    all_to_all x4, starting transfers between devices, swap(): lax.all_to_all(blocks, EVERY, split_axis=0, concat_axis=0, tiled=True)  17.7 us
    all_to_all x1, blocking collectives, swap(): lax.all_to_all(blocks, EVERY, split_axis=0, concat_axis=0, tiled=True)  17.2 us
    unnamed x32, local copies, waits for them, and re-layouts  14.3 us
    slice x6, local copies, waits for them, and re-layouts, by_planes(): data[:, a:b]  12.5 us
  transfers between devices with their start and end apart: 6, of which 3 were waited for; matrix products, arithmetic and copies ran while one was open for 17% of the time, Pallas kernels for 16%

profile of v1, /device:TPU:0, one launch (start us, length us, event | category | flops | bytes accessed | tf_op | source)
XLA Modules:
  0.0 494.6 jit_solution(13178611216562367215)
XLA Ops:
  0.0 1.1 convert_element_type.50
  1.5 0.5 fusion.17
  2.0 0.5 reshape.101
  2.5 1.3 slice.123
  3.8 1.0 copy.88
  4.8 1.3 pad_maximum_fusion.1
  6.1 7.3 %all-to-all-start = ((bf16[32,176,128]{2,1,0:T(8,128)(2,1)}), bf16[32,176,128]{2,1,0:T(8,128)(2,1)S(1)}, u32[]{:S(2)}, u32[]{:S(2)}) async-start(bf16[32,176,128]{2,1,0:T(8,128)(2,1)} %pad_maximum_fusion.1), calls=%async_computation | async-start | bytes 2883584 | tf_op jit(solution)/shard_map/all_to_all | solution.py:394
  13.5 9.2 %slice.126 = bf16[7,2,16,128,128]{4,3,2,1,0:T(8,128)(2,1)} slice(bf16[8,2,16,128,128]{4,3,2,1,0:T(8,128)(2,1)} %param.11), slice={[1:8], [0:2], [0:16], [0:128], [0:128]} | slice | bytes 14680064 | tf_op jit(solution)/shard_map/slice | solution.py:444
  22.7 12.0 %copy.89 = bf16[7,2,16,128,128]{3,2,1,0,4:T(8,128)(2,1)} copy(bf16[7,2,16,128,128]{4,3,2,1,0:T(8,128)(2,1)} %slice.126) | data formatting | bytes 14680064
  34.7 34.0 %all_gather.15 = bf16[8,128,128]{1,0,2:T(8,128)(2,1)S(1)} all-gather(bf16[8,128,16]{1,0,2:T(8,128)(2,1)S(1)} %copy_convert_fusion), channel_id=1, replica_groups=mesh['coil'=4,'slab'=8] {'slab'}, dimensions={2}, use_global_device_ids=true | all-gather | bytes 294912 | tf_op jit(solution)/shard_map/all_gather | solution.py:459
  68.7 3.9 all-to-all-start.1
  72.5 0.2 copy.67
  72.7 7.9 %multiply_bitcast_fusion = bf16[8,2,128,16,128,1]{4,3,2,1,0,5:T(8,128)(2,1)} fusion(bf16[8,2,128,16,128]{4,3,2,1,0:T(8,128)(2,1)} %param.10, bf16[8,128,16]{2,1,0:T(8,128)(2,1)S(1)} %copy.67), kind=kLoop, calls=%fused_computation.4 | loop fusion | flops 4194304 | bytes 16809984 | tf_op jit(solution)/shard_map/mul | solution.py:470
  80.6 9.2 %fusion.2 = bf16[128,8,2,16,128]{4,0,2,3,1:T(8,128)(2,1)} fusion(bf16[2,2,128,128,1,1]{3,2,0,1,5,4:T(8,128)(2,1)S(1)} %copy-done.13, bf16[8,2,128,16,128,1]{4,3,2,1,0,5:T(8,128)(2,1)} %multiply_bitcast_fusion), kind=kOutput, calls=%fused_computation.5 | convolution fusion | flops 4303355904 | bytes 16908288 | tf_op jit(solution)/shard_map/ckzyx,kjzw->xcjyw/dot_general | solution.py:472
  89.9 3.1 slice-done.1
  93.0 7.7 %copy.70 = bf16[128,7,2,16,128]{4,3,2,1,0:T(8,128)(2,1)} copy(bf16[128,7,2,16,128]{4,0,2,3,1:T(8,128)(2,1)S(1)} %slice-done.1) | data formatting | bytes 14680064 | tf_op jit(solution)/shard_map/slice | solution.py:476
  100.7 1.7 copy.71
  102.7 24.7 %all-gather = bf16[16,128,128]{2,1,0:T(8,128)(2,1)S(1)} all-gather(bf16[4,128,128]{2,1,0:T(8,128)(2,1)S(1)} %copy.72), channel_id=2, replica_groups=mesh['coil'=4,'slab'=8] {'coil'}, dimensions={0}, use_global_device_ids=true | all-gather | bytes 655360 | tf_op jit(solution)/shard_map/all_gather | solution.py:482
  127.6 7.3 %all-gather.1 = bf16[16,128,128]{2,1,0:T(8,128)(2,1)S(1)} all-gather(bf16[4,128,128]{2,1,0:T(8,128)(2,1)S(1)} %copy.73), channel_id=3, replica_groups=mesh['coil'=4,'slab'=8] {'coil'}, dimensions={0}, use_global_device_ids=true | all-gather | bytes 655360 | tf_op jit(solution)/shard_map/all_gather | solution.py:482
  135.0 100.6 %all-to-all-done.1 = bf16[32,4,7,2,16,128]{5,4,3,2,1,0:T(8,128)(2,1)} async-done(((bf16[32,4,7,2,16,128]{5,4,3,2,1,0:T(8,128)(2,1)}), bf16[32,4,7,2,16,128]{5,4,3,2,1,0:T(8,128)(2,1)}, u32[]{:S(2)}, u32[]{:S(2)}) %all-to-all-start.1) | async-done | bytes 7340064 | tf_op jit(solution)/shard_map/all_to_all | solution.py:394
  235.5 3.9 all-to-all-start.2
  239.4 1.1 slice_convert_fusion
  240.5 2.4 reshape.111
  242.9 1.9 slice.161
  244.8 5.7 %copy.74 = f32[6,2,8,16,4,32]{5,4,3,2,1,0:T(4,128)} copy(f32[6,2,8,16,4,32]{5,3,1,0,4,2:T(8,128)} %bitcast.61) | data formatting | bytes 1572864 | tf_op jit(solution)/shard_map/convert_element_type | solution.py:467
  250.5 2.7 copy.66
  253.1 2.4 slice.129.guess_ref
  255.6 2.8 convert_element_type.60
  258.4 3.2 slice_subtract_fusion
  261.6 3.2 copy.75
  264.8 3.3 sub.56
  268.2 0.2 slice_subtract_fusion.1
  268.5 0.2 multiply_reduce_fusion.4
  268.6 1.3 multiply_reduce_fusion.3
  270.1 1.1 broadcast_select_fusion
  271.3 0.8 copy-done.4
  272.1 1.0 fusion.25
  273.1 3.8 shard_map.100
  276.9 26.7 %shard_map.101 = f32[4,2,128,128]{3,2,1,0:T(8,128)S(1)} custom-call(f32[4,2,128,128]{3,2,1,0:T(8,128)S(1)} %slice.129.guess_ref, bf16[8,4,4,7,2,16,128]{6,5,4,3,2,1,0:T(8,128)(2,1)} %bitcast.8.maps_ref, bf16[4,8,128,128]{3,2,1,0:T(8,128)(2,1)S(1)} %pad_maximum_fusion.2.mask_ref, bf16[256,256]{1,0:T(8,128)(2,1)S(1)} %copy-done.3, ...), custom_call_target="tpu_custom_call" | custom-call | flops 7516192768 | bytes 7340032 | tf_op jit(solution)/shard_map/pallas_call | solution.py:349
  303.6 0.9 add.120
  304.6 97.9 %all-to-all-done.2 = bf16[32,4,7,2,16,128]{5,4,3,2,1,0:T(8,128)(2,1)} async-done(((bf16[32,4,7,2,16,128]{5,4,3,2,1,0:T(8,128)(2,1)}), bf16[32,4,7,2,16,128]{5,4,3,2,1,0:T(8,128)(2,1)}, u32[]{:S(2)}, u32[]{:S(2)}) %all-to-all-start.2) | async-done | bytes 7340064 | tf_op jit(solution)/shard_map/all_to_all | solution.py:394
  402.4 2.6 all-to-all-start.3
  405.1 2.9 shard_map.102
  408.0 17.0 %shard_map.103 = f32[4,2,128,128]{3,2,1,0:T(8,128)S(1)} custom-call(bf16[8,4,4,7,2,16,128]{6,5,4,3,2,1,0:T(8,128)(2,1)} %bitcast.23.data_ref, bf16[8,4,4,7,2,16,128]{6,5,4,3,2,1,0:T(8,128)(2,1)} %bitcast.8.maps_ref, bf16[256,256]{1,0:T(8,128)(2,1)S(1)} %copy-done), custom_call_target="tpu_custom_call" | custom-call | flops 1610612736 | bytes 12582912 | tf_op jit(solution)/shard_map/pallas_call | solution.py:349
  424.9 0.9 add.128
  425.8 5.5 %all-to-all-done.3 = bf16[32,4,1,2,16,128]{5,4,3,2,1,0:T(8,128)(2,1)S(1)} async-done(((bf16[32,4,1,2,16,128]{5,4,3,2,1,0:T(8,128)(2,1)}), bf16[32,4,1,2,16,128]{5,4,3,2,1,0:T(8,128)(2,1)S(1)}, u32[]{:S(2)}, u32[]{:S(2)}) %all-to-all-start.3) | async-done | bytes 1048608 | tf_op jit(solution)/shard_map/all_to_all | solution.py:394
  431.3 3.0 shard_map.104
  434.6 1.3 collective-permute-start
  435.9 26.7 %shard_map.106 = f32[4,2,128,128]{3,2,1,0:T(8,128)S(1)} custom-call(f32[4,2,128,128]{3,2,1,0:T(8,128)S(1)} %get-tuple-element.47.guess_ref, bf16[8,4,4,7,2,16,128]{6,5,4,3,2,1,0:T(8,128)(2,1)} %bitcast.8.maps_ref, bf16[4,8,128,128]{3,2,1,0:T(8,128)(2,1)S(1)} %copy-done.2, bf16[256,256]{1,0:T(8,128)(2,1)S(1)} %copy-done.3, bf16[256,256]{1,0:T(8,128)(2,1)S(1)} %copy-done, ...), custom_call_target="tpu_custom_call" | custom-call | flops 7516192768 | bytes 7340032 | tf_op jit(solution)/shard_map/pallas_call | solution.py:349
  462.6 1.4 collective-permute-start.1
  464.0 3.6 shard_map.105
  467.6 0.2 fusion.11
  468.2 0.2 multiply_reduce_fusion
  468.6 0.5 broadcast_multiply_fusion.1
  469.2 0.6 fusion.23
  469.8 0.4 reshape.109
  470.3 0.2 copy.98
  470.5 0.6 all_to_all.24
  471.1 0.5 broadcast.142
  471.6 2.2 reduce.2
  474.0 17.2 %all_to_all.30 = bf16[32,2,2048]{2,1,0:T(2,128)(2,1)S(1)} all-to-all(bf16[32,2,2048]{2,1,0:T(2,128)(2,1)S(1)} %reshape.121), channel_id=1, replica_groups=mesh['coil'=4,'slab'=8] {'slab','coil'}, dimensions={0} | all-to-all | bytes 524288 | tf_op jit(solution)/shard_map/all_to_all | solution.py:394
  491.3 0.3 reshape.122
  491.5 1.5 convert_reduce_fusion
  493.2 1.0 copy.78
  (57 shorter events, 2.5 us)
Async XLA Ops:
  6.1 62.6 %all-to-all-start = ((bf16[32,176,128]{2,1,0:T(8,128)(2,1)}), bf16[32,176,128]{2,1,0:T(8,128)(2,1)S(1)}, u32[]{:S(2)}, u32[]{:S(2)}) async-start(bf16[32,176,128]{2,1,0:T(8,128)(2,1)} %pad_maximum_fusion.1), calls=%async_computation | async-start | bytes 2883584 | tf_op jit(solution)/shard_map/all_to_all | solution.py:394
  22.7 12.0 %copy-start.12 = (s32[8,128,16]{1,2,0:T(8,128)S(1)}, s32[8,128,16]{1,2,0:T(8,128)}, u32[]{:S(2)}) copy-start(s32[8,128,16]{1,2,0:T(8,128)} %param.12) | copy-start | bytes 196612
  68.7 33.7 %copy-start.8 = (bf16[32,176,128]{2,1,0:T(8,128)(2,1)}, bf16[32,176,128]{2,1,0:T(8,128)(2,1)S(1)}, u32[]{:S(2)}) copy-start(bf16[32,176,128]{2,1,0:T(8,128)(2,1)S(1)} %all-to-all-done) | copy-start | bytes 4325380
  68.7 166.9 %all-to-all-start.1 = ((bf16[32,4,7,2,16,128]{5,4,3,2,1,0:T(8,128)(2,1)}), bf16[32,4,7,2,16,128]{5,4,3,2,1,0:T(8,128)(2,1)}, u32[]{:S(2)}, u32[]{:S(2)}) async-start(bf16[32,4,7,2,16,128]{5,4,3,2,1,0:T(8,128)(2,1)} %bitcast.64), calls=%async_computation.1 | async-start | bytes 14680064 | tf_op jit(solution)/shard_map/all_to_all | solution.py:394
  72.7 7.9 %copy-start.13 = (bf16[2,2,128,128,1,1]{3,2,0,1,5,4:T(8,128)(2,1)S(1)}, bf16[2,2,128,128,1,1]{3,2,0,1,5,4:T(8,128)(2,1)}, u32[]{:S(2)}) copy-start(bf16[2,2,128,128,1,1]{3,2,0,1,5,4:T(8,128)(2,1)} %constant.74) | copy-start | bytes 393220
  89.9 3.1 slice-start.1
  93.0 7.7 %slice-start = ((bf16[128,8,2,16,128]{4,0,2,3,1:T(8,128)(2,1)}), bf16[128,1,2,16,128]{4,0,2,3,1:T(8,128)(2,1)S(1)}, s32[]{:S(2)}) async-start(bf16[128,8,2,16,128]{4,0,2,3,1:T(8,128)(2,1)} %fusion.2), calls=%async_computation.5 | async-start | bytes 2097152 | tf_op jit(solution)/shard_map/slice | solution.py:476
  134.9 142.0 %copy-start.1 = (bf16[4,8,128,128]{3,2,1,0:T(8,128)(2,1)}, bf16[4,8,128,128]{3,2,1,0:T(8,128)(2,1)S(1)}, u32[]{:S(2)}) copy-start(bf16[4,8,128,128]{3,2,1,0:T(8,128)(2,1)S(1)} %pad_maximum_fusion.2.mask_ref) | copy-start | bytes 3145732
  235.5 166.9 %all-to-all-start.2 = ((bf16[32,4,7,2,16,128]{5,4,3,2,1,0:T(8,128)(2,1)}), bf16[32,4,7,2,16,128]{5,4,3,2,1,0:T(8,128)(2,1)}, u32[]{:S(2)}, u32[]{:S(2)}) async-start(bf16[32,4,7,2,16,128]{5,4,3,2,1,0:T(8,128)(2,1)} %bitcast.63), calls=%async_computation.2 | async-start | bytes 14680064 | tf_op jit(solution)/shard_map/all_to_all | solution.py:394
  268.1 2.0 copy-start.6
  268.4 4.7 copy-start
  268.4 4.7 copy-start.3
  271.2 0.9 copy-start.4
  402.4 28.8 %all-to-all-start.3 = ((bf16[32,4,1,2,16,128]{5,4,3,2,1,0:T(8,128)(2,1)}), bf16[32,4,1,2,16,128]{5,4,3,2,1,0:T(8,128)(2,1)S(1)}, u32[]{:S(2)}, u32[]{:S(2)}) async-start(bf16[32,4,1,2,16,128]{5,4,3,2,1,0:T(8,128)(2,1)} %bitcast.65), calls=%async_computation.3 | async-start | bytes 2097152 | tf_op jit(solution)/shard_map/all_to_all | solution.py:394
  431.3 3.1 copy-start.9
  431.3 3.1 copy-start.10
  431.3 3.1 copy-start.11
  431.3 4.6 copy-start.2
  434.6 33.0 %collective-permute-start = (f32[1,2,128,128]{3,2,1,0:T(8,128)S(1)}, f32[1,2,128,128]{3,2,1,0:T(8,128)S(1)}, u32[]{:S(2)}, u32[]{:S(2)}) collective-permute-start(f32[1,2,128,128]{3,2,1,0:T(8,128)S(1)} %get-tuple-element.52), channel_id=1, source_target_pairs={{0,8},{8,16},{16,24},{24,1},{1,9},{9,17},{17,25},{25,2},{2,10},{10... | collective-permute-start | bytes 393224 | tf_op jit(solution)/shard_map/ppermute | solution.py:515
  462.6 5.5 %copy-start.5 = (f32[5,2,128,128]{3,2,1,0:T(8,128)S(1)}, f32[5,2,128,128]{3,2,1,0:T(8,128)}, u32[]{:S(2)}) copy-start(f32[5,2,128,128]{3,2,1,0:T(8,128)} %copy-done.4) | copy-start | bytes 1966084
  462.6 5.6 %copy-start.7 = (f32[5,2,128,128]{3,2,1,0:T(8,128)S(1)}, f32[5,2,128,128]{3,2,1,0:T(8,128)}, u32[]{:S(2)}) copy-start(f32[5,2,128,128]{3,2,1,0:T(8,128)} %get-tuple-element.46) | copy-start | bytes 1966084
  462.6 5.6 %collective-permute-start.1 = (f32[1,2,128,128]{3,2,1,0:T(8,128)S(1)}, f32[1,2,128,128]{3,2,1,0:T(8,128)S(1)}, u32[]{:S(2)}, u32[]{:S(2)}) collective-permute-start(f32[1,2,128,128]{3,2,1,0:T(8,128)S(1)} %get-tuple-element.51), channel_id=1, source_target_pairs={{8,0},{16,8},{24,16},{1,24},{9,1},{17,9},{25,17},{2,25},{10,2},{18... | collective-permute-start | bytes 393224 | tf_op jit(solution)/shard_map/ppermute | solution.py:516

commit v2 on v1

--- a/solution.py
+++ b/solution.py
@@ -334,15 +334,149 @@
     combine_planes(out_ref, maps, dot(pieces, gy_ref[...]))
 
 
-def data_planes(data_ref, maps_ref, gy_ref, out_ref):
+def back_planes(out_ref, maps_ref, gz_ref, gy_ref, spectra):
+    nz, ny = out_ref.shape[2:]
+    shares = spectra[0][0].shape[0]
+    spectrum = jnp.concatenate([jnp.concatenate(parts, 1) for parts in spectra], 0)
+    pieces = dot(spectrum, gz_ref[...]).astype(bf16)
     columns = jnp.concatenate(
         [
-            jnp.concatenate([all_planes(data_ref, c, 0), all_planes(data_ref, c, 1)], 0)
-            for c in range(data_ref.shape[1])
-        ],
-        1,
+            jnp.concatenate(
+                [
+                    pieces[c * shares : (c + 1) * shares, j * nz : (j + 1) * nz]
+                    for c in range(len(spectra))
+                ],
+                1,
+            )
+            for j in range(2)
+        ],
+        0,
     )
     combine_planes(out_ref, planes_of(maps_ref), dot(columns, gy_ref[...], ((0,), (0,))))
+
+
+def dense_kernel(data_ref, maps_ref, gz_ref, gy_ref, out_ref):
+    spectra = [
+        (all_planes(data_ref, c, 0), all_planes(data_ref, c, 1)) for c in range(data_ref.shape[1])
+    ]
+    back_planes(out_ref, maps_ref, gz_ref, gy_ref, spectra)
+
+
+def lanes_at(array, place):
+    return jnp.take_along_axis(array, place, 1, mode="promise_in_bounds")
+
+
+def sparse_kernel(data_ref, code_ref, maps_ref, gz_ref, gy_ref, out_ref):
+    half = data_ref.shape[4] // 2
+    spectra = []
+    for coil in range(data_ref.shape[1]):
+        lines = data_ref[:, coil, 0, 0].astype(f32)
+        lines = [
+            lines[:, j * half : (j + 1) * half].reshape(-1, lines.shape[2]) for j in range(2)
+        ]
+        count = lines[0].shape[0]
+        codes = [code_ref[coil, 0, h * count : (h + 1) * count] for h in range(2)]
+        spectra.append(
+            [
+                jnp.concatenate(
+                    [
+                        jnp.where(code >= 0, lanes_at(line, jnp.maximum(code, 0)), 0.0)
+                        for code in codes
+                    ],
+                    0,
+                ).astype(bf16)
+                for line in lines
+            ]
+        )
+    back_planes(out_ref, maps_ref, gz_ref, gy_ref, spectra)
+
+
+def select_kernel(pick_ref, data_ref, out_ref):
+    half = data_ref.shape[3] // 2
+    lanes = data_ref.shape[4]
+
+    def one(plane_index, _):
+        for coil in range(data_ref.shape[1]):
+            pick = pick_ref[coil]
+            later = pick >= lanes
+            place = jnp.where(later, pick - lanes, pick)
+            parts = []
+            for part in range(2):
+                lines = data_ref[plane_index, coil, part].astype(f32)
+                parts.append(
+                    jnp.where(later, lanes_at(lines[half:], place), lanes_at(lines[:half], place))
+                )
+            out_ref[plane_index, coil] = jnp.concatenate(parts, 0).astype(bf16)
+        return 0
+
+    lax.fori_loop(0, data_ref.shape[0], one, 0)
+
+
+def selected(data, pick):
+    planes, coils, _, shares, lanes = data.shape
+    step = max(n for n in (1, 2, 4, 8) if planes % n == 0)
+    return pl.pallas_call(
+        select_kernel,
+        out_shape=jax.ShapeDtypeStruct((planes, coils, shares, lanes), bf16),
+        grid=(planes // step,),
+        in_specs=[
+            pl.BlockSpec(pick.shape, lambda x: (0, 0, 0)),
+            pl.BlockSpec((step,) + data.shape[1:], lambda x: (x, 0, 0, 0, 0)),
+        ],
+        out_specs=pl.BlockSpec((step, coils, shares, lanes), lambda x: (x, 0, 0, 0)),
+        compiler_params=pltpu.CompilerParams(dimension_semantics=("arbitrary",)),
+        cost_estimate=pl.CostEstimate(
+            flops=data.size * 64, bytes_accessed=data.size * 3, transcendentals=0
+        ),
+    )(pick, data)
+
+
+def share_kernel(own_ref, all_ref, send_sem, recv_sem):
+    count = lax.axis_size("slab")
+    slab, coil = lax.axis_index("slab"), lax.axis_index("coil")
+
+    def device(step):
+        return (coil, lax.rem(slab + step, count))
+
+    barrier = pltpu.get_barrier_semaphore()
+    for step in range(1, count):
+        pl.semaphore_signal(
+            barrier, inc=1, device_id=device(step), device_id_type=pl.DeviceIdType.MESH
+        )
+    pl.semaphore_wait(barrier, count - 1)
+    copies = [
+        pltpu.make_async_remote_copy(
+            own_ref,
+            all_ref.at[slab],
+            send_sem.at[step - 1],
+            recv_sem.at[step - 1],
+            device_id=device(step),
+            device_id_type=pl.DeviceIdType.MESH,
+        )
+        for step in range(1, count)
+    ]
+    for copy in copies:
+        copy.start()
+    all_ref[slab] = own_ref[...]
+    for copy in copies:
+        copy.wait()
+
+
+def shared(own, slabs):
+    return pl.pallas_call(
+        share_kernel,
+        out_shape=jax.ShapeDtypeStruct((slabs,) + own.shape, own.dtype),
+        in_specs=[pl.BlockSpec(memory_space=pltpu.VMEM)],
+        out_specs=pl.BlockSpec(memory_space=pltpu.VMEM),
+        scratch_shapes=[
+            pltpu.SemaphoreType.DMA((slabs - 1,)),
+            pltpu.SemaphoreType.DMA((slabs - 1,)),
+        ],
+        compiler_params=pltpu.CompilerParams(collective_id=0, has_side_effects=True),
+        cost_estimate=pl.CostEstimate(
+            flops=own.size * 64, bytes_accessed=own.size * 32, transcendentals=0
+        ),
+    )(own)
 
 
 def plane_call(kernel, operands, specs, shape, steps, flops, nbytes):
@@ -381,13 +515,40 @@
     )
 
 
-def back_of(data, maps, table, shape, data_start, maps_start, coils):
-    specs = [every_source(data, data_start), every_source(maps, maps_start), whole(table.shape)]
-    cells = maps.shape[1] * coils * shape[0] * shape[2] * shape[3]
-    return plane_call(data_planes, (data, maps, table), specs, shape, coils, cells * 1024, cells * 8)
+def back_of(data, code, maps, tables, shape, start):
+    coils = data.shape[3]
+    groups = maps.shape[1]
+    operands, specs = [data], []
+    if code is None:
+        specs.append(every_source(data))
+    else:
+        slabs, _, _, _, shares, lanes = data.shape
+        specs.append(
+            pl.BlockSpec(
+                (slabs, groups, 1, 1, shares, lanes), lambda x, c: (0, 0, x, c, 0, 0)
+            )
+        )
+        operands.append(code[0])
+        first = code[1]
+        specs.append(
+            pl.BlockSpec((groups, 1) + code[0].shape[2:], lambda x, c: (0, first + c, 0, 0))
+        )
+    operands += (maps,) + tables
+    specs += [every_source(maps, start)] + [whole(t.shape) for t in tables]
+    cells = groups * coils * shape[0] * shape[2] * shape[3]
+    kernel = dense_kernel if code is None else sparse_kernel
+    return plane_call(kernel, operands, specs, shape, coils, cells * 2048, cells * 8)
 
 
 EVERY = ("slab", "coil")
+LANES = 128
+SUBLANES = 8
+
+
+def ranks(flags):
+    before = jnp.triu(jnp.ones((flags.shape[-1],) * 2, bf16))
+    counts = jnp.einsum("...k,kl->...l", flags.astype(bf16), before, preferred_element_type=f32)
+    return counts.astype(jnp.int32)
 
 
 def swap(blocks):
@@ -456,7 +617,7 @@
         [first_maps.reshape(devices, -1, ny), image.reshape(devices, -1, ny)], 1
     )
     joined = swap(joined)
-    mask = lax.all_gather(sample_mask.astype(bf16), "slab", axis=2, tiled=True)
+    mask = shared(sample_mask.swapaxes(1, 2).astype(bf16), slabs)
     joined, mask, later_maps = hold((joined, mask, later_maps))
     later_maps = sent(later_maps)
 
@@ -468,46 +629,85 @@
     own = image[1:-1]
 
     data = kspace_data * sample_mask[:, None, :, :, None].astype(bf16)
-    data = jnp.einsum("ckzyx,kjxw->cjzyw", data, inverse_x, preferred_element_type=f32).astype(bf16)
-    data = jnp.einsum(
-        "ckzyx,kjzw->xcjyw", data, jnp.asarray(inverse_z), preferred_element_type=f32
-    ).astype(bf16)
-    back_edges = sorted({0, coils - few, coils})
-    data = [in_place(packed(data[:, a:b])) for a, b in zip(back_edges[:-1], back_edges[1:])]
-    mask, data = hold((mask, data))
+    data = jnp.einsum("ckzyx,kjxw->wcjyz", data, inverse_x, preferred_element_type=f32)
+    data = in_place(data.astype(bf16))
+    half = shares // 2
+    small = half == SUBLANES and nz == LANES
+    if small:
+        sampled = sample_mask.swapaxes(1, 2)
+        rank = ranks(sampled)
+        begin = rank[:, :half, -1:]
+        kz = lax.broadcasted_iota(jnp.int32, (1, 1, nz), 2)
+        slot = jnp.where(sampled > 0, rank, 0)
+        slot = jnp.concatenate([slot[:, :half], jnp.where(sampled[:, half:] > 0, begin + slot[:, half:], 0)], 2)
+        spot = jnp.arange(2 * nz, dtype=jnp.int32)
+        pick = jnp.sum(
+            jnp.where(slot[:, :, None, :] == 1 + kz[..., None], spot, 0), 3, dtype=jnp.int32
+        )
+        lines = selected(data, pick)
+        data, lines, mask = hold((data, lines, mask))
+    else:
+        data, mask = hold((data, mask))
+    mask = mask.swapaxes(0, 1).reshape(coils, slabs * shares, nz)
     masks = []
-    for half in (mask[: coils // 2], mask[coils // 2 :]):
+    for part in (mask[: coils // 2], mask[coils // 2 :]):
         if masks:
-            half, _ = hold((half, masks[0]))
-        masks.append(lax.all_gather(half, "coil", axis=0))
+            part, _ = hold((part, masks[0]))
+        masks.append(lax.all_gather(part, "coil", axis=0))
     mask = jnp.concatenate(masks, 1)
-    first_maps, later_maps, mask, data = hold((first_maps, later_maps, mask, data))
-
+
+    inverse = (on_right(inverse_z), on_right(inverse_y))
+    if small:
+        halves = mask.reshape(groups, coils, slabs, 2, half, nz).swapaxes(2, 3)
+        rank = ranks(halves)
+        begin = rank[:, :, :1, ..., -1:]
+        fits = jnp.max(begin + rank[:, :, 1:, ..., -1:]) <= nz
+        rank = jnp.concatenate([rank[:, :, :1], begin + rank[:, :, 1:]], 2)
+        code = jnp.where(halves > 0, rank - 1, -1).reshape(groups, coils, ny, nz)
+        order = np.arange(ny).reshape(slabs, 2, half).swapaxes(0, 1).reshape(-1)
+        sparse_inverse = (inverse[0], inverse[1].reshape(2, ny, -1)[:, order].reshape(2 * ny, -1))
+    mask = mask.swapaxes(2, 3)
+    duals, spread = tv_planes(image, None, me * width, nx)
+    normal = normal_of(own, first_maps, mask, 0, tables)
+    held = (first_maps, later_maps, mask, data, duals, spread, normal)
+    if small:
+        (first_maps, later_maps, mask, data, duals, spread, normal), lines, code = hold(
+            (held, lines, code)
+        )
+    else:
+        first_maps, later_maps, mask, data, duals, spread, normal = hold(held)
+
+    def finish(data, code, steps, inverse):
+        data = [packed(data[:, a:b]) for a, b in steps]
+        data = hold(data)
+        more = normal_of(own, later_maps, mask, few, tables)
+        back = ready = None
+        for piece, (a, b) in enumerate(steps):
+            got = sent(data[piece])
+            rest = data[piece + 1 :]
+            if ready is None:
+                got, more, rest = hold((got, more, rest))
+            else:
+                back = ready if back is None else back + ready
+                got, back, rest = hold((got, back, rest))
+            data[piece + 1 :] = rest
+            maps, start = (first_maps, a) if b <= few else (later_maps, a - few)
+            codes = None if code is None else (code, a)
+            ready = back_of(got, codes, maps, inverse, own.shape, start)
+        return more, ready if back is None else back + ready
+
+    def dense(_):
+        return finish(data, None, [(few, coils), (0, few)], inverse)
+
+    def sparse(_):
+        middle = few + (coils - few + 1) // 2
+        steps = [(few, middle), (middle, coils), (0, few)]
+        return finish(lines, code, steps, sparse_inverse)
+
+    more, back = lax.cond(fits, sparse, dense, 0) if small else dense(0)
+    normal = normal + more
     maps = [(first_maps, 0), (later_maps, few)]
     scale = dual_step / (1.0 + dual_step)
-    normal = sum(normal_of(own, m, mask, a, tables) for m, a in maps)
-    duals, spread = tv_planes(image, None, me * width, nx)
-    back = 0.0
-    ready = None
-    for piece, (a, b) in enumerate(zip(back_edges[:-1], back_edges[1:])):
-        got = sent(data[piece])
-        if ready is not None:
-            back += ready
-        if piece == 0:
-            got, normal, duals, spread, data = hold((got, normal, duals, spread, data))
-        elif piece < len(data) - 1:
-            got, back, data = hold((got, back, data))
-        else:
-            got, back = hold((got, back))
-        ready = None
-        for m, start in maps:
-            low, high = max(a, start), min(b, start + m.shape[3])
-            if low < high:
-                term = back_of(
-                    got, m, tables[3], own.shape, low - a, low - start, high - low
-                )
-                ready = term if ready is None else ready + term
-    back += ready
     data_grad = scale * (normal - back)
     change = -primal_step * (data_grad + spread)
     guess = own + 2.0 * change

time: 501 us -> 420 us (0.84)
  waiting for transfers between devices: 204 us -> 82 us
  Pallas kernels: 83.6 us -> 129 us
  blocking collectives: 83.2 us -> 49.4 us
  local copies, waits for them, and re-layouts: 66.4 us -> 83.2 us
  starting transfers between devices: 20.4 us -> 26.1 us
  other arithmetic: 26.8 us -> 32.4 us
    all_to_all x4 -> x5, waiting for transfers between devices: 204 us -> 82 us  [swap(): lax.all_to_all(blocks, EVERY, split_axis=0, concat_axis=0, tiled=True)]
    pallas_call x0 -> x2, Pallas kernels: none -> 36.1 us  [the longest x1 18.3 us: shared(): pl.pallas_call(share_kernel, out_shape=jax.ShapeDtypeStruct((slabs,) + ow...]
    all_gather x3 -> x2, blocking collectives: 66 us -> 33.1 us  [by_planes(): masks.append(lax.all_gather(part, 'coil', axis=0))]
    dot_general x0 -> x1, local copies, waits for them, and re-layouts: none -> 13.3 us  [by_planes(): jnp.einsum('ckzyx,kjxw->wcjyz', data, inverse_x, preferred_element_type=f32)]
    slice x6 -> x5, local copies, waits for them, and re-layouts: 12.5 us -> 2.91 us  [the longest x3 2.62 us: finish(): data = [packed(data[:, a:b]) for a, b in steps]]
    pallas_call x7, Pallas kernels: 83.6 us -> 92.7 us  [plane_call(): pl.pallas_call(kernel, out_shape=jax.ShapeDtypeStruct(shape, f32), grid=(...]
    mul x1 -> x0, other arithmetic: 7.88 us -> none  [by_planes(): data = kspace_data * sample_mask[:, None, :, :, None].astype(bf16)]
    reduce_max x0 -> x1, other arithmetic: none -> 5.56 us  [by_planes(): fits = jnp.max(begin + rank[:, :, 1:, ..., -1:]) <= nz]
  transfers between devices with their start and end apart: 6 -> 7, of which waited for: 3 -> 4; matrix products, arithmetic and copies ran while one was open for 17% -> 23% of each run, Pallas kernels for 16% -> 30%
where the time goes in v2:
time: 420 us; the launch traced here: 413 us
  Pallas kernels  129 us (31%)
  local copies, waits for them, and re-layouts  83.2 us (20%)
  waiting for transfers between devices  82 us (20%)
  blocking collectives  49.4 us (12%)
  other arithmetic  32.4 us (8%)
  starting transfers between devices  26.1 us (6%)
  matrix products  8.75 us (2%)
    pallas_call x7, Pallas kernels, plane_call(): pl.pallas_call(kernel, out_shape=jax.ShapeDtypeStruct(shape, f32), grid=(...  92.7 us
    all_to_all x5, waiting for transfers between devices, swap(): lax.all_to_all(blocks, EVERY, split_axis=0, concat_axis=0, tiled=True)  82 us
    all_gather x2, blocking collectives, by_planes(): masks.append(lax.all_gather(part, 'coil', axis=0))  33.1 us
    all_to_all x5, starting transfers between devices, swap(): lax.all_to_all(blocks, EVERY, split_axis=0, concat_axis=0, tiled=True)  22.7 us
    pallas_call x1, Pallas kernels, shared(): pl.pallas_call(share_kernel, out_shape=jax.ShapeDtypeStruct((slabs,) + ow...  18.3 us
    pallas_call x1, Pallas kernels, selected(): pl.pallas_call(select_kernel, out_shape=jax.ShapeDtypeStruct((planes, coi...  17.8 us
    unnamed x54, local copies, waits for them, and re-layouts  17.2 us
    all_to_all x1, blocking collectives, swap(): lax.all_to_all(blocks, EVERY, split_axis=0, concat_axis=0, tiled=True)  16.3 us
  transfers between devices with their start and end apart: 7, of which 4 were waited for; matrix products, arithmetic and copies ran while one was open for 23% of the time, Pallas kernels for 30%

profile of v2, /device:TPU:0, one launch (start us, length us, event | category | flops | bytes accessed | tf_op | source)
XLA Modules:
  0.0 412.5 jit_solution(14588161910210229042)
XLA Ops:
  0.0 1.1 convert_element_type.59
  2.5 1.0 copy.135
  3.5 1.3 pad_maximum_fusion.1
  4.8 7.3 %all-to-all-start.5 = ((bf16[32,176,128]{2,1,0:T(8,128)(2,1)}), bf16[32,176,128]{2,1,0:T(8,128)(2,1)S(1)}, u32[]{:S(2)}, u32[]{:S(2)}) async-start(bf16[32,176,128]{2,1,0:T(8,128)(2,1)} %pad_maximum_fusion.1), calls=%async_computation.5 | async-start | bytes 2883584 | tf_op jit(solution)/shard_map/all_to_all | solution.py:555
  12.1 9.2 %slice.163 = bf16[7,2,16,128,128]{4,3,2,1,0:T(8,128)(2,1)} slice(bf16[8,2,16,128,128]{4,3,2,1,0:T(8,128)(2,1)} %param.16), slice={[1:8], [0:2], [0:16], [0:128], [0:128]} | slice | bytes 14680064 | tf_op jit(solution)/shard_map/slice | solution.py:605
  21.4 12.3 %copy.136 = bf16[7,2,16,128,128]{3,2,1,0,4:T(8,128)(2,1)} copy(bf16[7,2,16,128,128]{4,3,2,1,0:T(8,128)(2,1)} %slice.163) | data formatting | bytes 14680064
  34.3 18.3 %shard_map.129 = bf16[8,8,16,128]{3,2,1,0:T(8,128)(2,1)} custom-call(bf16[8,16,128]{2,1,0:T(8,128)(2,1)} %get-tuple-element.307.own_ref), custom_call_target="tpu_custom_call" | custom-call | flops 1048576 | bytes 524288 | tf_op jit(solution)/shard_map/pallas_call | solution.py:466
  52.6 4.8 %all-to-all-start.6 = ((bf16[32,4,7,2,16,128]{5,4,3,2,1,0:T(8,128)(2,1)}), bf16[32,4,7,2,16,128]{5,4,3,2,1,0:T(8,128)(2,1)}, u32[]{:S(2)}, u32[]{:S(2)}) async-start(bf16[32,4,7,2,16,128]{5,4,3,2,1,0:T(8,128)(2,1)} %bitcast.86), calls=%async_computation.6 | async-start | bytes 14680064 | tf_op jit(solution)/shard_map/all_to_all | solution.py:555
  57.6 6.8 %convolution_bitcast_fusion = bf16[8,128,16,2,128]{4,2,3,1,0:T(8,128)(2,1)} fusion(bf16[2,2,128,128,1,1]{2,3,0,1,5,4:T(8,128)(2,1)S(1)} %copy-done.28, bf16[8,2,128,16,128]{4,3,2,1,0:T(8,128)(2,1)} %param.15, bf16[8,128,16]{2,1,0:T(8,128)(2,1)S(1)} %copy.111), kind=kOutput, calls=%fused_computation.2 | convolution fusion | flops 2151677952 | bytes 16941056 | tf_op jit(solution)/shard_map/ckzyx,kjxw->wcjyz/dot_general | solution.py:632
  64.4 13.3 %copy.113 = bf16[8,128,16,2,128]{1,2,3,0,4:T(8,128)(2,1)} copy(bf16[8,128,16,2,128]{4,2,3,1,0:T(8,128)(2,1)} %convolution_bitcast_fusion) | data formatting | bytes 16777216 | tf_op jit(solution)/shard_map/ckzyx,kjxw->wcjyz/dot_general | solution.py:632
  78.3 2.4 select_reduce_fusion.pick_ref
  80.8 17.8 %shard_map.130 = bf16[128,8,16,128]{3,2,1,0:T(8,128)(2,1)} custom-call(s32[8,8,128]{2,1,0:T(8,128)} %select_reduce_fusion.pick_ref, bf16[128,8,2,16,128]{4,3,2,1,0:T(8,128)(2,1)} %bitcast.80), custom_call_target="tpu_custom_call" | custom-call | flops 268435456 | bytes 12582912 | tf_op jit(solution)/shard_map/pallas_call | solution.py:418
  98.6 1.0 slice_convert_fusion
  99.6 1.8 reshape.153
  101.4 3.7 copy.118
  105.1 1.7 slice.212
  106.8 1.1 slice.167
  108.0 8.6 %all_gather.13 = bf16[4,4,128,128]{3,2,1,0:T(8,128)(2,1)} all-gather(bf16[1,4,128,128]{3,2,1,0:T(8,128)(2,1)S(1)} %bitcast.107), channel_id=1, replica_groups=mesh['coil'=4,'slab'=8] {'coil'}, dimensions={0}, use_global_device_ids=true | all-gather | bytes 655360 | tf_op jit(solution)/shard_map/all_gather | solution.py:656
  116.6 2.0 copy.117
  118.7 24.5 %all-gather = bf16[16,128,128]{2,1,0:T(8,128)(2,1)} all-gather(bf16[4,128,128]{2,1,0:T(8,128)(2,1)S(1)} %bitcast.106), channel_id=2, replica_groups=mesh['coil'=4,'slab'=8] {'coil'}, dimensions={0}, use_global_device_ids=true | all-gather | bytes 655360 | tf_op jit(solution)/shard_map/all_gather | solution.py:656
  143.2 2.0 copy.116
  145.2 2.7 pad_maximum_fusion.2
  147.9 2.3 copy.120
  150.2 3.8 convert_element_type.70
  154.3 1.7 copy.119
  156.0 2.0 sub.60
  159.4 1.4 broadcast_select_fusion
  160.8 0.9 copy-done.3
  162.5 0.8 slice.227
  163.3 1.4 copy.110
  164.7 1.7 slice.166.guess_ref
  166.4 1.8 convolution_convert_fusion
  168.1 5.6 %fusion.3 = (s32[]{:T(128)}, s32[4,8,8,8]{3,2,1,0:T(8,128)S(1)}) fusion(s32[4,8,2,8,8,128]{5,4,3,2,1,0:T(8,128)S(1)} %convolution_convert_fusion), kind=kLoop, calls=%fused_computation.20 | loop fusion | flops 4095 | bytes 24580 | tf_op jit(solution)/shard_map/reduce_max | solution.py:664
  174.4 5.2 %shard_map.131 = f32[4,2,128,128]{3,2,1,0:T(8,128)S(1)} custom-call(f32[4,2,128,128]{3,2,1,0:T(8,128)} %slice.166.guess_ref, bf16[8,4,4,1,2,16,128]{6,5,4,3,2,1,0:T(8,128)(2,1)} %bitcast.90, bf16[4,8,128,128]{3,2,1,0:T(8,128)(2,1)} %get-tuple-element.142.mask_ref, bf16[256,256]{1,0:T(8,128)(2,1)} %constant.79.clone.fy_ref.gz_ref, ...), custom_call_target="tpu_custom_call" | custom-call | flops 1073741824 | bytes 1048576 | tf_op jit(solution)/shard_map/pallas_call | solution.py:483
  179.6 2.7 fusion.26
  183.6 1.7 fusion.1
  185.3 35.1 %all-to-all-done.6 = bf16[32,4,7,2,16,128]{5,4,3,2,1,0:T(8,128)(2,1)} async-done(((bf16[32,4,7,2,16,128]{5,4,3,2,1,0:T(8,128)(2,1)}), bf16[32,4,7,2,16,128]{5,4,3,2,1,0:T(8,128)(2,1)}, u32[]{:S(2)}, u32[]{:S(2)}) %all-to-all-start.6) | async-done | bytes 7340064 | tf_op jit(solution)/shard_map/all_to_all | solution.py:555
  220.4 128.2 %conditional.1 = (f32[4,2,128,128]{3,2,1,0:T(8,128)}, f32[4,2,128,128]{3,2,1,0:T(8,128)}, f32[4,2,128,128]{3,2,1,0:T(8,128)}) conditional(s32[]{:T(128)} %convert_element_type.72, (bf16[128,8,2,16,128]{4,3,2,1,0:T(8,128)(2,1)}, f32[4,2,128,128]{3,2,1,0:T(8,128)S(1)}, bf16[8,4,4,7,2,16,128]{6,5,4,3,2,1,0:T(8,128)(2,1)}, ...), branch_computations={%region_5.6_spmd, %region_6.7_spmd} | conditional | flops 11811292160 | bytes 97517656 | solution.py:707
  220.4 3.7 copy.123
  224.5 1.4 slice.208
  226.8 2.0 copy.103
  228.8 2.7 all-to-all-start.2
  231.5 28.1 %branch_1_fun.4 = f32[4,2,128,128]{3,2,1,0:T(8,128)} custom-call(f32[4,2,128,128]{3,2,1,0:T(8,128)S(1)} %get-tuple-element.87.guess_ref, bf16[8,4,4,7,2,16,128]{6,5,4,3,2,1,0:T(8,128)(2,1)} %get-tuple-element.88.maps_ref, bf16[4,8,128,128]{3,2,1,0:T(8,128)(2,1)} %copy-done.21, bf16[256,256]{1,0:T(8,128)(2,1)S(1)} %get-tuple-element.92.gz_ref, ...), custom_call_target="tpu_custom_call" | custom-call | flops 7516192768 | bytes 7340032 | tf_op jit(solution)/shard_map/cond/branch_1_fun/pallas_call | solution.py:483
  259.6 20.8 %all-to-all-done.2 = bf16[32,4,4,16,128]{4,3,2,1,0:T(8,128)(2,1)S(1)} async-done(((bf16[32,4,4,16,128]{4,3,2,1,0:T(8,128)(2,1)}), bf16[32,4,4,16,128]{4,3,2,1,0:T(8,128)(2,1)S(1)}, u32[]{:S(2)}, u32[]{:S(2)}) %all-to-all-start.2) | async-done | bytes 2097184 | tf_op jit(solution)/shard_map/cond/branch_1_fun/all_to_all | solution.py:555
  280.3 2.9 copy.104
  283.3 4.1 all-to-all-start.3
  287.5 0.9 gather_fusion
  288.4 14.1 %branch_1_fun.5 = f32[4,2,128,128]{3,2,1,0:T(8,128)S(1)} custom-call(bf16[8,4,4,4,16,128]{5,4,3,2,1,0:T(8,128)(2,1)S(1)} %bitcast.74, s32[4,8,128,128]{3,2,1,0:T(8,128)} %get-tuple-element.99.code_ref, bf16[8,4,4,7,2,16,128]{6,5,4,3,2,1,0:T(8,128)(2,1)} %get-tuple-element.88.maps_ref, bf16[256,256]{1,0:T(8,128)(2,1)S(1)} %get-tuple-element.100.gz_ref, ...), custom_call_target="tpu_custom_call" | custom-call | flops 2147483648 | bytes 8388608 | tf_op jit(solution)/shard_map/cond/branch_1_fun/pallas_call | solution.py:483
  302.5 22.5 %all-to-all-done.3 = bf16[32,4,3,16,128]{4,3,2,1,0:T(8,128)(2,1)} async-done(((bf16[32,4,3,16,128]{4,3,2,1,0:T(8,128)(2,1)}), bf16[32,4,3,16,128]{4,3,2,1,0:T(8,128)(2,1)}, u32[]{:S(2)}, u32[]{:S(2)}) %all-to-all-start.3) | async-done | bytes 1572896 | tf_op jit(solution)/shard_map/cond/branch_1_fun/all_to_all | solution.py:555
  325.0 3.8 all-to-all-start.4
  328.8 11.0 %branch_1_fun.6 = f32[4,2,128,128]{3,2,1,0:T(8,128)S(1)} custom-call(bf16[8,4,4,3,16,128]{5,4,3,2,1,0:T(8,128)(2,1)} %bitcast.8.data_ref, s32[4,8,128,128]{3,2,1,0:T(8,128)} %get-tuple-element.99.code_ref, bf16[8,4,4,7,2,16,128]{6,5,4,3,2,1,0:T(8,128)(2,1)} %get-tuple-element.88.maps_ref, bf16[256,256]{1,0:T(8,128)(2,1)S(1)} %get-tuple-element.100.gz_ref, ...), custom_call_target="tpu_custom_call" | custom-call | flops 1610612736 | bytes 6291456 | tf_op jit(solution)/shard_map/cond/branch_1_fun/pallas_call | solution.py:483
  339.9 0.9 add.123
  340.7 3.7 all-to-all-done.4
  344.4 4.1 branch_1_fun.7
  348.6 2.0 multiply_add_fusion.2
  350.6 1.9 collective-permute-start
  352.6 26.7 %shard_map.133 = f32[4,2,128,128]{3,2,1,0:T(8,128)S(1)} custom-call(f32[4,2,128,128]{3,2,1,0:T(8,128)S(1)} %get-tuple-element.285.guess_ref, bf16[8,4,4,7,2,16,128]{6,5,4,3,2,1,0:T(8,128)(2,1)} %bitcast.22.maps_ref, bf16[4,8,128,128]{3,2,1,0:T(8,128)(2,1)S(1)} %copy-done.20, bf16[256,256]{1,0:T(8,128)(2,1)S(1)} %copy-done.27, ...), custom_call_target="tpu_custom_call" | custom-call | flops 7516192768 | bytes 7340032 | tf_op jit(solution)/shard_map/pallas_call | solution.py:483
  379.3 1.4 collective-permute-start.1
  380.7 3.6 shard_map.132
  387.2 1.8 fusion.24
  390.8 2.2 reduce.6
  393.1 16.3 %all_to_all.40 = bf16[32,2,2048]{2,1,0:T(2,128)(2,1)S(1)} all-to-all(bf16[32,2,2048]{2,1,0:T(2,128)(2,1)S(1)} %reshape.172), channel_id=1, replica_groups=mesh['coil'=4,'slab'=8] {'slab','coil'}, dimensions={0} | all-to-all | bytes 524288 | tf_op jit(solution)/shard_map/all_to_all | solution.py:555
  409.7 1.5 convert_reduce_fusion
  411.3 1.0 copy.126
  (109 shorter events, 13.2 us)
Async XLA Ops:
  1.1 1.4 slice-start
  4.8 47.8 %all-to-all-start.5 = ((bf16[32,176,128]{2,1,0:T(8,128)(2,1)}), bf16[32,176,128]{2,1,0:T(8,128)(2,1)S(1)}, u32[]{:S(2)}, u32[]{:S(2)}) async-start(bf16[32,176,128]{2,1,0:T(8,128)(2,1)} %pad_maximum_fusion.1), calls=%async_computation.5 | async-start | bytes 2883584 | tf_op jit(solution)/shard_map/all_to_all | solution.py:555
  21.4 12.3 %copy-start.23 = (s32[8,128,16]{1,2,0:T(8,128)S(1)}, s32[8,128,16]{1,2,0:T(8,128)}, u32[]{:S(2)}) copy-start(s32[8,128,16]{1,2,0:T(8,128)} %param.17) | copy-start | bytes 196612
  52.6 46.0 %copy-start.14 = (bf16[32,176,128]{2,1,0:T(8,128)(2,1)}, bf16[32,176,128]{2,1,0:T(8,128)(2,1)S(1)}, u32[]{:S(2)}) copy-start(bf16[32,176,128]{2,1,0:T(8,128)(2,1)S(1)} %all-to-all-done.5) | copy-start | bytes 4325380
  52.6 5.0 %copy-start.28 = (bf16[2,2,128,128,1,1]{2,3,0,1,5,4:T(8,128)(2,1)S(1)}, bf16[2,2,128,128,1,1]{2,3,0,1,5,4:T(8,128)(2,1)}, u32[]{:S(2)}) copy-start(bf16[2,2,128,128,1,1]{2,3,0,1,5,4:T(8,128)(2,1)} %constant.105) | copy-start | bytes 393220
  52.6 167.7 %all-to-all-start.6 = ((bf16[32,4,7,2,16,128]{5,4,3,2,1,0:T(8,128)(2,1)}), bf16[32,4,7,2,16,128]{5,4,3,2,1,0:T(8,128)(2,1)}, u32[]{:S(2)}, u32[]{:S(2)}) async-start(bf16[32,4,7,2,16,128]{5,4,3,2,1,0:T(8,128)(2,1)} %bitcast.86), calls=%async_computation.6 | async-start | bytes 14680064 | tf_op jit(solution)/shard_map/all_to_all | solution.py:555
  64.4 13.3 %copy-start.24 = (bf16[8,16,128]{2,1,0:T(8,128)(2,1)S(1)}, bf16[8,16,128]{2,1,0:T(8,128)(2,1)}, u32[]{:S(2)}) copy-start(bf16[8,16,128]{2,1,0:T(8,128)(2,1)} %get-tuple-element.307.own_ref) | copy-start | bytes 98308
  105.1 1.7 copy-start.15
  105.1 2.8 copy-start.22
  156.0 2.0 copy-start
  158.0 1.1 copy-start.12
  159.4 3.9 copy-start.11
  160.8 0.9 copy-start.3
  160.8 18.8 %copy-start.1 = (f32[5,2,128,128]{3,2,1,0:T(8,128)}, f32[5,2,128,128]{3,2,1,0:T(8,128)S(1)}, u32[]{:S(2)}) copy-start(f32[5,2,128,128]{3,2,1,0:T(8,128)S(1)} %get-tuple-element.151) | copy-start | bytes 1966084
  166.4 8.0 %copy-start.10 = (bf16[256,256]{1,0:T(8,128)(2,1)S(1)}, bf16[256,256]{1,0:T(8,128)(2,1)}, u32[]{:S(2)}) copy-start(bf16[256,256]{1,0:T(8,128)(2,1)} %constant.80.clone.fz_ref.gy_ref) | copy-start | bytes 393220
  182.4 1.2 copy-start.5
  182.8 37.5 %copy-start.6 = (bf16[32,128,128]{2,1,0:T(8,128)(2,1)S(1)}, bf16[32,128,128]{2,1,0:T(8,128)(2,1)}, u32[]{:S(2)}) copy-start(bf16[32,128,128]{2,1,0:T(8,128)(2,1)} %slice.167) | copy-start | bytes 3145732
  182.9 37.5 %copy-start.16 = (f32[4,2,128,128]{3,2,1,0:T(8,128)S(1)}, f32[4,2,128,128]{3,2,1,0:T(8,128)}, u32[]{:S(2)}) copy-start(f32[4,2,128,128]{3,2,1,0:T(8,128)} %slice.166.guess_ref) | copy-start | bytes 1572868
  182.9 37.5 %copy-start.19 = (bf16[4,8,128,128]{3,2,1,0:T(8,128)(2,1)S(1)}, bf16[4,8,128,128]{3,2,1,0:T(8,128)(2,1)}, u32[]{:S(2)}) copy-start(bf16[4,8,128,128]{3,2,1,0:T(8,128)(2,1)} %get-tuple-element.142.mask_ref) | copy-start | bytes 3145732
  182.9 37.5 %copy-start.26 = (bf16[256,256]{1,0:T(8,128)(2,1)S(1)}, bf16[256,256]{1,0:T(8,128)(2,1)}, u32[]{:S(2)}) copy-start(bf16[256,256]{1,0:T(8,128)(2,1)} %constant.79.clone.fy_ref.gz_ref) | copy-start | bytes 393220
  220.4 3.7 copy-start.8
  220.4 3.7 copy-start.21
  228.8 51.5 %all-to-all-start.2 = ((bf16[32,4,4,16,128]{4,3,2,1,0:T(8,128)(2,1)}), bf16[32,4,4,16,128]{4,3,2,1,0:T(8,128)(2,1)S(1)}, u32[]{:S(2)}, u32[]{:S(2)}) async-start(bf16[32,4,4,16,128]{4,3,2,1,0:T(8,128)(2,1)} %copy.103), calls=%async_computation.2 | async-start | bytes 4194304 | tf_op jit(solution)/shard_map/cond/branch_1_fun/all_to_all | solution.py:555
  280.3 7.2 %copy-start.25 = (s32[128]{0:T(128)S(1)}, s32[128]{0:T(128)}, u32[]{:S(2)}) copy-start(s32[128]{0:T(128)} %constant.104) | copy-start | bytes 1540 | tf_op jit(solution)/shard_map/cond
  283.3 41.7 %all-to-all-start.3 = ((bf16[32,4,3,16,128]{4,3,2,1,0:T(8,128)(2,1)}), bf16[32,4,3,16,128]{4,3,2,1,0:T(8,128)(2,1)}, u32[]{:S(2)}, u32[]{:S(2)}) async-start(bf16[32,4,3,16,128]{4,3,2,1,0:T(8,128)(2,1)} %copy.104), calls=%async_computation.3 | async-start | bytes 3145728 | tf_op jit(solution)/shard_map/cond/branch_1_fun/all_to_all | solution.py:555
  325.0 19.4 %all-to-all-start.4 = ((bf16[32,4,1,16,128]{4,3,1,2,0:T(8,128)(2,1)}), bf16[32,4,1,16,128]{4,3,1,2,0:T(8,128)(2,1)S(1)}, u32[]{:S(2)}, u32[]{:S(2)}) async-start(bf16[32,4,1,16,128]{4,3,1,2,0:T(8,128)(2,1)} %bitcast.100), calls=%async_computation.4 | async-start | bytes 1048576 | tf_op jit(solution)/shard_map/cond/branch_1_fun/all_to_all | solution.py:555
  328.8 15.6 %copy-start.9 = (bf16[8,4,4,1,2,16,128]{6,5,4,3,2,1,0:T(8,128)(2,1)S(1)}, bf16[8,4,4,1,2,16,128]{6,5,4,3,2,1,0:T(8,128)(2,1)}, u32[]{:S(2)}) copy-start(bf16[8,4,4,1,2,16,128]{6,5,4,3,2,1,0:T(8,128)(2,1)} %copy-done.8) | copy-start | bytes 3145732 | tf_op jit(solution)/shard_map/cond
  348.6 4.0 copy-start.20
  348.6 4.0 copy-start.27
  350.6 30.1 %copy-start.7 = (bf16[32,128,128]{2,1,0:T(8,128)(2,1)S(1)}, bf16[32,128,128]{2,1,0:T(8,128)(2,1)}, u32[]{:S(2)}) copy-start(bf16[32,128,128]{2,1,0:T(8,128)(2,1)} %slice.167) | copy-start | bytes 3145732
  350.6 33.7 %collective-permute-start = (f32[1,2,128,128]{3,2,1,0:T(8,128)S(1)}, f32[1,2,128,128]{3,2,1,0:T(8,128)S(1)}, u32[]{:S(2)}, u32[]{:S(2)}) collective-permute-start(f32[1,2,128,128]{3,2,1,0:T(8,128)S(1)} %get-tuple-element.294), channel_id=1, source_target_pairs={{0,8},{8,16},{16,24},{24,1},{1,9},{9,17},{17,25},{25,2},{2,10},{10... | collective-permute-start | bytes 393224 | tf_op jit(solution)/shard_map/ppermute | solution.py:715
  379.3 5.3 %copy-start.2 = (f32[5,2,128,128]{3,2,1,0:T(8,128)S(1)}, f32[5,2,128,128]{3,2,1,0:T(8,128)}, u32[]{:S(2)}) copy-start(f32[5,2,128,128]{3,2,1,0:T(8,128)} %copy-done.1) | copy-start | bytes 1966084
  379.3 6.2 %collective-permute-start.1 = (f32[1,2,128,128]{3,2,1,0:T(8,128)S(1)}, f32[1,2,128,128]{3,2,1,0:T(8,128)S(1)}, u32[]{:S(2)}, u32[]{:S(2)}) collective-permute-start(f32[1,2,128,128]{3,2,1,0:T(8,128)S(1)} %get-tuple-element.293), channel_id=1, source_target_pairs={{8,0},{16,8},{24,16},{1,24},{9,1},{17,9},{25,17},{2,25},{10,2},{18... | collective-permute-start | bytes 393224 | tf_op jit(solution)/shard_map/ppermute | solution.py:716
  384.3 1.1 copy-start.4
  384.3 1.3 copy-start.13
  386.0 1.0 copy-start.17
  386.0 1.2 copy-start.18

commit v3 on v2

--- a/solution.py
+++ b/solution.py
@@ -263,13 +263,13 @@
     return share.transpose(1, 2, 3, 0, 4).reshape(2, planes, rows, nx)
 
 
-def all_planes(ref, coil, part):
-    block = ref[:, coil, 0, 0, part]
+def all_planes(ref, coil, turn, part):
+    block = ref[:, coil, 0, turn, part]
     return block.reshape(block.shape[0] * block.shape[1], block.shape[2])
 
 
-def combine_planes(out_ref, maps, images):
-    nz, ny = out_ref.shape[2:]
+def terms(maps, images):
+    nz, ny = maps[0][0].shape
     real_sum = imag_sum = None
     for coil, (maps_real, maps_imag) in enumerate(maps):
         real = images[coil * nz : (coil + 1) * nz, :ny]
@@ -278,6 +278,12 @@
         imag_term = maps_real * imag - maps_imag * real
         real_sum = real_term if coil == 0 else real_sum + real_term
         imag_sum = imag_term if coil == 0 else imag_sum + imag_term
+    return real_sum, imag_sum
+
+
+def add_up(out_ref, sums):
+    real_sum = functools.reduce(lambda a, b: a + b, [real for real, _ in sums])
+    imag_sum = functools.reduce(lambda a, b: a + b, [imag for _, imag in sums])
 
     @pl.when(pl.program_id(1) == 0)
     def _():
@@ -290,9 +296,9 @@
         out_ref[0, 1] += imag_sum
 
 
-def planes_of(maps_ref):
+def planes_of(maps_ref, turn):
     return [
-        (all_planes(maps_ref, c, 0).astype(f32), all_planes(maps_ref, c, 1).astype(f32))
+        (all_planes(maps_ref, c, turn, 0).astype(f32), all_planes(maps_ref, c, turn, 1).astype(f32))
         for c in range(maps_ref.shape[1])
     ]
 
@@ -302,40 +308,43 @@
     group = maps_ref.shape[1]
     guess_real = guess_ref[0, 0]
     guess_imag = guess_ref[0, 1]
-    maps = planes_of(maps_ref)
-    rows = []
-    for maps_real, maps_imag in maps:
-        real = maps_real * guess_real - maps_imag * guess_imag
-        imag = maps_real * guess_imag + maps_imag * guess_real
-        rows.append(jnp.concatenate([real.astype(bf16), imag.astype(bf16)], 1))
-    pieces = dot(jnp.concatenate(rows, 0), fy_ref[...]).astype(bf16)
-    pieces = jnp.concatenate(
-        [
-            jnp.concatenate(
-                [pieces[c * nz : (c + 1) * nz, j * ny : (j + 1) * ny] for c in range(group)], 1
-            )
-            for j in range(2)
-        ],
-        0,
-    )
-    spectrum = dot(fz_ref[...], pieces).astype(bf16)
-    mask = jnp.concatenate([mask_ref[c, 0] for c in range(group)], 1)
-    spectrum = spectrum * jnp.concatenate([mask, mask], 0)
-    pieces = dot(gz_ref[...], spectrum).astype(bf16)
-    pieces = jnp.concatenate(
-        [
-            jnp.concatenate(
-                [pieces[j * nz : (j + 1) * nz, c * ny : (c + 1) * ny] for j in range(2)], 1
-            )
-            for c in range(group)
-        ],
-        0,
-    )
-    combine_planes(out_ref, maps, dot(pieces, gy_ref[...]))
-
-
-def back_planes(out_ref, maps_ref, gz_ref, gy_ref, spectra):
-    nz, ny = out_ref.shape[2:]
+    sums = []
+    for turn in range(maps_ref.shape[3]):
+        maps = planes_of(maps_ref, turn)
+        rows = []
+        for maps_real, maps_imag in maps:
+            real = maps_real * guess_real - maps_imag * guess_imag
+            imag = maps_real * guess_imag + maps_imag * guess_real
+            rows.append(jnp.concatenate([real.astype(bf16), imag.astype(bf16)], 1))
+        pieces = dot(jnp.concatenate(rows, 0), fy_ref[...]).astype(bf16)
+        pieces = jnp.concatenate(
+            [
+                jnp.concatenate(
+                    [pieces[c * nz : (c + 1) * nz, j * ny : (j + 1) * ny] for c in range(group)], 1
+                )
+                for j in range(2)
+            ],
+            0,
+        )
+        spectrum = dot(fz_ref[...], pieces).astype(bf16)
+        mask = jnp.concatenate([mask_ref[c, turn] for c in range(group)], 1)
+        spectrum = spectrum * jnp.concatenate([mask, mask], 0)
+        pieces = dot(gz_ref[...], spectrum).astype(bf16)
+        pieces = jnp.concatenate(
+            [
+                jnp.concatenate(
+                    [pieces[j * nz : (j + 1) * nz, c * ny : (c + 1) * ny] for j in range(2)], 1
+                )
+                for c in range(group)
+            ],
+            0,
+        )
+        sums.append(terms(maps, dot(pieces, gy_ref[...])))
+    add_up(out_ref, sums)
+
+
+def back_terms(maps_ref, turn, gz_ref, gy_ref, spectra):
+    nz = gz_ref.shape[1] // 2
     shares = spectra[0][0].shape[0]
     spectrum = jnp.concatenate([jnp.concatenate(parts, 1) for parts in spectra], 0)
     pieces = dot(spectrum, gz_ref[...]).astype(bf16)
@@ -352,14 +361,18 @@
         ],
         0,
     )
-    combine_planes(out_ref, planes_of(maps_ref), dot(columns, gy_ref[...], ((0,), (0,))))
+    return terms(planes_of(maps_ref, turn), dot(columns, gy_ref[...], ((0,), (0,))))
 
 
 def dense_kernel(data_ref, maps_ref, gz_ref, gy_ref, out_ref):
-    spectra = [
-        (all_planes(data_ref, c, 0), all_planes(data_ref, c, 1)) for c in range(data_ref.shape[1])
-    ]
-    back_planes(out_ref, maps_ref, gz_ref, gy_ref, spectra)
+    sums = []
+    for turn in range(maps_ref.shape[3]):
+        spectra = [
+            (all_planes(data_ref, c, turn, 0), all_planes(data_ref, c, turn, 1))
+            for c in range(data_ref.shape[1])
+        ]
+        sums.append(back_terms(maps_ref, turn, gz_ref, gy_ref, spectra))
+    add_up(out_ref, sums)
 
 
 def lanes_at(array, place):
@@ -368,67 +381,136 @@
 
 def sparse_kernel(data_ref, code_ref, maps_ref, gz_ref, gy_ref, out_ref):
     half = data_ref.shape[4] // 2
-    spectra = []
-    for coil in range(data_ref.shape[1]):
-        lines = data_ref[:, coil, 0, 0].astype(f32)
-        lines = [
-            lines[:, j * half : (j + 1) * half].reshape(-1, lines.shape[2]) for j in range(2)
-        ]
-        count = lines[0].shape[0]
-        codes = [code_ref[coil, 0, h * count : (h + 1) * count] for h in range(2)]
-        spectra.append(
-            [
-                jnp.concatenate(
-                    [
-                        jnp.where(code >= 0, lanes_at(line, jnp.maximum(code, 0)), 0.0)
-                        for code in codes
-                    ],
-                    0,
-                ).astype(bf16)
-                for line in lines
+    sums = []
+    for turn in range(maps_ref.shape[3]):
+        spectra = []
+        for coil in range(data_ref.shape[1]):
+            lines = data_ref[:, coil, 0, turn].astype(f32)
+            lines = [
+                lines[:, j * half : (j + 1) * half].reshape(-1, lines.shape[2]) for j in range(2)
             ]
-        )
-    back_planes(out_ref, maps_ref, gz_ref, gy_ref, spectra)
-
-
-def select_kernel(pick_ref, data_ref, out_ref):
+            count = lines[0].shape[0]
+            codes = [code_ref[coil, turn, h * count : (h + 1) * count] for h in range(2)]
+            spectra.append(
+                [
+                    jnp.concatenate(
+                        [
+                            jnp.where(code >= 0, lanes_at(line, jnp.maximum(code, 0)), 0.0)
+                            for code in codes
+                        ],
+                        0,
+                    ).astype(bf16)
+                    for line in lines
+                ]
+            )
+        sums.append(back_terms(maps_ref, turn, gz_ref, gy_ref, spectra))
+    add_up(out_ref, sums)
+
+
+def select_kernel(edges, pick_ref, data_ref, *out_refs):
     half = data_ref.shape[3] // 2
     lanes = data_ref.shape[4]
 
     def one(plane_index, _):
-        for coil in range(data_ref.shape[1]):
-            pick = pick_ref[coil]
-            later = pick >= lanes
-            place = jnp.where(later, pick - lanes, pick)
-            parts = []
-            for part in range(2):
-                lines = data_ref[plane_index, coil, part].astype(f32)
-                parts.append(
-                    jnp.where(later, lanes_at(lines[half:], place), lanes_at(lines[:half], place))
-                )
-            out_ref[plane_index, coil] = jnp.concatenate(parts, 0).astype(bf16)
+        for out_ref, (first, last) in zip(out_refs, edges):
+            for coil in range(first, last):
+                pick = pick_ref[coil]
+                later = pick >= lanes
+                place = jnp.where(later, pick - lanes, pick)
+                parts = []
+                for part in range(2):
+                    lines = data_ref[plane_index, coil, part].astype(f32)
+                    parts.append(
+                        jnp.where(
+                            later, lanes_at(lines[half:], place), lanes_at(lines[:half], place)
+                        )
+                    )
+                out_ref[plane_index, coil - first] = jnp.concatenate(parts, 0).astype(bf16)
         return 0
 
     lax.fori_loop(0, data_ref.shape[0], one, 0)
 
 
-def selected(data, pick):
-    planes, coils, _, shares, lanes = data.shape
+def selected(data, pick, edges):
+    planes, _, _, shares, lanes = data.shape
     step = max(n for n in (1, 2, 4, 8) if planes % n == 0)
     return pl.pallas_call(
-        select_kernel,
-        out_shape=jax.ShapeDtypeStruct((planes, coils, shares, lanes), bf16),
+        functools.partial(select_kernel, edges),
+        out_shape=[
+            jax.ShapeDtypeStruct((planes, b - a, shares, lanes), bf16) for a, b in edges
+        ],
         grid=(planes // step,),
         in_specs=[
             pl.BlockSpec(pick.shape, lambda x: (0, 0, 0)),
             pl.BlockSpec((step,) + data.shape[1:], lambda x: (x, 0, 0, 0, 0)),
         ],
-        out_specs=pl.BlockSpec((step, coils, shares, lanes), lambda x: (x, 0, 0, 0)),
+        out_specs=[
+            pl.BlockSpec((step, b - a, shares, lanes), lambda x: (x, 0, 0, 0)) for a, b in edges
+        ],
         compiler_params=pltpu.CompilerParams(dimension_semantics=("arbitrary",)),
         cost_estimate=pl.CostEstimate(
             flops=data.size * 64, bytes_accessed=data.size * 3, transcendentals=0
         ),
     )(pick, data)
+
+
+def deliver_kernel(block_ref, got_ref, send_sem, recv_sem):
+    groups = lax.axis_size("coil")
+    count = groups * lax.axis_size("slab")
+    me = lax.axis_index("slab") * groups + lax.axis_index("coil")
+    barrier = pltpu.get_barrier_semaphore()
+
+    def place(step):
+        other = lax.rem(me + step, count)
+        return other, (lax.rem(other, groups), other // groups)
+
+    def greet(step, _):
+        pl.semaphore_signal(
+            barrier, inc=1, device_id=place(step)[1], device_id_type=pl.DeviceIdType.MESH
+        )
+        return 0
+
+    def copy(step):
+        other, device = place(step)
+        return pltpu.make_async_remote_copy(
+            block_ref.at[other],
+            got_ref.at[me],
+            send_sem.at[step - 1],
+            recv_sem.at[step - 1],
+            device_id=device,
+            device_id_type=pl.DeviceIdType.MESH,
+        )
+
+    def begin(step, _):
+        copy(step).start()
+        return 0
+
+    def end(step, _):
+        copy(step).wait()
+        return 0
+
+    lax.fori_loop(1, count, greet, 0)
+    pl.semaphore_wait(barrier, count - 1)
+    lax.fori_loop(1, count, begin, 0)
+    got_ref[me] = block_ref[me]
+    lax.fori_loop(1, count, end, 0)
+
+
+def delivered(blocks):
+    return pl.pallas_call(
+        deliver_kernel,
+        out_shape=jax.ShapeDtypeStruct(blocks.shape, blocks.dtype),
+        in_specs=[pl.BlockSpec(memory_space=pltpu.VMEM)],
+        out_specs=pl.BlockSpec(memory_space=pltpu.VMEM),
+        scratch_shapes=[
+            pltpu.SemaphoreType.DMA((blocks.shape[0] - 1,)),
+            pltpu.SemaphoreType.DMA((blocks.shape[0] - 1,)),
+        ],
+        compiler_params=pltpu.CompilerParams(collective_id=1, has_side_effects=True),
+        cost_estimate=pl.CostEstimate(
+            flops=blocks.size * 64, bytes_accessed=blocks.size * 4, transcendentals=0
+        ),
+    )(blocks)
 
 
 def share_kernel(own_ref, all_ref, send_sem, recv_sem):
@@ -493,51 +575,48 @@
     )(*operands)
 
 
-def every_source(array, start=0):
-    slabs, groups, _, _, parts, rows, cols = array.shape
+def every_source(array, turns, start=0):
+    slabs, groups, _, _, *rest = array.shape
     return pl.BlockSpec(
-        (slabs, groups, 1, 1, parts, rows, cols), lambda x, c: (0, 0, x, start + c, 0, 0, 0)
-    )
-
-
-def normal_of(guess, maps, mask, first, tables):
+        (slabs, groups, 1, turns, *rest),
+        lambda x, c: (0, 0, x, start + c) + (0,) * len(rest),
+    )
+
+
+def per_coil(array, turns, start=0):
+    return pl.BlockSpec(
+        (array.shape[0], turns) + array.shape[2:], lambda x, c: (0, start + c, 0, 0)
+    )
+
+
+def normal_of(guess, maps, mask, tables):
     shape = guess.shape
-    coils = maps.shape[3]
-    groups = maps.shape[1]
+    groups, coils = maps.shape[1], maps.shape[3]
+    turns = math.gcd(coils, 4)
     specs = [
         pl.BlockSpec((1,) + shape[1:], lambda x, c: (x, 0, 0, 0)),
-        every_source(maps),
-        pl.BlockSpec((groups, 1) + mask.shape[2:], lambda x, c: (0, first + c, 0, 0)),
+        every_source(maps, turns),
+        per_coil(mask, turns),
     ] + [whole(t.shape) for t in tables]
     cells = groups * coils * shape[0] * shape[2] * shape[3]
-    return plane_call(
-        normal_planes, (guess, maps, mask) + tables, specs, shape, coils, cells * 4096, cells * 4
-    )
+    operands = (guess, maps, mask) + tables
+    steps = coils // turns
+    return plane_call(normal_planes, operands, specs, shape, steps, cells * 4096, cells * 4)
 
 
 def back_of(data, code, maps, tables, shape, start):
-    coils = data.shape[3]
-    groups = maps.shape[1]
-    operands, specs = [data], []
-    if code is None:
-        specs.append(every_source(data))
-    else:
-        slabs, _, _, _, shares, lanes = data.shape
-        specs.append(
-            pl.BlockSpec(
-                (slabs, groups, 1, 1, shares, lanes), lambda x, c: (0, 0, x, c, 0, 0)
-            )
-        )
-        operands.append(code[0])
-        first = code[1]
-        specs.append(
-            pl.BlockSpec((groups, 1) + code[0].shape[2:], lambda x, c: (0, first + c, 0, 0))
-        )
+    groups, coils = maps.shape[1], data.shape[3]
+    turns = math.gcd(math.gcd(coils, start), 2)
+    steps, start = coils // turns, start // turns
+    operands, specs = [data], [every_source(data, turns)]
+    if code is not None:
+        operands.append(code)
+        specs.append(per_coil(code, turns, start))
     operands += (maps,) + tables
-    specs += [every_source(maps, start)] + [whole(t.shape) for t in tables]
+    specs += [every_source(maps, turns, start)] + [whole(t.shape) for t in tables]
     cells = groups * coils * shape[0] * shape[2] * shape[3]
     kernel = dense_kernel if code is None else sparse_kernel
-    return plane_call(kernel, operands, specs, shape, coils, cells * 2048, cells * 8)
+    return plane_call(kernel, operands, specs, shape, steps, cells * 2048, cells * 8)
 
 
 EVERY = ("slab", "coil")
@@ -546,9 +625,15 @@
 
 
 def ranks(flags):
-    before = jnp.triu(jnp.ones((flags.shape[-1],) * 2, bf16))
-    counts = jnp.einsum("...k,kl->...l", flags.astype(bf16), before, preferred_element_type=f32)
-    return counts.astype(jnp.int32)
+    size = flags.shape[-1]
+    flags = flags.astype(bf16)
+
+    def count(table):
+        sums = jnp.einsum("...k,kl->...l", flags, table, preferred_element_type=f32)
+        return sums.astype(jnp.int32)
+
+    every = jnp.ones((size, size), bf16)
+    return count(jnp.triu(every)), count(every)
 
 
 def swap(blocks):
@@ -588,7 +673,6 @@
     forward_z, inverse_z = dft_table(nz, False), dft_table(nz, True)
     inverse_x = jnp.asarray(dft_table(nx, True))
     tables = (on_right(forward_y), on_left(forward_z), on_left(inverse_z), on_right(inverse_y))
-    few = max(1, coils // 8)
     hold = lax.optimization_barrier
 
     def packed(array):
@@ -601,8 +685,6 @@
         order = Layout(major_to_minor=tuple(range(array.ndim)))
         return with_layout_constraint(array, order)
 
-    first_maps = packed(coil_maps[:few].transpose(4, 0, 1, 2, 3))
-    later_maps = packed(coil_maps[few:].transpose(4, 0, 1, 2, 3))
     image = initial_image.reshape(-1, nx).astype(bf16).T.reshape(devices, width, -1)
     edge = jnp.zeros_like(image[:1, :1])
     image = jnp.concatenate(
@@ -613,19 +695,17 @@
         ],
         1,
     )
-    joined = jnp.concatenate(
-        [first_maps.reshape(devices, -1, ny), image.reshape(devices, -1, ny)], 1
-    )
-    joined = swap(joined)
+    image = image.reshape(devices, -1, ny)
+    image, coil_maps = hold((image, coil_maps))
+    image = swap(image)
     mask = shared(sample_mask.swapaxes(1, 2).astype(bf16), slabs)
-    joined, mask, later_maps = hold((joined, mask, later_maps))
-    later_maps = sent(later_maps)
-
-    image = joined[:, -image.shape[1] * image.shape[2] // ny :]
-    first_maps = joined[:, : joined.shape[1] - image.shape[1]]
-    first_maps = first_maps.reshape(slabs, groups, width, few, 2, depth, ny)
+    maps = packed(coil_maps.transpose(4, 0, 1, 2, 3))
+    image, mask, maps = hold((image, mask, maps))
+    maps = sent(maps)
+
     image = image.reshape(slabs, groups, width + 2, 2, depth, rows)
-    image = image.transpose(2, 3, 0, 4, 1, 5).reshape(width + 2, 2, nz, ny).astype(f32)
+    image = image.transpose(2, 3, 0, 4, 1, 5).reshape(width + 2, 2, nz, ny)
+    image = hold(image).astype(f32)
     own = image[1:-1]
 
     data = kspace_data * sample_mask[:, None, :, :, None].astype(bf16)
@@ -633,18 +713,21 @@
     data = in_place(data.astype(bf16))
     half = shares // 2
     small = half == SUBLANES and nz == LANES
+    last = max(1, coils // 4)
+    edges = [(0, coils - last), (coils - last, coils)]
     if small:
         sampled = sample_mask.swapaxes(1, 2)
-        rank = ranks(sampled)
-        begin = rank[:, :half, -1:]
+        rank, total = ranks(sampled)
+        begin = total[:, :half]
         kz = lax.broadcasted_iota(jnp.int32, (1, 1, nz), 2)
         slot = jnp.where(sampled > 0, rank, 0)
-        slot = jnp.concatenate([slot[:, :half], jnp.where(sampled[:, half:] > 0, begin + slot[:, half:], 0)], 2)
+        second = jnp.where(sampled[:, half:] > 0, begin + slot[:, half:], 0)
+        slot = jnp.concatenate([slot[:, :half], second], 2)
         spot = jnp.arange(2 * nz, dtype=jnp.int32)
         pick = jnp.sum(
             jnp.where(slot[:, :, None, :] == 1 + kz[..., None], spot, 0), 3, dtype=jnp.int32
         )
-        lines = selected(data, pick)
+        lines = [packed(piece) for piece in selected(data, pick, edges)]
         data, lines, mask = hold((data, lines, mask))
     else:
         data, mask = hold((data, mask))
@@ -658,55 +741,41 @@
 
     inverse = (on_right(inverse_z), on_right(inverse_y))
     if small:
-        halves = mask.reshape(groups, coils, slabs, 2, half, nz).swapaxes(2, 3)
-        rank = ranks(halves)
-        begin = rank[:, :, :1, ..., -1:]
-        fits = jnp.max(begin + rank[:, :, 1:, ..., -1:]) <= nz
+        halves = hold(mask.reshape(groups, coils, slabs, 2, half, nz).swapaxes(2, 3))
+        rank, total = ranks(halves)
+        begin = total[:, :, :1]
+        fits = jnp.max(begin + total[:, :, 1:]) <= nz
         rank = jnp.concatenate([rank[:, :, :1], begin + rank[:, :, 1:]], 2)
         code = jnp.where(halves > 0, rank - 1, -1).reshape(groups, coils, ny, nz)
         order = np.arange(ny).reshape(slabs, 2, half).swapaxes(0, 1).reshape(-1)
         sparse_inverse = (inverse[0], inverse[1].reshape(2, ny, -1)[:, order].reshape(2 * ny, -1))
     mask = mask.swapaxes(2, 3)
     duals, spread = tv_planes(image, None, me * width, nx)
-    normal = normal_of(own, first_maps, mask, 0, tables)
-    held = (first_maps, later_maps, mask, data, duals, spread, normal)
+    held = (maps, mask, data, own, duals, spread)
     if small:
-        (first_maps, later_maps, mask, data, duals, spread, normal), lines, code = hold(
-            (held, lines, code)
-        )
+        (maps, mask, data, own, duals, spread), lines, code = hold((held, lines, code))
     else:
-        first_maps, later_maps, mask, data, duals, spread, normal = hold(held)
-
-    def finish(data, code, steps, inverse):
-        data = [packed(data[:, a:b]) for a, b in steps]
-        data = hold(data)
-        more = normal_of(own, later_maps, mask, few, tables)
-        back = ready = None
-        for piece, (a, b) in enumerate(steps):
-            got = sent(data[piece])
-            rest = data[piece + 1 :]
-            if ready is None:
-                got, more, rest = hold((got, more, rest))
-            else:
-                back = ready if back is None else back + ready
-                got, back, rest = hold((got, back, rest))
-            data[piece + 1 :] = rest
-            maps, start = (first_maps, a) if b <= few else (later_maps, a - few)
-            codes = None if code is None else (code, a)
-            ready = back_of(got, codes, maps, inverse, own.shape, start)
-        return more, ready if back is None else back + ready
+        maps, mask, data, own, duals, spread = hold(held)
+
+    def finish(pieces, code, inverse):
+        normal = normal_of(own, maps, mask, tables)
+        back, start = None, 0
+        for turn in range(len(pieces)):
+            got = sent(pieces[turn])
+            if turn == 0:
+                got, normal, pieces = hold((got, normal, pieces))
+            term = back_of(got, code, maps, inverse, own.shape, start)
+            back = term if back is None else back + term
+            start += got.shape[3]
+        return normal, back
 
     def dense(_):
-        return finish(data, None, [(few, coils), (0, few)], inverse)
+        return finish([packed(data)], None, inverse)
 
     def sparse(_):
-        middle = few + (coils - few + 1) // 2
-        steps = [(few, middle), (middle, coils), (0, few)]
-        return finish(lines, code, steps, sparse_inverse)
-
-    more, back = lax.cond(fits, sparse, dense, 0) if small else dense(0)
-    normal = normal + more
-    maps = [(first_maps, 0), (later_maps, few)]
+        return finish(lines, code, sparse_inverse)
+
+    normal, back = lax.cond(fits, sparse, dense, 0) if small else dense(0)
     scale = dual_step / (1.0 + dual_step)
     data_grad = scale * (normal - back)
     change = -primal_step * (data_grad + spread)
@@ -714,12 +783,12 @@
     line = [g * slabs + s for s in range(slabs) for g in range(groups)]
     before = lax.ppermute(guess[-1:], ("coil", "slab"), list(zip(line[:-1], line[1:])))
     after = lax.ppermute(guess[:1], ("coil", "slab"), list(zip(line[1:], line[:-1])))
-    normal = sum(normal_of(guess, m, mask, a, tables) for m, a in maps)
+    normal = normal_of(guess, maps, mask, tables)
     _, spread = tv_planes(jnp.concatenate([before, guess, after], 0), duals, me * width, nx)
     data_grad = data_grad / (1.0 + dual_step) + scale * (normal - back)
     final = (own + change - primal_step * (data_grad + spread)).astype(bf16)
     final = final.reshape(width, 2, slabs, depth, groups, rows).transpose(2, 4, 0, 1, 3, 5)
-    final = swap(final.reshape(devices, -1)).reshape(nx, -1).T
+    final = delivered(final.reshape(devices, -1, LANES)).reshape(nx, -1).T
     return final.reshape(initial_image.shape).astype(f32)
 
 

time: 420 us -> 393 us (0.936)
  waiting for transfers between devices: 82 us -> 162 us
  local copies, waits for them, and re-layouts: 83.2 us -> 42 us
  blocking collectives: 49.4 us -> 24.1 us
  Pallas kernels: 129 us -> 106 us
  other arithmetic: 32.4 us -> 22 us
    all_to_all x5 -> x4, waiting for transfers between devices: 82 us -> 159 us  [swap(): lax.all_to_all(blocks, EVERY, split_axis=0, concat_axis=0, tiled=True)]
    pallas_call x7 -> x4, Pallas kernels: 92.7 us -> 62.8 us  [plane_call(): pl.pallas_call(kernel, out_shape=jax.ShapeDtypeStruct(shape, f32), grid=(...]
    unnamed x54 -> x26, local copies, waits for them, and re-layouts: 17.2 us -> 0.07 us
    all_to_all x1 -> x0, blocking collectives: 16.3 us -> none  [swap(): lax.all_to_all(blocks, EVERY, split_axis=0, concat_axis=0, tiled=True)]
    pallas_call x1 -> x2, Pallas kernels: 17.8 us -> 32.2 us  [the longest x1 17.9 us: selected(): pl.pallas_call(functools.partial(select_kernel, edges), out_shape=[jax.Sh...]
    slice x8 -> x0, local copies, waits for them, and re-layouts: 13.3 us -> none  [the longest x1 9.22 us: by_planes(): later_maps = packed(coil_maps[few:].transpose(4, 0, 1, 2, 3))]
    convert_element_type x3 -> x0, local copies, waits for them, and re-layouts: 9.24 us -> none  [by_planes(): image.transpose(2, 3, 0, 4, 1, 5).reshape(width + 2, 2, nz, ny).astype(f32)]
    all_gather x2, blocking collectives: 33.1 us -> 24.1 us  [by_planes(): masks.append(lax.all_gather(part, 'coil', axis=0))]
  transfers between devices with their start and end apart: 7 -> 6, of which waited for: 4 -> 4; matrix products, arithmetic and copies ran while one was open for 23% -> 15% of each run, Pallas kernels for 30% -> 22%
where the time goes in v3:
time: 393 us; the launch traced here: 389 us
  waiting for transfers between devices  162 us (41%)
  Pallas kernels  106 us (27%)
  local copies, waits for them, and re-layouts  42 us (11%)
  blocking collectives  24.1 us (6%)
  starting transfers between devices  23.5 us (6%)
  other arithmetic  22 us (6%)
  matrix products  8.08 us (2%)
    all_to_all x4, waiting for transfers between devices, swap(): lax.all_to_all(blocks, EVERY, split_axis=0, concat_axis=0, tiled=True)  159 us
    pallas_call x4, Pallas kernels, plane_call(): pl.pallas_call(kernel, out_shape=jax.ShapeDtypeStruct(shape, f32), grid=(...  62.8 us
    all_gather x2, blocking collectives, by_planes(): masks.append(lax.all_gather(part, 'coil', axis=0))  24.1 us
    all_to_all x4, starting transfers between devices, swap(): lax.all_to_all(blocks, EVERY, split_axis=0, concat_axis=0, tiled=True)  20.8 us
    pallas_call x1, Pallas kernels, selected(): pl.pallas_call(functools.partial(select_kernel, edges), out_shape=[jax.Sh...  17.9 us
    pallas_call x1, Pallas kernels, delivered(): pl.pallas_call(deliver_kernel, out_shape=jax.ShapeDtypeStruct(blocks.shap...  14.3 us
    dot_general x1, local copies, waits for them, and re-layouts, by_planes(): jnp.einsum('ckzyx,kjxw->wcjyz', data, inverse_x, preferred_element_type=f32)  13.2 us
    optimization_barrier x1, local copies, waits for them, and re-layouts, by_planes(): image, coil_maps = hold((image, coil_maps))  12.6 us
  transfers between devices with their start and end apart: 6, of which 4 were waited for; matrix products, arithmetic and copies ran while one was open for 15% of the time, Pallas kernels for 22%

profile of v3, /device:TPU:0, one launch (start us, length us, event | category | flops | bytes accessed | tf_op | source)
XLA Modules:
  0.0 389.5 jit_solution(15477785344397174965)
XLA Ops:
  0.0 1.1 convert_element_type.59
  1.3 0.2 fusion.55
  1.5 0.5 fusion.19
  2.0 1.2 reshape.123
  3.2 7.3 %all-to-all-start.3 = ((bf16[32,48,128]{2,1,0:T(8,128)(2,1)}), bf16[32,48,128]{2,1,0:T(8,128)(2,1)S(1)}, u32[]{:S(2)}, u32[]{:S(2)}) async-start(bf16[32,48,128]{2,1,0:T(8,128)(2,1)} %reshape.123), calls=%async_computation.3 | async-start | bytes 786432 | tf_op jit(solution)/shard_map/all_to_all | solution.py:640
  10.6 12.6 %copy.74 = bf16[8,2,16,128,128]{3,2,1,0,4:T(8,128)(2,1)} copy(bf16[8,2,16,128,128]{4,3,2,1,0:T(8,128)(2,1)} %param.16) | data formatting | bytes 16777216 | tf_op jit(solution)/shard_map/optimization_barrier | solution.py:699
  23.2 0.6 fusion.57
  23.8 11.0 %shard_map.129 = bf16[8,8,16,128]{3,2,1,0:T(8,128)(2,1)} custom-call(bf16[8,16,128]{2,1,0:T(8,128)(2,1)} %get-tuple-element.167.own_ref), custom_call_target="tpu_custom_call" | custom-call | flops 1048576 | bytes 524288 | tf_op jit(solution)/shard_map/pallas_call | solution.py:548
  34.9 6.7 %all-to-all-start.4 = ((bf16[32,4,8,2,16,128]{5,4,3,2,1,0:T(8,128)(2,1)}), bf16[32,4,8,2,16,128]{5,4,3,2,1,0:T(8,128)(2,1)}, u32[]{:S(2)}, u32[]{:S(2)}) async-start(bf16[32,4,8,2,16,128]{5,4,3,2,1,0:T(8,128)(2,1)} %bitcast.80), calls=%async_computation.4 | async-start | bytes 16777216 | tf_op jit(solution)/shard_map/all_to_all | solution.py:640
  41.8 6.8 %convolution_bitcast_fusion = bf16[8,128,16,2,128]{4,2,3,1,0:T(8,128)(2,1)} fusion(bf16[2,2,128,128,1,1]{2,3,0,1,5,4:T(8,128)(2,1)S(1)} %copy-done.18, bf16[8,2,128,16,128]{4,3,2,1,0:T(8,128)(2,1)} %param.15, bf16[8,128,16]{2,1,0:T(8,128)(2,1)S(1)} %copy.75), kind=kOutput, calls=%fused_computation.2 | convolution fusion | flops 2151677952 | bytes 16941056 | tf_op jit(solution)/shard_map/ckzyx,kjxw->wcjyz/dot_general | solution.py:712
  48.6 13.2 %copy.77 = bf16[8,128,16,2,128]{1,2,3,0,4:T(8,128)(2,1)} copy(bf16[8,128,16,2,128]{4,2,3,1,0:T(8,128)(2,1)} %convolution_bitcast_fusion) | data formatting | bytes 16777216 | tf_op jit(solution)/shard_map/ckzyx,kjxw->wcjyz/dot_general | solution.py:712
  62.0 0.2 fusion.4
  62.2 2.4 select_reduce_fusion.pick_ref
  64.7 17.9 %shard_map.130 = (bf16[128,6,16,128]{3,2,1,0:T(8,128)(2,1)}, bf16[128,2,16,128]{3,2,1,0:T(8,128)(2,1)}) custom-call(s32[8,8,128]{2,1,0:T(8,128)} %select_reduce_fusion.pick_ref, bf16[128,8,2,16,128]{4,3,2,1,0:T(8,128)(2,1)} %bitcast.77), custom_call_target="tpu_custom_call" | custom-call | flops 268435456 | bytes 12582912 | tf_op jit(solution)/shard_map/pallas_call | solution.py:437
  82.5 0.6 reshape.128
  83.2 2.0 copy.82
  85.2 0.8 reshape.129
  86.0 0.8 slice.176
  87.0 16.6 %all_gather.13 = bf16[4,4,128,128]{3,2,1,0:T(8,128)(2,1)S(1)} all-gather(bf16[1,4,128,128]{3,2,1,0:T(8,128)(2,1)S(1)} %bitcast.98), channel_id=1, replica_groups=mesh['coil'=4,'slab'=8] {'coil'}, dimensions={0}, use_global_device_ids=true | all-gather | bytes 655360 | tf_op jit(solution)/shard_map/all_gather | solution.py:739
  103.6 0.3 copy.81
  103.9 7.5 %all-gather = bf16[16,128,128]{2,1,0:T(8,128)(2,1)S(1)} all-gather(bf16[4,128,128]{2,1,0:T(8,128)(2,1)S(1)} %bitcast.97), channel_id=2, replica_groups=mesh['coil'=4,'slab'=8] {'coil'}, dimensions={0}, use_global_device_ids=true | all-gather | bytes 655360 | tf_op jit(solution)/shard_map/all_gather | solution.py:739
  111.4 0.3 copy.80
  111.7 1.1 pad_maximum_fusion.1
  112.8 0.7 copy.83
  113.5 0.2 copy.101
  113.8 0.2 slice_subtract_fusion.1
  114.0 0.2 multiply_reduce_fusion.4
  114.2 0.2 multiply_reduce_fusion.3
  114.6 1.4 broadcast_select_fusion
  116.0 0.9 slice.185
  117.0 0.9 slice.183
  117.9 0.4 convolution_convert_fusion
  118.3 0.5 convolution_convert_fusion.1
  118.8 2.3 fusion.5
  121.8 2.6 fusion.27
  124.4 3.5 fusion.1
  127.9 99.7 %all-to-all-done.4 = bf16[32,4,8,2,16,128]{5,4,3,2,1,0:T(8,128)(2,1)} async-done(((bf16[32,4,8,2,16,128]{5,4,3,2,1,0:T(8,128)(2,1)}), bf16[32,4,8,2,16,128]{5,4,3,2,1,0:T(8,128)(2,1)}, u32[]{:S(2)}, u32[]{:S(2)}) %all-to-all-start.4) | async-done | bytes 8388640 | tf_op jit(solution)/shard_map/all_to_all | solution.py:640
  227.6 111.3 %conditional.1 = (f32[4,2,128,128]{3,2,1,0:T(8,128)S(1)}, f32[4,2,128,128]{3,2,1,0:T(8,128)}) conditional(s32[]{:T(128)} %convert_element_type.72, (bf16[128,8,2,16,128]{4,3,2,1,0:T(8,128)(2,1)}, f32[4,2,128,128]{3,2,1,0:T(8,128)S(1)}, bf16[8,4,4,8,2,16,128]{6,5,4,3,2,1,0:T(8,128)(2,1)}, bf16[4,8,128,128]{3,2,1,0:T(8,128)(2,1)}, ...), branch_computations={%region_5.6_spmd, %region_6.7_spmd} | conditional | flops 12885033984 | bytes 54526028 | solution.py:778
  227.6 0.8 copy-done.10
  228.4 2.8 all-to-all-start.1
  231.2 22.2 %branch_1_fun.3 = f32[4,2,128,128]{3,2,1,0:T(8,128)} custom-call(f32[4,2,128,128]{3,2,1,0:T(8,128)} %copy-done.10, bf16[8,4,4,8,2,16,128]{6,5,4,3,2,1,0:T(8,128)(2,1)} %get-tuple-element.76.maps_ref, bf16[4,8,128,128]{3,2,1,0:T(8,128)(2,1)} %get-tuple-element.77.mask_ref, bf16[256,256]{1,0:T(8,128)(2,1)S(1)} %get-tuple-element.80.gz_ref, ...), custom_call_target="tpu_custom_call" | custom-call | flops 8589934592 | bytes 8388608 | tf_op jit(solution)/shard_map/cond/branch_1_fun/pallas_call | solution.py:565
  253.4 49.3 %all-to-all-done.1 = bf16[32,4,6,16,128]{4,3,2,1,0:T(8,128)(2,1)S(1)} async-done(((bf16[32,4,6,16,128]{4,3,2,1,0:T(8,128)(2,1)}), bf16[32,4,6,16,128]{4,3,2,1,0:T(8,128)(2,1)S(1)}, u32[]{:S(2)}, u32[]{:S(2)}) %all-to-all-start.1) | async-done | bytes 3145760 | tf_op jit(solution)/shard_map/cond/branch_1_fun/all_to_all | solution.py:640
  302.6 4.0 %all-to-all-start.2 = ((bf16[32,4,2,16,128]{4,3,2,1,0:T(8,128)(2,1)}), bf16[32,4,2,16,128]{4,3,2,1,0:T(8,128)(2,1)}, u32[]{:S(2)}, u32[]{:S(2)}) async-start(bf16[32,4,2,16,128]{4,3,2,1,0:T(8,128)(2,1)} %get-tuple-element.90), calls=%async_computation.2 | async-start | bytes 2097152 | tf_op jit(solution)/shard_map/cond/branch_1_fun/all_to_all | solution.py:640
  306.8 0.9 gather_fusion
  307.7 13.8 %branch_1_fun.4 = f32[4,2,128,128]{3,2,1,0:T(8,128)S(1)} custom-call(bf16[8,4,4,6,16,128]{5,4,3,2,1,0:T(8,128)(2,1)S(1)} %bitcast.74, s32[4,8,128,128]{3,2,1,0:T(8,128)} %get-tuple-element.85.code_ref, bf16[8,4,4,8,2,16,128]{6,5,4,3,2,1,0:T(8,128)(2,1)} %get-tuple-element.76.maps_ref, bf16[256,256]{1,0:T(8,128)(2,1)S(1)} %get-tuple-element.86.gz_ref, ...), custom_call_target="tpu_custom_call" | custom-call | flops 3221225472 | bytes 12582912 | tf_op jit(solution)/shard_map/cond/branch_1_fun/pallas_call | solution.py:565
  321.5 0.8 copy-done
  322.3 10.5 %all-to-all-done.2 = bf16[32,4,2,16,128]{4,3,2,1,0:T(8,128)(2,1)} async-done(((bf16[32,4,2,16,128]{4,3,2,1,0:T(8,128)(2,1)}), bf16[32,4,2,16,128]{4,3,2,1,0:T(8,128)(2,1)}, u32[]{:S(2)}, u32[]{:S(2)}) %all-to-all-start.2) | async-done | bytes 1048608 | tf_op jit(solution)/shard_map/cond/branch_1_fun/all_to_all | solution.py:640
  332.8 5.1 %branch_1_fun.5 = f32[4,2,128,128]{3,2,1,0:T(8,128)S(1)} custom-call(bf16[8,4,4,2,16,128]{5,4,3,2,1,0:T(8,128)(2,1)} %bitcast.6.data_ref, s32[4,8,128,128]{3,2,1,0:T(8,128)} %get-tuple-element.85.code_ref, bf16[8,4,4,8,2,16,128]{6,5,4,3,2,1,0:T(8,128)(2,1)} %get-tuple-element.76.maps_ref, bf16[256,256]{1,0:T(8,128)(2,1)S(1)} %get-tuple-element.86.gz_ref, ...), custom_call_target="tpu_custom_call" | custom-call | flops 1073741824 | bytes 4194304 | tf_op jit(solution)/shard_map/cond/branch_1_fun/pallas_call | solution.py:565
  338.0 0.9 add.105
  338.9 1.5 multiply_add_fusion.2.guess_ref
  340.4 1.4 collective-permute-start
  341.8 21.8 %shard_map.131 = f32[4,2,128,128]{3,2,1,0:T(8,128)S(1)} custom-call(f32[4,2,128,128]{3,2,1,0:T(8,128)S(1)} %multiply_add_fusion.2.guess_ref, bf16[8,4,4,8,2,16,128]{6,5,4,3,2,1,0:T(8,128)(2,1)} %bitcast.12.maps_ref, bf16[4,8,128,128]{3,2,1,0:T(8,128)(2,1)} %get-tuple-element.131.mask_ref, bf16[256,256]{1,0:T(8,128)(2,1)} %constant.79.clone.fy_ref.gz_ref, ...), custom_call_target="tpu_custom_call" | custom-call | flops 8589934592 | bytes 8388608 | tf_op jit(solution)/shard_map/pallas_call | solution.py:565
  363.6 1.3 collective-permute-start.1
  364.9 0.2 fusion.12
  365.5 3.0 collective-permute-done.1
  368.5 0.2 multiply_reduce_fusion
  368.9 0.5 broadcast_multiply_fusion.1
  369.5 1.7 fusion.25
  371.2 0.4 reshape.132
  371.6 0.2 copy.100
  371.9 1.2 reshape.133.block_ref
  373.1 14.3 %shard_map.132 = bf16[32,32,128]{2,1,0:T(8,128)(2,1)} custom-call(bf16[32,32,128]{2,1,0:T(8,128)(2,1)} %reshape.133.block_ref), custom_call_target="tpu_custom_call" | custom-call | flops 8388608 | bytes 524288 | tf_op jit(solution)/shard_map/pallas_call | solution.py:500
  387.4 1.1 reshape.135
  388.5 1.0 copy.86
  (61 shorter events, 1.8 us)
Async XLA Ops:
  3.2 31.6 %all-to-all-start.3 = ((bf16[32,48,128]{2,1,0:T(8,128)(2,1)}), bf16[32,48,128]{2,1,0:T(8,128)(2,1)S(1)}, u32[]{:S(2)}, u32[]{:S(2)}) async-start(bf16[32,48,128]{2,1,0:T(8,128)(2,1)} %reshape.123), calls=%async_computation.3 | async-start | bytes 786432 | tf_op jit(solution)/shard_map/all_to_all | solution.py:640
  10.6 12.7 %copy-start.15 = (s32[8,128,16]{1,2,0:T(8,128)S(1)}, s32[8,128,16]{1,2,0:T(8,128)}, u32[]{:S(2)}) copy-start(s32[8,128,16]{1,2,0:T(8,128)} %param.17) | copy-start | bytes 196612
  34.9 6.9 %copy-start.18 = (bf16[2,2,128,128,1,1]{2,3,0,1,5,4:T(8,128)(2,1)S(1)}, bf16[2,2,128,128,1,1]{2,3,0,1,5,4:T(8,128)(2,1)}, u32[]{:S(2)}) copy-start(bf16[2,2,128,128,1,1]{2,3,0,1,5,4:T(8,128)(2,1)} %constant.105) | copy-start | bytes 393220
  34.9 192.7 %all-to-all-start.4 = ((bf16[32,4,8,2,16,128]{5,4,3,2,1,0:T(8,128)(2,1)}), bf16[32,4,8,2,16,128]{5,4,3,2,1,0:T(8,128)(2,1)}, u32[]{:S(2)}, u32[]{:S(2)}) async-start(bf16[32,4,8,2,16,128]{5,4,3,2,1,0:T(8,128)(2,1)} %bitcast.80), calls=%async_computation.4 | async-start | bytes 16777216 | tf_op jit(solution)/shard_map/all_to_all | solution.py:640
  64.7 22.3 %copy-start.14 = (bf16[8,8,16,128]{3,2,1,0:T(8,128)(2,1)S(1)}, bf16[8,8,16,128]{3,2,1,0:T(8,128)(2,1)}, u32[]{:S(2)}) copy-start(bf16[8,8,16,128]{3,2,1,0:T(8,128)(2,1)} %shard_map.129) | copy-start | bytes 786436
  116.0 8.4 %copy-start.2 = (f32[5,2,128,128]{3,2,1,0:T(8,128)}, f32[5,2,128,128]{3,2,1,0:T(8,128)S(1)}, u32[]{:S(2)}) copy-start(f32[5,2,128,128]{3,2,1,0:T(8,128)S(1)} %get-tuple-element.139) | copy-start | bytes 1966084
  116.0 8.4 %copy-start.4 = (f32[5,2,128,128]{3,2,1,0:T(8,128)}, f32[5,2,128,128]{3,2,1,0:T(8,128)S(1)}, u32[]{:S(2)}) copy-start(f32[5,2,128,128]{3,2,1,0:T(8,128)S(1)} %get-tuple-element.138) | copy-start | bytes 1966084
  118.8 108.8 %copy-start.8 = (f32[4,2,128,128]{3,2,1,0:T(8,128)S(1)}, f32[4,2,128,128]{3,2,1,0:T(8,128)}, u32[]{:S(2)}) copy-start(f32[4,2,128,128]{3,2,1,0:T(8,128)} %slice.176) | copy-start | bytes 1572868
  118.8 108.8 %copy-start.11 = (bf16[256,256]{1,0:T(8,128)(2,1)S(1)}, bf16[256,256]{1,0:T(8,128)(2,1)}, u32[]{:S(2)}) copy-start(bf16[256,256]{1,0:T(8,128)(2,1)} %constant.80.clone.fz_ref.gy_ref) | copy-start | bytes 393220
  118.8 108.8 %copy-start.17 = (bf16[256,256]{1,0:T(8,128)(2,1)S(1)}, bf16[256,256]{1,0:T(8,128)(2,1)}, u32[]{:S(2)}) copy-start(bf16[256,256]{1,0:T(8,128)(2,1)} %constant.79.clone.fy_ref.gz_ref) | copy-start | bytes 393220
  227.6 0.8 copy-start.10
  228.4 74.2 %all-to-all-start.1 = ((bf16[32,4,6,16,128]{4,3,2,1,0:T(8,128)(2,1)}), bf16[32,4,6,16,128]{4,3,2,1,0:T(8,128)(2,1)S(1)}, u32[]{:S(2)}, u32[]{:S(2)}) async-start(bf16[32,4,6,16,128]{4,3,2,1,0:T(8,128)(2,1)} %get-tuple-element.74), calls=%async_computation.1 | async-start | bytes 6291456 | tf_op jit(solution)/shard_map/cond/branch_1_fun/all_to_all | solution.py:640
  231.2 75.6 %copy-start.16 = (s32[128]{0:T(128)S(1)}, s32[128]{0:T(128)}, u32[]{:S(2)}) copy-start(s32[128]{0:T(128)} %constant.104) | copy-start | bytes 1540 | tf_op jit(solution)/shard_map/cond
  302.6 30.2 %all-to-all-start.2 = ((bf16[32,4,2,16,128]{4,3,2,1,0:T(8,128)(2,1)}), bf16[32,4,2,16,128]{4,3,2,1,0:T(8,128)(2,1)}, u32[]{:S(2)}, u32[]{:S(2)}) async-start(bf16[32,4,2,16,128]{4,3,2,1,0:T(8,128)(2,1)} %get-tuple-element.90), calls=%async_computation.2 | async-start | bytes 2097152 | tf_op jit(solution)/shard_map/cond/branch_1_fun/all_to_all | solution.py:640
  321.5 0.8 copy-start
  322.3 16.6 %copy-start.12 = (f32[4,2,128,128]{3,2,1,0:T(8,128)S(1)}, f32[4,2,128,128]{3,2,1,0:T(8,128)}, u32[]{:S(2)}) copy-start(f32[4,2,128,128]{3,2,1,0:T(8,128)} %branch_1_fun.3) | copy-start | bytes 1572868 | tf_op jit(solution)/shard_map/cond
  332.8 5.1 %copy-start.1 = (f32[4,2,128,128]{3,2,1,0:T(8,128)S(1)}, f32[4,2,128,128]{3,2,1,0:T(8,128)}, u32[]{:S(2)}) copy-start(f32[4,2,128,128]{3,2,1,0:T(8,128)} %copy-done) | copy-start | bytes 1572868 | tf_op jit(solution)/shard_map/cond
  340.4 24.8 %copy-start.3 = (f32[5,2,128,128]{3,2,1,0:T(8,128)S(1)}, f32[5,2,128,128]{3,2,1,0:T(8,128)}, u32[]{:S(2)}) copy-start(f32[5,2,128,128]{3,2,1,0:T(8,128)} %copy-done.2) | copy-start | bytes 1966084
  340.4 25.0 %copy-start.5 = (f32[5,2,128,128]{3,2,1,0:T(8,128)S(1)}, f32[5,2,128,128]{3,2,1,0:T(8,128)}, u32[]{:S(2)}) copy-start(f32[5,2,128,128]{3,2,1,0:T(8,128)} %copy-done.4) | copy-start | bytes 1966084
  340.4 28.2 %copy-start.6 = (f32[5,2,128,128]{3,2,1,0:T(8,128)S(1)}, f32[5,2,128,128]{3,2,1,0:T(8,128)}, u32[]{:S(2)}) copy-start(f32[5,2,128,128]{3,2,1,0:T(8,128)} %get-tuple-element.140) | copy-start | bytes 1966084
  340.4 24.5 %collective-permute-start = (f32[1,2,128,128]{3,2,1,0:T(8,128)S(1)}, f32[1,2,128,128]{3,2,1,0:T(8,128)S(1)}, u32[]{:S(2)}, u32[]{:S(2)}) collective-permute-start(f32[1,2,128,128]{3,2,1,0:T(8,128)S(1)} %get-tuple-element.154), channel_id=1, source_target_pairs={{0,8},{8,16},{16,24},{24,1},{1,9},{9,17},{17,25},{25,2},{2,10},{10... | collective-permute-start | bytes 393224 | tf_op jit(solution)/shard_map/ppermute | solution.py:784
  363.6 4.9 %collective-permute-start.1 = (f32[1,2,128,128]{3,2,1,0:T(8,128)S(1)}, f32[1,2,128,128]{3,2,1,0:T(8,128)S(1)}, u32[]{:S(2)}, u32[]{:S(2)}) collective-permute-start(f32[1,2,128,128]{3,2,1,0:T(8,128)S(1)} %get-tuple-element.153), channel_id=1, source_target_pairs={{8,0},{16,8},{24,16},{1,24},{9,1},{17,9},{25,17},{2,25},{10,2},{18... | collective-permute-start | bytes 393224 | tf_op jit(solution)/shard_map/ppermute | solution.py:785
  365.1 4.3 %copy-start.7 = (f32[4,2,128,128]{3,2,1,0:T(8,128)S(1)}, f32[4,2,128,128]{3,2,1,0:T(8,128)}, u32[]{:S(2)}) copy-start(f32[4,2,128,128]{3,2,1,0:T(8,128)} %fusion.27) | copy-start | bytes 1572868
  365.2 4.3 %copy-start.9 = (f32[4,2,128,128]{3,2,1,0:T(8,128)S(1)}, f32[4,2,128,128]{3,2,1,0:T(8,128)}, u32[]{:S(2)}) copy-start(f32[4,2,128,128]{3,2,1,0:T(8,128)} %slice.176) | copy-start | bytes 1572868

commit v4 on v3

--- a/solution.py
+++ b/solution.py
@@ -11,7 +11,6 @@
 from jax.experimental.pallas import tpu as pltpu
 from jax.sharding import PartitionSpec as P
 
-ITERS = 2
 
 dual_step = 0.25
 primal_step = 0.25
@@ -326,9 +325,9 @@
             ],
             0,
         )
-        spectrum = dot(fz_ref[...], pieces).astype(bf16)
-        mask = jnp.concatenate([mask_ref[c, turn] for c in range(group)], 1)
-        spectrum = spectrum * jnp.concatenate([mask, mask], 0)
+        mask = jnp.concatenate([mask_ref[c, turn] for c in range(group)], 1).astype(f32)
+        spectrum = dot(fz_ref[...], pieces) * jnp.concatenate([mask, mask], 0)
+        spectrum = spectrum.astype(bf16)
         pieces = dot(gz_ref[...], spectrum).astype(bf16)
         pieces = jnp.concatenate(
             [

time: 393 us -> 393 us (level)
  no operation moved by 1% of the time
where the time goes in v4:
time: 393 us; the launch traced here: 389 us
  waiting for transfers between devices  162 us (41%)
  Pallas kernels  106 us (27%)
  local copies, waits for them, and re-layouts  42 us (11%)
  blocking collectives  24.1 us (6%)
  starting transfers between devices  23.5 us (6%)
  other arithmetic  22 us (6%)
  matrix products  8.08 us (2%)
    all_to_all x4, waiting for transfers between devices, swap(): lax.all_to_all(blocks, EVERY, split_axis=0, concat_axis=0, tiled=True)  159 us
    pallas_call x4, Pallas kernels, plane_call(): pl.pallas_call(kernel, out_shape=jax.ShapeDtypeStruct(shape, f32), grid=(...  62.8 us
    all_gather x2, blocking collectives, by_planes(): masks.append(lax.all_gather(part, 'coil', axis=0))  24.1 us
    all_to_all x4, starting transfers between devices, swap(): lax.all_to_all(blocks, EVERY, split_axis=0, concat_axis=0, tiled=True)  20.8 us
    pallas_call x1, Pallas kernels, selected(): pl.pallas_call(functools.partial(select_kernel, edges), out_shape=[jax.Sh...  17.9 us
    pallas_call x1, Pallas kernels, delivered(): pl.pallas_call(deliver_kernel, out_shape=jax.ShapeDtypeStruct(blocks.shap...  14.3 us
    dot_general x1, local copies, waits for them, and re-layouts, by_planes(): jnp.einsum('ckzyx,kjxw->wcjyz', data, inverse_x, preferred_element_type=f32)  13.2 us
    optimization_barrier x1, local copies, waits for them, and re-layouts, by_planes(): image, coil_maps = hold((image, coil_maps))  12.6 us
  transfers between devices with their start and end apart: 6, of which 4 were waited for; matrix products, arithmetic and copies ran while one was open for 15% of the time, Pallas kernels for 22%

profile of v4, /device:TPU:0, one launch (start us, length us, event | category | flops | bytes accessed | tf_op | source)
XLA Modules:
  0.0 389.5 jit_solution(8032845332828676458)
XLA Ops:
  0.0 1.1 convert_element_type.59
  1.3 0.2 fusion.55
  1.5 0.5 fusion.19
  2.0 1.2 reshape.123
  3.2 7.3 %all-to-all-start.3 = ((bf16[32,48,128]{2,1,0:T(8,128)(2,1)}), bf16[32,48,128]{2,1,0:T(8,128)(2,1)S(1)}, u32[]{:S(2)}, u32[]{:S(2)}) async-start(bf16[32,48,128]{2,1,0:T(8,128)(2,1)} %reshape.123), calls=%async_computation.3 | async-start | bytes 786432 | tf_op jit(solution)/shard_map/all_to_all | solution.py:639
  10.6 12.6 %copy.74 = bf16[8,2,16,128,128]{3,2,1,0,4:T(8,128)(2,1)} copy(bf16[8,2,16,128,128]{4,3,2,1,0:T(8,128)(2,1)} %param.16) | data formatting | bytes 16777216 | tf_op jit(solution)/shard_map/optimization_barrier | solution.py:698
  23.2 0.6 fusion.57
  23.8 11.0 %shard_map.129 = bf16[8,8,16,128]{3,2,1,0:T(8,128)(2,1)} custom-call(bf16[8,16,128]{2,1,0:T(8,128)(2,1)} %get-tuple-element.167.own_ref), custom_call_target="tpu_custom_call" | custom-call | flops 1048576 | bytes 524288 | tf_op jit(solution)/shard_map/pallas_call | solution.py:547
  34.9 6.7 %all-to-all-start.4 = ((bf16[32,4,8,2,16,128]{5,4,3,2,1,0:T(8,128)(2,1)}), bf16[32,4,8,2,16,128]{5,4,3,2,1,0:T(8,128)(2,1)}, u32[]{:S(2)}, u32[]{:S(2)}) async-start(bf16[32,4,8,2,16,128]{5,4,3,2,1,0:T(8,128)(2,1)} %bitcast.80), calls=%async_computation.4 | async-start | bytes 16777216 | tf_op jit(solution)/shard_map/all_to_all | solution.py:639
  41.8 6.8 %convolution_bitcast_fusion = bf16[8,128,16,2,128]{4,2,3,1,0:T(8,128)(2,1)} fusion(bf16[2,2,128,128,1,1]{2,3,0,1,5,4:T(8,128)(2,1)S(1)} %copy-done.18, bf16[8,2,128,16,128]{4,3,2,1,0:T(8,128)(2,1)} %param.15, bf16[8,128,16]{2,1,0:T(8,128)(2,1)S(1)} %copy.75), kind=kOutput, calls=%fused_computation.2 | convolution fusion | flops 2151677952 | bytes 16941056 | tf_op jit(solution)/shard_map/ckzyx,kjxw->wcjyz/dot_general | solution.py:711
  48.6 13.2 %copy.77 = bf16[8,128,16,2,128]{1,2,3,0,4:T(8,128)(2,1)} copy(bf16[8,128,16,2,128]{4,2,3,1,0:T(8,128)(2,1)} %convolution_bitcast_fusion) | data formatting | bytes 16777216 | tf_op jit(solution)/shard_map/ckzyx,kjxw->wcjyz/dot_general | solution.py:711
  62.0 0.2 fusion.4
  62.2 2.4 select_reduce_fusion.pick_ref
  64.7 17.9 %shard_map.130 = (bf16[128,6,16,128]{3,2,1,0:T(8,128)(2,1)}, bf16[128,2,16,128]{3,2,1,0:T(8,128)(2,1)}) custom-call(s32[8,8,128]{2,1,0:T(8,128)} %select_reduce_fusion.pick_ref, bf16[128,8,2,16,128]{4,3,2,1,0:T(8,128)(2,1)} %bitcast.77), custom_call_target="tpu_custom_call" | custom-call | flops 268435456 | bytes 12582912 | tf_op jit(solution)/shard_map/pallas_call | solution.py:436
  82.5 0.6 reshape.128
  83.2 2.0 copy.82
  85.2 0.8 reshape.129
  86.0 0.8 slice.176
  87.0 16.6 %all_gather.13 = bf16[4,4,128,128]{3,2,1,0:T(8,128)(2,1)S(1)} all-gather(bf16[1,4,128,128]{3,2,1,0:T(8,128)(2,1)S(1)} %bitcast.98), channel_id=1, replica_groups=mesh['coil'=4,'slab'=8] {'coil'}, dimensions={0}, use_global_device_ids=true | all-gather | bytes 655360 | tf_op jit(solution)/shard_map/all_gather | solution.py:738
  103.6 0.3 copy.81
  103.9 7.5 %all-gather = bf16[16,128,128]{2,1,0:T(8,128)(2,1)S(1)} all-gather(bf16[4,128,128]{2,1,0:T(8,128)(2,1)S(1)} %bitcast.97), channel_id=2, replica_groups=mesh['coil'=4,'slab'=8] {'coil'}, dimensions={0}, use_global_device_ids=true | all-gather | bytes 655360 | tf_op jit(solution)/shard_map/all_gather | solution.py:738
  111.4 0.3 copy.80
  111.7 1.1 pad_maximum_fusion.1
  112.8 0.7 copy.83
  113.5 0.2 copy.101
  113.8 0.2 slice_subtract_fusion.1
  114.0 0.2 multiply_reduce_fusion.4
  114.2 0.2 multiply_reduce_fusion.3
  114.6 1.4 broadcast_select_fusion
  116.0 0.9 slice.185
  117.0 0.9 slice.183
  117.9 0.4 convolution_convert_fusion
  118.3 0.5 convolution_convert_fusion.1
  118.8 2.3 fusion.5
  121.8 2.6 fusion.27
  124.4 3.5 fusion.1
  127.9 99.7 %all-to-all-done.4 = bf16[32,4,8,2,16,128]{5,4,3,2,1,0:T(8,128)(2,1)} async-done(((bf16[32,4,8,2,16,128]{5,4,3,2,1,0:T(8,128)(2,1)}), bf16[32,4,8,2,16,128]{5,4,3,2,1,0:T(8,128)(2,1)}, u32[]{:S(2)}, u32[]{:S(2)}) %all-to-all-start.4) | async-done | bytes 8388640 | tf_op jit(solution)/shard_map/all_to_all | solution.py:639
  227.6 111.3 %conditional.1 = (f32[4,2,128,128]{3,2,1,0:T(8,128)S(1)}, f32[4,2,128,128]{3,2,1,0:T(8,128)}) conditional(s32[]{:T(128)} %convert_element_type.72, (bf16[128,8,2,16,128]{4,3,2,1,0:T(8,128)(2,1)}, f32[4,2,128,128]{3,2,1,0:T(8,128)S(1)}, bf16[8,4,4,8,2,16,128]{6,5,4,3,2,1,0:T(8,128)(2,1)}, bf16[4,8,128,128]{3,2,1,0:T(8,128)(2,1)}, ...), branch_computations={%region_5.6_spmd, %region_6.7_spmd} | conditional | flops 12885033984 | bytes 54526028 | solution.py:777
  227.6 0.8 copy-done.10
  228.4 2.8 all-to-all-start.1
  231.2 22.2 %branch_1_fun.3 = f32[4,2,128,128]{3,2,1,0:T(8,128)} custom-call(f32[4,2,128,128]{3,2,1,0:T(8,128)} %copy-done.10, bf16[8,4,4,8,2,16,128]{6,5,4,3,2,1,0:T(8,128)(2,1)} %get-tuple-element.76.maps_ref, bf16[4,8,128,128]{3,2,1,0:T(8,128)(2,1)} %get-tuple-element.77.mask_ref, bf16[256,256]{1,0:T(8,128)(2,1)S(1)} %get-tuple-element.80.gz_ref, ...), custom_call_target="tpu_custom_call" | custom-call | flops 8589934592 | bytes 8388608 | tf_op jit(solution)/shard_map/cond/branch_1_fun/pallas_call | solution.py:564
  253.4 49.3 %all-to-all-done.1 = bf16[32,4,6,16,128]{4,3,2,1,0:T(8,128)(2,1)S(1)} async-done(((bf16[32,4,6,16,128]{4,3,2,1,0:T(8,128)(2,1)}), bf16[32,4,6,16,128]{4,3,2,1,0:T(8,128)(2,1)S(1)}, u32[]{:S(2)}, u32[]{:S(2)}) %all-to-all-start.1) | async-done | bytes 3145760 | tf_op jit(solution)/shard_map/cond/branch_1_fun/all_to_all | solution.py:639
  302.6 4.0 %all-to-all-start.2 = ((bf16[32,4,2,16,128]{4,3,2,1,0:T(8,128)(2,1)}), bf16[32,4,2,16,128]{4,3,2,1,0:T(8,128)(2,1)}, u32[]{:S(2)}, u32[]{:S(2)}) async-start(bf16[32,4,2,16,128]{4,3,2,1,0:T(8,128)(2,1)} %get-tuple-element.90), calls=%async_computation.2 | async-start | bytes 2097152 | tf_op jit(solution)/shard_map/cond/branch_1_fun/all_to_all | solution.py:639
  306.8 0.9 gather_fusion
  307.7 13.8 %branch_1_fun.4 = f32[4,2,128,128]{3,2,1,0:T(8,128)S(1)} custom-call(bf16[8,4,4,6,16,128]{5,4,3,2,1,0:T(8,128)(2,1)S(1)} %bitcast.74, s32[4,8,128,128]{3,2,1,0:T(8,128)} %get-tuple-element.85.code_ref, bf16[8,4,4,8,2,16,128]{6,5,4,3,2,1,0:T(8,128)(2,1)} %get-tuple-element.76.maps_ref, bf16[256,256]{1,0:T(8,128)(2,1)S(1)} %get-tuple-element.86.gz_ref, ...), custom_call_target="tpu_custom_call" | custom-call | flops 3221225472 | bytes 12582912 | tf_op jit(solution)/shard_map/cond/branch_1_fun/pallas_call | solution.py:564
  321.5 0.8 copy-done
  322.3 10.5 %all-to-all-done.2 = bf16[32,4,2,16,128]{4,3,2,1,0:T(8,128)(2,1)} async-done(((bf16[32,4,2,16,128]{4,3,2,1,0:T(8,128)(2,1)}), bf16[32,4,2,16,128]{4,3,2,1,0:T(8,128)(2,1)}, u32[]{:S(2)}, u32[]{:S(2)}) %all-to-all-start.2) | async-done | bytes 1048608 | tf_op jit(solution)/shard_map/cond/branch_1_fun/all_to_all | solution.py:639
  332.8 5.1 %branch_1_fun.5 = f32[4,2,128,128]{3,2,1,0:T(8,128)S(1)} custom-call(bf16[8,4,4,2,16,128]{5,4,3,2,1,0:T(8,128)(2,1)} %bitcast.6.data_ref, s32[4,8,128,128]{3,2,1,0:T(8,128)} %get-tuple-element.85.code_ref, bf16[8,4,4,8,2,16,128]{6,5,4,3,2,1,0:T(8,128)(2,1)} %get-tuple-element.76.maps_ref, bf16[256,256]{1,0:T(8,128)(2,1)S(1)} %get-tuple-element.86.gz_ref, ...), custom_call_target="tpu_custom_call" | custom-call | flops 1073741824 | bytes 4194304 | tf_op jit(solution)/shard_map/cond/branch_1_fun/pallas_call | solution.py:564
  338.0 0.9 add.105
  338.9 1.5 multiply_add_fusion.2.guess_ref
  340.4 1.4 collective-permute-start
  341.8 21.8 %shard_map.131 = f32[4,2,128,128]{3,2,1,0:T(8,128)S(1)} custom-call(f32[4,2,128,128]{3,2,1,0:T(8,128)S(1)} %multiply_add_fusion.2.guess_ref, bf16[8,4,4,8,2,16,128]{6,5,4,3,2,1,0:T(8,128)(2,1)} %bitcast.12.maps_ref, bf16[4,8,128,128]{3,2,1,0:T(8,128)(2,1)} %get-tuple-element.131.mask_ref, bf16[256,256]{1,0:T(8,128)(2,1)} %constant.79.clone.fy_ref.gz_ref, ...), custom_call_target="tpu_custom_call" | custom-call | flops 8589934592 | bytes 8388608 | tf_op jit(solution)/shard_map/pallas_call | solution.py:564
  363.6 1.3 collective-permute-start.1
  364.9 0.2 fusion.12
  365.5 3.0 collective-permute-done.1
  368.5 0.2 multiply_reduce_fusion
  368.9 0.5 broadcast_multiply_fusion.1
  369.5 1.7 fusion.25
  371.2 0.4 reshape.132
  371.6 0.2 copy.100
  371.9 1.2 reshape.133.block_ref
  373.1 14.3 %shard_map.132 = bf16[32,32,128]{2,1,0:T(8,128)(2,1)} custom-call(bf16[32,32,128]{2,1,0:T(8,128)(2,1)} %reshape.133.block_ref), custom_call_target="tpu_custom_call" | custom-call | flops 8388608 | bytes 524288 | tf_op jit(solution)/shard_map/pallas_call | solution.py:499
  387.4 1.1 reshape.135
  388.5 1.0 copy.86
  (61 shorter events, 1.8 us)
Async XLA Ops:
  3.2 31.6 %all-to-all-start.3 = ((bf16[32,48,128]{2,1,0:T(8,128)(2,1)}), bf16[32,48,128]{2,1,0:T(8,128)(2,1)S(1)}, u32[]{:S(2)}, u32[]{:S(2)}) async-start(bf16[32,48,128]{2,1,0:T(8,128)(2,1)} %reshape.123), calls=%async_computation.3 | async-start | bytes 786432 | tf_op jit(solution)/shard_map/all_to_all | solution.py:639
  10.6 12.7 %copy-start.15 = (s32[8,128,16]{1,2,0:T(8,128)S(1)}, s32[8,128,16]{1,2,0:T(8,128)}, u32[]{:S(2)}) copy-start(s32[8,128,16]{1,2,0:T(8,128)} %param.17) | copy-start | bytes 196612
  34.9 6.9 %copy-start.18 = (bf16[2,2,128,128,1,1]{2,3,0,1,5,4:T(8,128)(2,1)S(1)}, bf16[2,2,128,128,1,1]{2,3,0,1,5,4:T(8,128)(2,1)}, u32[]{:S(2)}) copy-start(bf16[2,2,128,128,1,1]{2,3,0,1,5,4:T(8,128)(2,1)} %constant.105) | copy-start | bytes 393220
  34.9 192.7 %all-to-all-start.4 = ((bf16[32,4,8,2,16,128]{5,4,3,2,1,0:T(8,128)(2,1)}), bf16[32,4,8,2,16,128]{5,4,3,2,1,0:T(8,128)(2,1)}, u32[]{:S(2)}, u32[]{:S(2)}) async-start(bf16[32,4,8,2,16,128]{5,4,3,2,1,0:T(8,128)(2,1)} %bitcast.80), calls=%async_computation.4 | async-start | bytes 16777216 | tf_op jit(solution)/shard_map/all_to_all | solution.py:639
  64.7 22.3 %copy-start.14 = (bf16[8,8,16,128]{3,2,1,0:T(8,128)(2,1)S(1)}, bf16[8,8,16,128]{3,2,1,0:T(8,128)(2,1)}, u32[]{:S(2)}) copy-start(bf16[8,8,16,128]{3,2,1,0:T(8,128)(2,1)} %shard_map.129) | copy-start | bytes 786436
  116.0 8.4 %copy-start.2 = (f32[5,2,128,128]{3,2,1,0:T(8,128)}, f32[5,2,128,128]{3,2,1,0:T(8,128)S(1)}, u32[]{:S(2)}) copy-start(f32[5,2,128,128]{3,2,1,0:T(8,128)S(1)} %get-tuple-element.139) | copy-start | bytes 1966084
  116.0 8.4 %copy-start.4 = (f32[5,2,128,128]{3,2,1,0:T(8,128)}, f32[5,2,128,128]{3,2,1,0:T(8,128)S(1)}, u32[]{:S(2)}) copy-start(f32[5,2,128,128]{3,2,1,0:T(8,128)S(1)} %get-tuple-element.138) | copy-start | bytes 1966084
  118.8 108.8 %copy-start.8 = (f32[4,2,128,128]{3,2,1,0:T(8,128)S(1)}, f32[4,2,128,128]{3,2,1,0:T(8,128)}, u32[]{:S(2)}) copy-start(f32[4,2,128,128]{3,2,1,0:T(8,128)} %slice.176) | copy-start | bytes 1572868
  118.8 108.8 %copy-start.11 = (bf16[256,256]{1,0:T(8,128)(2,1)S(1)}, bf16[256,256]{1,0:T(8,128)(2,1)}, u32[]{:S(2)}) copy-start(bf16[256,256]{1,0:T(8,128)(2,1)} %constant.80.clone.fz_ref.gy_ref) | copy-start | bytes 393220
  118.8 108.8 %copy-start.17 = (bf16[256,256]{1,0:T(8,128)(2,1)S(1)}, bf16[256,256]{1,0:T(8,128)(2,1)}, u32[]{:S(2)}) copy-start(bf16[256,256]{1,0:T(8,128)(2,1)} %constant.79.clone.fy_ref.gz_ref) | copy-start | bytes 393220
  227.6 0.8 copy-start.10
  228.4 74.2 %all-to-all-start.1 = ((bf16[32,4,6,16,128]{4,3,2,1,0:T(8,128)(2,1)}), bf16[32,4,6,16,128]{4,3,2,1,0:T(8,128)(2,1)S(1)}, u32[]{:S(2)}, u32[]{:S(2)}) async-start(bf16[32,4,6,16,128]{4,3,2,1,0:T(8,128)(2,1)} %get-tuple-element.74), calls=%async_computation.1 | async-start | bytes 6291456 | tf_op jit(solution)/shard_map/cond/branch_1_fun/all_to_all | solution.py:639
  231.2 75.6 %copy-start.16 = (s32[128]{0:T(128)S(1)}, s32[128]{0:T(128)}, u32[]{:S(2)}) copy-start(s32[128]{0:T(128)} %constant.104) | copy-start | bytes 1540 | tf_op jit(solution)/shard_map/cond
  302.6 30.2 %all-to-all-start.2 = ((bf16[32,4,2,16,128]{4,3,2,1,0:T(8,128)(2,1)}), bf16[32,4,2,16,128]{4,3,2,1,0:T(8,128)(2,1)}, u32[]{:S(2)}, u32[]{:S(2)}) async-start(bf16[32,4,2,16,128]{4,3,2,1,0:T(8,128)(2,1)} %get-tuple-element.90), calls=%async_computation.2 | async-start | bytes 2097152 | tf_op jit(solution)/shard_map/cond/branch_1_fun/all_to_all | solution.py:639
  321.5 0.8 copy-start
  322.3 16.6 %copy-start.12 = (f32[4,2,128,128]{3,2,1,0:T(8,128)S(1)}, f32[4,2,128,128]{3,2,1,0:T(8,128)}, u32[]{:S(2)}) copy-start(f32[4,2,128,128]{3,2,1,0:T(8,128)} %branch_1_fun.3) | copy-start | bytes 1572868 | tf_op jit(solution)/shard_map/cond
  332.8 5.1 %copy-start.1 = (f32[4,2,128,128]{3,2,1,0:T(8,128)S(1)}, f32[4,2,128,128]{3,2,1,0:T(8,128)}, u32[]{:S(2)}) copy-start(f32[4,2,128,128]{3,2,1,0:T(8,128)} %copy-done) | copy-start | bytes 1572868 | tf_op jit(solution)/shard_map/cond
  340.4 24.8 %copy-start.3 = (f32[5,2,128,128]{3,2,1,0:T(8,128)S(1)}, f32[5,2,128,128]{3,2,1,0:T(8,128)}, u32[]{:S(2)}) copy-start(f32[5,2,128,128]{3,2,1,0:T(8,128)} %copy-done.2) | copy-start | bytes 1966084
  340.4 25.0 %copy-start.5 = (f32[5,2,128,128]{3,2,1,0:T(8,128)S(1)}, f32[5,2,128,128]{3,2,1,0:T(8,128)}, u32[]{:S(2)}) copy-start(f32[5,2,128,128]{3,2,1,0:T(8,128)} %copy-done.4) | copy-start | bytes 1966084
  340.4 28.2 %copy-start.6 = (f32[5,2,128,128]{3,2,1,0:T(8,128)S(1)}, f32[5,2,128,128]{3,2,1,0:T(8,128)}, u32[]{:S(2)}) copy-start(f32[5,2,128,128]{3,2,1,0:T(8,128)} %get-tuple-element.140) | copy-start | bytes 1966084
  340.4 24.5 %collective-permute-start = (f32[1,2,128,128]{3,2,1,0:T(8,128)S(1)}, f32[1,2,128,128]{3,2,1,0:T(8,128)S(1)}, u32[]{:S(2)}, u32[]{:S(2)}) collective-permute-start(f32[1,2,128,128]{3,2,1,0:T(8,128)S(1)} %get-tuple-element.154), channel_id=1, source_target_pairs={{0,8},{8,16},{16,24},{24,1},{1,9},{9,17},{17,25},{25,2},{2,10},{10... | collective-permute-start | bytes 393224 | tf_op jit(solution)/shard_map/ppermute | solution.py:783
  363.6 4.9 %collective-permute-start.1 = (f32[1,2,128,128]{3,2,1,0:T(8,128)S(1)}, f32[1,2,128,128]{3,2,1,0:T(8,128)S(1)}, u32[]{:S(2)}, u32[]{:S(2)}) collective-permute-start(f32[1,2,128,128]{3,2,1,0:T(8,128)S(1)} %get-tuple-element.153), channel_id=1, source_target_pairs={{8,0},{16,8},{24,16},{1,24},{9,1},{17,9},{25,17},{2,25},{10,2},{18... | collective-permute-start | bytes 393224 | tf_op jit(solution)/shard_map/ppermute | solution.py:784
  365.1 4.3 %copy-start.7 = (f32[4,2,128,128]{3,2,1,0:T(8,128)S(1)}, f32[4,2,128,128]{3,2,1,0:T(8,128)}, u32[]{:S(2)}) copy-start(f32[4,2,128,128]{3,2,1,0:T(8,128)} %fusion.27) | copy-start | bytes 1572868
  365.2 4.3 %copy-start.9 = (f32[4,2,128,128]{3,2,1,0:T(8,128)S(1)}, f32[4,2,128,128]{3,2,1,0:T(8,128)}, u32[]{:S(2)}) copy-start(f32[4,2,128,128]{3,2,1,0:T(8,128)} %slice.176) | copy-start | bytes 1572868

commit v5 on v4

--- a/solution.py
+++ b/solution.py
@@ -481,7 +481,7 @@
         )
 
     def begin(step, _):
-        copy(step).start()
+        copy(1 + lax.rem(step - 1 + count // 2 - 1, count - 1)).start()
         return 0
 
     def end(step, _):
@@ -536,7 +536,8 @@
         )
         for step in range(1, count)
     ]
-    for copy in copies:
+    far = count // 2 - 1
+    for copy in copies[far:] + copies[:far]:
         copy.start()
     all_ref[slab] = own_ref[...]
     for copy in copies:

time: 393 us -> 394 us (level)
  Pallas kernels: 106 us -> 112 us
  transfers between devices with their start and end apart: 6 -> 6, of which waited for: 4 -> 4; matrix products, arithmetic and copies ran while one was open for 15% -> 15% of each run, Pallas kernels for 22% -> 23%
where the time goes in v5:
time: 394 us; the launch traced here: 392 us
  waiting for transfers between devices  162 us (41%)
  Pallas kernels  112 us (28%)
  local copies, waits for them, and re-layouts  42 us (11%)
  blocking collectives  24.1 us (6%)
  other arithmetic  22 us (6%)
  starting transfers between devices  20.8 us (5%)
  matrix products  8.07 us (2%)
    all_to_all x4, waiting for transfers between devices, swap(): lax.all_to_all(blocks, EVERY, split_axis=0, concat_axis=0, tiled=True)  159 us
    pallas_call x4, Pallas kernels, plane_call(): pl.pallas_call(kernel, out_shape=jax.ShapeDtypeStruct(shape, f32), grid=(...  62.8 us
    all_gather x2, blocking collectives, by_planes(): masks.append(lax.all_gather(part, 'coil', axis=0))  24.1 us
    all_to_all x4, starting transfers between devices, swap(): lax.all_to_all(blocks, EVERY, split_axis=0, concat_axis=0, tiled=True)  18.1 us
    pallas_call x1, Pallas kernels, delivered(): pl.pallas_call(deliver_kernel, out_shape=jax.ShapeDtypeStruct(blocks.shap...  17.9 us
    pallas_call x1, Pallas kernels, selected(): pl.pallas_call(functools.partial(select_kernel, edges), out_shape=[jax.Sh...  17.9 us
    dot_general x1, local copies, waits for them, and re-layouts, by_planes(): jnp.einsum('ckzyx,kjxw->wcjyz', data, inverse_x, preferred_element_type=f32)  13.2 us
    pallas_call x1, Pallas kernels, shared(): pl.pallas_call(share_kernel, out_shape=jax.ShapeDtypeStruct((slabs,) + ow...  13 us
  transfers between devices with their start and end apart: 6, of which 4 were waited for; matrix products, arithmetic and copies ran while one was open for 15% of the time, Pallas kernels for 23%

profile of v5, /device:TPU:0, one launch (start us, length us, event | category | flops | bytes accessed | tf_op | source)
XLA Modules:
  0.0 392.3 jit_solution(4681730169667485116)
XLA Ops:
  0.0 1.1 convert_element_type.59
  1.3 0.2 fusion.55
  1.5 0.5 fusion.19
  2.0 1.2 reshape.123
  3.2 7.3 %all-to-all-start.3 = ((bf16[32,48,128]{2,1,0:T(8,128)(2,1)}), bf16[32,48,128]{2,1,0:T(8,128)(2,1)S(1)}, u32[]{:S(2)}, u32[]{:S(2)}) async-start(bf16[32,48,128]{2,1,0:T(8,128)(2,1)} %reshape.123), calls=%async_computation.3 | async-start | bytes 786432 | tf_op jit(solution)/shard_map/all_to_all | solution.py:640
  10.6 12.6 %copy.74 = bf16[8,2,16,128,128]{3,2,1,0,4:T(8,128)(2,1)} copy(bf16[8,2,16,128,128]{4,3,2,1,0:T(8,128)(2,1)} %param.16) | data formatting | bytes 16777216 | tf_op jit(solution)/shard_map/optimization_barrier | solution.py:699
  23.2 0.6 fusion.57
  23.8 13.0 %shard_map.129 = bf16[8,8,16,128]{3,2,1,0:T(8,128)(2,1)} custom-call(bf16[8,16,128]{2,1,0:T(8,128)(2,1)} %get-tuple-element.167.own_ref), custom_call_target="tpu_custom_call" | custom-call | flops 1048576 | bytes 524288 | tf_op jit(solution)/shard_map/pallas_call | solution.py:548
  36.9 4.0 %all-to-all-start.4 = ((bf16[32,4,8,2,16,128]{5,4,3,2,1,0:T(8,128)(2,1)}), bf16[32,4,8,2,16,128]{5,4,3,2,1,0:T(8,128)(2,1)}, u32[]{:S(2)}, u32[]{:S(2)}) async-start(bf16[32,4,8,2,16,128]{5,4,3,2,1,0:T(8,128)(2,1)} %bitcast.80), calls=%async_computation.4 | async-start | bytes 16777216 | tf_op jit(solution)/shard_map/all_to_all | solution.py:640
  41.1 6.8 %convolution_bitcast_fusion = bf16[8,128,16,2,128]{4,2,3,1,0:T(8,128)(2,1)} fusion(bf16[2,2,128,128,1,1]{2,3,0,1,5,4:T(8,128)(2,1)S(1)} %copy-done.18, bf16[8,2,128,16,128]{4,3,2,1,0:T(8,128)(2,1)} %param.15, bf16[8,128,16]{2,1,0:T(8,128)(2,1)S(1)} %copy.75), kind=kOutput, calls=%fused_computation.2 | convolution fusion | flops 2151677952 | bytes 16941056 | tf_op jit(solution)/shard_map/ckzyx,kjxw->wcjyz/dot_general | solution.py:712
  47.9 13.2 %copy.77 = bf16[8,128,16,2,128]{1,2,3,0,4:T(8,128)(2,1)} copy(bf16[8,128,16,2,128]{4,2,3,1,0:T(8,128)(2,1)} %convolution_bitcast_fusion) | data formatting | bytes 16777216 | tf_op jit(solution)/shard_map/ckzyx,kjxw->wcjyz/dot_general | solution.py:712
  61.3 0.2 fusion.4
  61.5 2.4 select_reduce_fusion.pick_ref
  64.0 17.9 %shard_map.130 = (bf16[128,6,16,128]{3,2,1,0:T(8,128)(2,1)}, bf16[128,2,16,128]{3,2,1,0:T(8,128)(2,1)}) custom-call(s32[8,8,128]{2,1,0:T(8,128)} %select_reduce_fusion.pick_ref, bf16[128,8,2,16,128]{4,3,2,1,0:T(8,128)(2,1)} %bitcast.77), custom_call_target="tpu_custom_call" | custom-call | flops 268435456 | bytes 12582912 | tf_op jit(solution)/shard_map/pallas_call | solution.py:436
  81.8 0.6 reshape.128
  82.5 2.0 copy.82
  84.5 0.8 reshape.129
  85.3 0.8 slice.176
  86.3 16.6 %all_gather.13 = bf16[4,4,128,128]{3,2,1,0:T(8,128)(2,1)S(1)} all-gather(bf16[1,4,128,128]{3,2,1,0:T(8,128)(2,1)S(1)} %bitcast.98), channel_id=1, replica_groups=mesh['coil'=4,'slab'=8] {'coil'}, dimensions={0}, use_global_device_ids=true | all-gather | bytes 655360 | tf_op jit(solution)/shard_map/all_gather | solution.py:739
  102.9 0.3 copy.81
  103.2 7.5 %all-gather = bf16[16,128,128]{2,1,0:T(8,128)(2,1)S(1)} all-gather(bf16[4,128,128]{2,1,0:T(8,128)(2,1)S(1)} %bitcast.97), channel_id=2, replica_groups=mesh['coil'=4,'slab'=8] {'coil'}, dimensions={0}, use_global_device_ids=true | all-gather | bytes 655360 | tf_op jit(solution)/shard_map/all_gather | solution.py:739
  110.7 0.3 copy.80
  111.0 1.1 pad_maximum_fusion.1
  112.1 0.7 copy.83
  112.8 0.2 copy.101
  113.1 0.2 slice_subtract_fusion.1
  113.3 0.2 multiply_reduce_fusion.4
  113.5 0.2 multiply_reduce_fusion.3
  113.9 1.4 broadcast_select_fusion
  115.3 0.9 slice.185
  116.2 0.9 slice.183
  117.2 0.4 convolution_convert_fusion
  117.6 0.5 convolution_convert_fusion.1
  118.1 2.3 fusion.5
  121.1 2.6 fusion.27
  123.7 3.5 fusion.1
  127.2 99.7 %all-to-all-done.4 = bf16[32,4,8,2,16,128]{5,4,3,2,1,0:T(8,128)(2,1)} async-done(((bf16[32,4,8,2,16,128]{5,4,3,2,1,0:T(8,128)(2,1)}), bf16[32,4,8,2,16,128]{5,4,3,2,1,0:T(8,128)(2,1)}, u32[]{:S(2)}, u32[]{:S(2)}) %all-to-all-start.4) | async-done | bytes 8388640 | tf_op jit(solution)/shard_map/all_to_all | solution.py:640
  226.9 111.3 %conditional.1 = (f32[4,2,128,128]{3,2,1,0:T(8,128)S(1)}, f32[4,2,128,128]{3,2,1,0:T(8,128)}) conditional(s32[]{:T(128)} %convert_element_type.72, (bf16[128,8,2,16,128]{4,3,2,1,0:T(8,128)(2,1)}, f32[4,2,128,128]{3,2,1,0:T(8,128)S(1)}, bf16[8,4,4,8,2,16,128]{6,5,4,3,2,1,0:T(8,128)(2,1)}, bf16[4,8,128,128]{3,2,1,0:T(8,128)(2,1)}, ...), branch_computations={%region_5.6_spmd, %region_6.7_spmd} | conditional | flops 12885033984 | bytes 54526028 | solution.py:778
  226.9 0.8 copy-done.10
  227.7 2.8 all-to-all-start.1
  230.5 22.1 %branch_1_fun.3 = f32[4,2,128,128]{3,2,1,0:T(8,128)} custom-call(f32[4,2,128,128]{3,2,1,0:T(8,128)} %copy-done.10, bf16[8,4,4,8,2,16,128]{6,5,4,3,2,1,0:T(8,128)(2,1)} %get-tuple-element.76.maps_ref, bf16[4,8,128,128]{3,2,1,0:T(8,128)(2,1)} %get-tuple-element.77.mask_ref, bf16[256,256]{1,0:T(8,128)(2,1)S(1)} %get-tuple-element.80.gz_ref, ...), custom_call_target="tpu_custom_call" | custom-call | flops 8589934592 | bytes 8388608 | tf_op jit(solution)/shard_map/cond/branch_1_fun/pallas_call | solution.py:565
  252.6 49.3 %all-to-all-done.1 = bf16[32,4,6,16,128]{4,3,2,1,0:T(8,128)(2,1)S(1)} async-done(((bf16[32,4,6,16,128]{4,3,2,1,0:T(8,128)(2,1)}), bf16[32,4,6,16,128]{4,3,2,1,0:T(8,128)(2,1)S(1)}, u32[]{:S(2)}, u32[]{:S(2)}) %all-to-all-start.1) | async-done | bytes 3145760 | tf_op jit(solution)/shard_map/cond/branch_1_fun/all_to_all | solution.py:640
  301.9 4.0 %all-to-all-start.2 = ((bf16[32,4,2,16,128]{4,3,2,1,0:T(8,128)(2,1)}), bf16[32,4,2,16,128]{4,3,2,1,0:T(8,128)(2,1)}, u32[]{:S(2)}, u32[]{:S(2)}) async-start(bf16[32,4,2,16,128]{4,3,2,1,0:T(8,128)(2,1)} %get-tuple-element.90), calls=%async_computation.2 | async-start | bytes 2097152 | tf_op jit(solution)/shard_map/cond/branch_1_fun/all_to_all | solution.py:640
  306.1 0.9 gather_fusion
  307.0 13.8 %branch_1_fun.4 = f32[4,2,128,128]{3,2,1,0:T(8,128)S(1)} custom-call(bf16[8,4,4,6,16,128]{5,4,3,2,1,0:T(8,128)(2,1)S(1)} %bitcast.74, s32[4,8,128,128]{3,2,1,0:T(8,128)} %get-tuple-element.85.code_ref, bf16[8,4,4,8,2,16,128]{6,5,4,3,2,1,0:T(8,128)(2,1)} %get-tuple-element.76.maps_ref, bf16[256,256]{1,0:T(8,128)(2,1)S(1)} %get-tuple-element.86.gz_ref, ...), custom_call_target="tpu_custom_call" | custom-call | flops 3221225472 | bytes 12582912 | tf_op jit(solution)/shard_map/cond/branch_1_fun/pallas_call | solution.py:565
  320.8 0.8 copy-done
  321.6 10.5 %all-to-all-done.2 = bf16[32,4,2,16,128]{4,3,2,1,0:T(8,128)(2,1)} async-done(((bf16[32,4,2,16,128]{4,3,2,1,0:T(8,128)(2,1)}), bf16[32,4,2,16,128]{4,3,2,1,0:T(8,128)(2,1)}, u32[]{:S(2)}, u32[]{:S(2)}) %all-to-all-start.2) | async-done | bytes 1048608 | tf_op jit(solution)/shard_map/cond/branch_1_fun/all_to_all | solution.py:640
  332.1 5.1 %branch_1_fun.5 = f32[4,2,128,128]{3,2,1,0:T(8,128)S(1)} custom-call(bf16[8,4,4,2,16,128]{5,4,3,2,1,0:T(8,128)(2,1)} %bitcast.6.data_ref, s32[4,8,128,128]{3,2,1,0:T(8,128)} %get-tuple-element.85.code_ref, bf16[8,4,4,8,2,16,128]{6,5,4,3,2,1,0:T(8,128)(2,1)} %get-tuple-element.76.maps_ref, bf16[256,256]{1,0:T(8,128)(2,1)S(1)} %get-tuple-element.86.gz_ref, ...), custom_call_target="tpu_custom_call" | custom-call | flops 1073741824 | bytes 4194304 | tf_op jit(solution)/shard_map/cond/branch_1_fun/pallas_call | solution.py:565
  337.3 0.9 add.105
  338.1 1.5 multiply_add_fusion.2.guess_ref
  339.7 1.4 collective-permute-start
  341.1 21.8 %shard_map.131 = f32[4,2,128,128]{3,2,1,0:T(8,128)S(1)} custom-call(f32[4,2,128,128]{3,2,1,0:T(8,128)S(1)} %multiply_add_fusion.2.guess_ref, bf16[8,4,4,8,2,16,128]{6,5,4,3,2,1,0:T(8,128)(2,1)} %bitcast.12.maps_ref, bf16[4,8,128,128]{3,2,1,0:T(8,128)(2,1)} %get-tuple-element.131.mask_ref, bf16[256,256]{1,0:T(8,128)(2,1)} %constant.79.clone.fy_ref.gz_ref, ...), custom_call_target="tpu_custom_call" | custom-call | flops 8589934592 | bytes 8388608 | tf_op jit(solution)/shard_map/pallas_call | solution.py:565
  362.9 1.3 collective-permute-start.1
  364.2 0.2 fusion.12
  364.8 3.0 collective-permute-done.1
  367.8 0.2 multiply_reduce_fusion
  368.2 0.5 broadcast_multiply_fusion.1
  368.8 1.7 fusion.25
  370.5 0.4 reshape.132
  370.9 0.2 copy.100
  371.2 1.2 reshape.133.block_ref
  372.4 17.9 %shard_map.132 = bf16[32,32,128]{2,1,0:T(8,128)(2,1)} custom-call(bf16[32,32,128]{2,1,0:T(8,128)(2,1)} %reshape.133.block_ref), custom_call_target="tpu_custom_call" | custom-call | flops 8388608 | bytes 524288 | tf_op jit(solution)/shard_map/pallas_call | solution.py:499
  390.3 1.1 reshape.135
  391.3 1.0 copy.86
  (61 shorter events, 1.8 us)
Async XLA Ops:
  3.2 33.6 %all-to-all-start.3 = ((bf16[32,48,128]{2,1,0:T(8,128)(2,1)}), bf16[32,48,128]{2,1,0:T(8,128)(2,1)S(1)}, u32[]{:S(2)}, u32[]{:S(2)}) async-start(bf16[32,48,128]{2,1,0:T(8,128)(2,1)} %reshape.123), calls=%async_computation.3 | async-start | bytes 786432 | tf_op jit(solution)/shard_map/all_to_all | solution.py:640
  10.6 12.7 %copy-start.15 = (s32[8,128,16]{1,2,0:T(8,128)S(1)}, s32[8,128,16]{1,2,0:T(8,128)}, u32[]{:S(2)}) copy-start(s32[8,128,16]{1,2,0:T(8,128)} %param.17) | copy-start | bytes 196612
  36.9 4.2 %copy-start.18 = (bf16[2,2,128,128,1,1]{2,3,0,1,5,4:T(8,128)(2,1)S(1)}, bf16[2,2,128,128,1,1]{2,3,0,1,5,4:T(8,128)(2,1)}, u32[]{:S(2)}) copy-start(bf16[2,2,128,128,1,1]{2,3,0,1,5,4:T(8,128)(2,1)} %constant.105) | copy-start | bytes 393220
  36.9 190.0 %all-to-all-start.4 = ((bf16[32,4,8,2,16,128]{5,4,3,2,1,0:T(8,128)(2,1)}), bf16[32,4,8,2,16,128]{5,4,3,2,1,0:T(8,128)(2,1)}, u32[]{:S(2)}, u32[]{:S(2)}) async-start(bf16[32,4,8,2,16,128]{5,4,3,2,1,0:T(8,128)(2,1)} %bitcast.80), calls=%async_computation.4 | async-start | bytes 16777216 | tf_op jit(solution)/shard_map/all_to_all | solution.py:640
  64.0 22.3 %copy-start.14 = (bf16[8,8,16,128]{3,2,1,0:T(8,128)(2,1)S(1)}, bf16[8,8,16,128]{3,2,1,0:T(8,128)(2,1)}, u32[]{:S(2)}) copy-start(bf16[8,8,16,128]{3,2,1,0:T(8,128)(2,1)} %shard_map.129) | copy-start | bytes 786436
  115.3 8.4 %copy-start.2 = (f32[5,2,128,128]{3,2,1,0:T(8,128)}, f32[5,2,128,128]{3,2,1,0:T(8,128)S(1)}, u32[]{:S(2)}) copy-start(f32[5,2,128,128]{3,2,1,0:T(8,128)S(1)} %get-tuple-element.139) | copy-start | bytes 1966084
  115.3 8.4 %copy-start.4 = (f32[5,2,128,128]{3,2,1,0:T(8,128)}, f32[5,2,128,128]{3,2,1,0:T(8,128)S(1)}, u32[]{:S(2)}) copy-start(f32[5,2,128,128]{3,2,1,0:T(8,128)S(1)} %get-tuple-element.138) | copy-start | bytes 1966084
  118.1 108.8 %copy-start.8 = (f32[4,2,128,128]{3,2,1,0:T(8,128)S(1)}, f32[4,2,128,128]{3,2,1,0:T(8,128)}, u32[]{:S(2)}) copy-start(f32[4,2,128,128]{3,2,1,0:T(8,128)} %slice.176) | copy-start | bytes 1572868
  118.1 108.8 %copy-start.11 = (bf16[256,256]{1,0:T(8,128)(2,1)S(1)}, bf16[256,256]{1,0:T(8,128)(2,1)}, u32[]{:S(2)}) copy-start(bf16[256,256]{1,0:T(8,128)(2,1)} %constant.80.clone.fz_ref.gy_ref) | copy-start | bytes 393220
  118.1 108.8 %copy-start.17 = (bf16[256,256]{1,0:T(8,128)(2,1)S(1)}, bf16[256,256]{1,0:T(8,128)(2,1)}, u32[]{:S(2)}) copy-start(bf16[256,256]{1,0:T(8,128)(2,1)} %constant.79.clone.fy_ref.gz_ref) | copy-start | bytes 393220
  226.9 0.8 copy-start.10
  227.7 74.2 %all-to-all-start.1 = ((bf16[32,4,6,16,128]{4,3,2,1,0:T(8,128)(2,1)}), bf16[32,4,6,16,128]{4,3,2,1,0:T(8,128)(2,1)S(1)}, u32[]{:S(2)}, u32[]{:S(2)}) async-start(bf16[32,4,6,16,128]{4,3,2,1,0:T(8,128)(2,1)} %get-tuple-element.74), calls=%async_computation.1 | async-start | bytes 6291456 | tf_op jit(solution)/shard_map/cond/branch_1_fun/all_to_all | solution.py:640
  230.5 75.6 %copy-start.16 = (s32[128]{0:T(128)S(1)}, s32[128]{0:T(128)}, u32[]{:S(2)}) copy-start(s32[128]{0:T(128)} %constant.104) | copy-start | bytes 1540 | tf_op jit(solution)/shard_map/cond
  301.9 30.2 %all-to-all-start.2 = ((bf16[32,4,2,16,128]{4,3,2,1,0:T(8,128)(2,1)}), bf16[32,4,2,16,128]{4,3,2,1,0:T(8,128)(2,1)}, u32[]{:S(2)}, u32[]{:S(2)}) async-start(bf16[32,4,2,16,128]{4,3,2,1,0:T(8,128)(2,1)} %get-tuple-element.90), calls=%async_computation.2 | async-start | bytes 2097152 | tf_op jit(solution)/shard_map/cond/branch_1_fun/all_to_all | solution.py:640
  320.8 0.8 copy-start
  321.6 16.6 %copy-start.12 = (f32[4,2,128,128]{3,2,1,0:T(8,128)S(1)}, f32[4,2,128,128]{3,2,1,0:T(8,128)}, u32[]{:S(2)}) copy-start(f32[4,2,128,128]{3,2,1,0:T(8,128)} %branch_1_fun.3) | copy-start | bytes 1572868 | tf_op jit(solution)/shard_map/cond
  332.1 5.1 %copy-start.1 = (f32[4,2,128,128]{3,2,1,0:T(8,128)S(1)}, f32[4,2,128,128]{3,2,1,0:T(8,128)}, u32[]{:S(2)}) copy-start(f32[4,2,128,128]{3,2,1,0:T(8,128)} %copy-done) | copy-start | bytes 1572868 | tf_op jit(solution)/shard_map/cond
  339.6 24.8 %copy-start.3 = (f32[5,2,128,128]{3,2,1,0:T(8,128)S(1)}, f32[5,2,128,128]{3,2,1,0:T(8,128)}, u32[]{:S(2)}) copy-start(f32[5,2,128,128]{3,2,1,0:T(8,128)} %copy-done.2) | copy-start | bytes 1966084
  339.7 25.0 %copy-start.5 = (f32[5,2,128,128]{3,2,1,0:T(8,128)S(1)}, f32[5,2,128,128]{3,2,1,0:T(8,128)}, u32[]{:S(2)}) copy-start(f32[5,2,128,128]{3,2,1,0:T(8,128)} %copy-done.4) | copy-start | bytes 1966084
  339.7 28.2 %copy-start.6 = (f32[5,2,128,128]{3,2,1,0:T(8,128)S(1)}, f32[5,2,128,128]{3,2,1,0:T(8,128)}, u32[]{:S(2)}) copy-start(f32[5,2,128,128]{3,2,1,0:T(8,128)} %get-tuple-element.140) | copy-start | bytes 1966084
  339.7 24.5 %collective-permute-start = (f32[1,2,128,128]{3,2,1,0:T(8,128)S(1)}, f32[1,2,128,128]{3,2,1,0:T(8,128)S(1)}, u32[]{:S(2)}, u32[]{:S(2)}) collective-permute-start(f32[1,2,128,128]{3,2,1,0:T(8,128)S(1)} %get-tuple-element.154), channel_id=1, source_target_pairs={{0,8},{8,16},{16,24},{24,1},{1,9},{9,17},{17,25},{25,2},{2,10},{10... | collective-permute-start | bytes 393224 | tf_op jit(solution)/shard_map/ppermute | solution.py:784
  362.9 4.9 %collective-permute-start.1 = (f32[1,2,128,128]{3,2,1,0:T(8,128)S(1)}, f32[1,2,128,128]{3,2,1,0:T(8,128)S(1)}, u32[]{:S(2)}, u32[]{:S(2)}) collective-permute-start(f32[1,2,128,128]{3,2,1,0:T(8,128)S(1)} %get-tuple-element.153), channel_id=1, source_target_pairs={{8,0},{16,8},{24,16},{1,24},{9,1},{17,9},{25,17},{2,25},{10,2},{18... | collective-permute-start | bytes 393224 | tf_op jit(solution)/shard_map/ppermute | solution.py:785
  364.4 4.3 %copy-start.7 = (f32[4,2,128,128]{3,2,1,0:T(8,128)S(1)}, f32[4,2,128,128]{3,2,1,0:T(8,128)}, u32[]{:S(2)}) copy-start(f32[4,2,128,128]{3,2,1,0:T(8,128)} %fusion.27) | copy-start | bytes 1572868
  364.5 4.3 %copy-start.9 = (f32[4,2,128,128]{3,2,1,0:T(8,128)S(1)}, f32[4,2,128,128]{3,2,1,0:T(8,128)}, u32[]{:S(2)}) copy-start(f32[4,2,128,128]{3,2,1,0:T(8,128)} %slice.176) | copy-start | bytes 1572868
